TPU v7x, 8 devices: a whole 2x2x1 slice. The times are simulated.
8 devices in a mesh: dp: 2 (over z, y), sp: 4 (over x, core).
Axes of the slice: x: 2, y: 2, z: 1, core: 2. Of those that a mesh axis runs over, the one named last changes fastest.
Arguments:
- dec_hidden: bfloat16 [2048, 1280], P(('dp', 'sp')), parts along dimension 0
- enc_memory: bfloat16 [8192, 1280], P(('dp', 'sp')), parts along dimension 0
- mem_len: int32 [2], P('dp'), parts along dimension 0
- norm_self: bfloat16 [2, 1280], replicated
- norm_cross: bfloat16 [2, 1280], replicated
- norm_mlp: bfloat16 [2, 1280], replicated
- self_q: bfloat16 [2, 1280, 1280], replicated
- self_k: bfloat16 [2, 1280, 1280], replicated
- self_v: bfloat16 [2, 1280, 1280], replicated
- self_o: bfloat16 [2, 20, 64, 1280], replicated
- cross_q: bfloat16 [2, 1280, 1280], replicated
- cross_k: bfloat16 [2, 1280, 1280], replicated
- cross_v: bfloat16 [2, 1280, 1280], replicated
- cross_o: bfloat16 [2, 20, 64, 1280], replicated
- mlp_gate: bfloat16 [2, 1280, 5120], replicated
- mlp_up: bfloat16 [2, 1280, 5120], replicated
- mlp_down: bfloat16 [2, 5120, 1280], replicated
Outputs:
- output: bfloat16 [2048, 1280], P(('dp', 'sp')), parts along dimension 0
There are 2 independent parts. A program takes and returns all parts, laid end to end along the dimension named above; an argument that names none is the same for every part.
All inputs are finite; a program needn't handle non-finite values.
Results may differ from a plain program's by a relative error of at most 0.015751.
Values are sent between devices in bfloat16 or wider.
A program may use at most 1 GiB of HBM per device.

v0:
```python
import functools

import jax
import jax.numpy as jnp
from jax import lax
from jax.experimental import pallas as pl
from jax.experimental.pallas import tpu as pltpu
from jax.sharding import PartitionSpec as P


EPS = 1e-6
NEG_BIG = -1e30
F32 = jnp.float32
BF16 = jnp.bfloat16
CH = 512
VMEM_LIMIT = 62 * 1024 * 1024
ANY = pl.BlockSpec(memory_space=pl.ANY)
SMEM = pl.BlockSpec(memory_space=pltpu.SMEM)
VMEM = pl.BlockSpec(memory_space=pltpu.VMEM)


def rms(h, gain):
    h32 = h.astype(F32)
    inv = lax.rsqrt(jnp.mean(h32 * h32, axis=-1, keepdims=True) + EPS)
    return (h32 * inv * gain.astype(F32)).astype(BF16)


def dot(a, b):
    return jnp.dot(a, b, preferred_element_type=F32)


def dot_nt(a, b):
    return lax.dot_general(a, b, (((1,), (1,)), ((), ())), preferred_element_type=F32)


def kv_kernel(layers, n_src, lim_ref, pick_ref, *refs):
    srcs, (wk, wv, k_out, vt_out, mem, w_s, k_s, vt_s, sem, w_sems, o_sems) = refs[:n_src], refs[n_src:]
    rows = mem.shape[0]
    lo, n = layers

    def from_src(go):
        if n_src == 1:
            go(pltpu.make_async_copy(srcs[0], mem, sem))
        else:
            @pl.when(pick_ref[0] == 0)
            def _():
                go(pltpu.make_async_copy(srcs[0], mem, sem))

            @pl.when(pick_ref[0] != 0)
            def _():
                go(pltpu.make_async_copy(srcs[1], mem.at[pl.ds(0, CH)], sem))

    w_copies = []
    for i in range(n):
        for v, src in enumerate((wk, wv)):
            w_copies.append(pltpu.make_async_copy(src.at[lo + i], w_s.at[2 * i + v], w_sems.at[2 * i + v]))
    w_copies[0].start()
    from_src(lambda cp: cp.start())
    for cp in w_copies[1:]:
        cp.start()
    from_src(lambda cp: cp.wait())

    def out_copy(i, v, c):
        at = pl.ds(c * CH, CH)
        if v == 0:
            return pltpu.make_async_copy(k_s.at[i, at, :], k_out.at[i, at, :], o_sems.at[i, v, c])
        return pltpu.make_async_copy(vt_s.at[i, :, at], vt_out.at[i, :, at], o_sems.at[i, v, c])

    for i in range(n):
        for v in range(2):
            w_copies[2 * i + v].wait()
            for c in range(rows // CH):
                @pl.when(lim_ref[c] > 0)
                def _(i=i, v=v, c=c):
                    def step(r, _):
                        at = pl.ds(pl.multiple_of(c * CH + r * 256, 256), 256)
                        out = dot(mem[at, :], w_s[2 * i + v]).astype(BF16)
                        if v == 0:
                            k_s[i, at, :] = out
                        else:
                            vt_s[i, :, at] = out.T
                        return 0

                    lax.fori_loop(0, CH // 256, step, 0)
                    out_copy(i, v, c).start()
    for i in range(n):
        for v in range(2):
            for c in range(rows // CH):
                @pl.when(lim_ref[c] > 0)
                def _(i=i, v=v, c=c):
                    out_copy(i, v, c).wait()


def kv_project(lims, pick, srcs, wk, wv, rows, layers):
    width, cols = wk.shape[1], wk.shape[2]
    n = layers[1]
    flops = n * 4 * rows * width * cols
    return pl.pallas_call(
        functools.partial(kv_kernel, layers, len(srcs)),
        in_specs=[SMEM, SMEM] + [ANY] * (len(srcs) + 2),
        out_specs=[ANY, ANY],
        out_shape=[jax.ShapeDtypeStruct((n, rows, cols), BF16), jax.ShapeDtypeStruct((n, cols, rows), BF16)],
        scratch_shapes=[
            pltpu.VMEM((rows, width), BF16),
            pltpu.VMEM((2 * n, width, cols), BF16),
            pltpu.VMEM((n, rows, cols), BF16),
            pltpu.VMEM((n, cols, rows), BF16),
            pltpu.SemaphoreType.DMA,
            pltpu.SemaphoreType.DMA((2 * n,)),
            pltpu.SemaphoreType.DMA((n, 2, rows // CH)),
        ],
        cost_estimate=pl.CostEstimate(flops=flops, bytes_accessed=n * 4 * width * cols, transcendentals=0),
        compiler_params=pltpu.CompilerParams(vmem_limit_bytes=48 * 1024 * 1024),
        name="kv_project",
    )(lims, pick, *srcs, wk, wv)


def pair_queries(q):
    lane = lax.broadcasted_iota(jnp.int32, q.shape, 1)
    zero = jnp.zeros_like(q)
    return jnp.where(lane < 64, q, zero), jnp.where(lane < 64, zero, q)


def attend_all(pairs, n_chunks, scores, values, enter, at_ref, s_refs, mx_refs, m_ref, l_ref, acc_ref):
    def stage1(pair, j, buf):
        for h, s in enumerate(scores(pair, j)):
            s_refs[buf][h] = s
            mx_refs[buf][h:h + 1, :] = jnp.max(s, axis=0, keepdims=True)

    def stage2(pair, j, buf):
        vt = values(pair, j)
        for h in range(2):
            m_old = m_ref[h:h + 1, :]
            m_new = jnp.maximum(m_old, mx_refs[buf][h:h + 1, :])
            p = jnp.exp(s_refs[buf][h] - m_new)
            alpha = jnp.exp(m_old - m_new)
            m_ref[h:h + 1, :] = m_new
            l_ref[h:h + 1, :] = l_ref[h:h + 1, :] * alpha + jnp.sum(p, axis=0, keepdims=True)
            acc_ref[h] = acc_ref[h] * alpha + dot(vt[h * 64:(h + 1) * 64, :], p.astype(BF16))

    def advance(pair, j):
        wrap = j + 1 == n_chunks
        return jnp.where(wrap, pair + 1, pair), jnp.where(wrap, 0, j + 1)

    enter(0)
    stage1(0, 0, 0)

    def step(_, now):
        pair, j = now
        for buf in range(2):
            pair_next, j_next = advance(pair, j)

            @pl.when(j == 0)
            def _():
                m_ref[...] = jnp.full_like(m_ref, -jnp.inf)
                l_ref[...] = jnp.zeros_like(l_ref)
                acc_ref[...] = jnp.zeros_like(acc_ref)

            @pl.when((j_next == 0) & (pair_next < pairs))
            def _(pair_next=pair_next):
                enter(pair_next)

            stage1(jnp.minimum(pair_next, pairs - 1), j_next, 1 - buf)
            stage2(pair, j, buf)

            @pl.when(j_next == 0)
            def _(pair=pair):
                for h in range(2):
                    rows = pl.ds(pl.multiple_of(pair * 128 + h * 64, 64), 64)
                    at_ref[rows, :] = (acc_ref[h] / l_ref[h:h + 1, :]).astype(BF16)

            pair, j = pair_next, j_next
        return pair, j

    lax.fori_loop(0, pairs * n_chunks // 2, step, (jnp.int32(0), jnp.int32(0)))


def attend_scratch(rows):
    return [pltpu.VMEM((2, CH, rows), F32)] * 2 + [pltpu.VMEM((2, rows), F32)] * 4 + [pltpu.VMEM((2, 64, rows), F32)]


def self_kernel(layer, dev_ref, own_ref, s1_ref, s2_ref, s3_ref, gs_ref, gc_ref, wq, wk, wv, wo, wcq, hid_ref, q_ref,
                w_s, x_s, k_s, vt_s, qs, bias, at_s, a_s, s0, s1, mx0, mx1, m_s, l_s, acc_s, sems):
    rows, width = own_ref.shape
    tiles = width // 256
    dev = dev_ref[0]
    chip1 = dev >= 2

    w_copies = [pltpu.make_async_copy(src.at[layer], w_s.at[n], sems.at[n]) for n, src in enumerate((wk, wv, wq, wo, wcq))]
    w_copies[0].start()
    w_copies[1].start()

    gain = gs_ref[layer:layer + 1, :]
    x_s[pl.ds(0, rows), :] = rms(own_ref[...], gain)
    x_s[pl.ds(rows, rows), :] = rms(s1_ref[...], gain)

    @pl.when(chip1)
    def _():
        x_s[pl.ds(2 * rows, rows), :] = rms(s2_ref[...], gain)
        x_s[pl.ds(3 * rows, rows), :] = rms(s3_ref[...], gain)

    key = lax.broadcasted_iota(jnp.int32, (rows, rows), 0)
    query = lax.broadcasted_iota(jnp.int32, (rows, rows), 1)
    bias[pl.ds(0, rows), :] = jnp.where(key <= query, 0.0, NEG_BIG)
    bias[pl.ds(rows, rows), :] = jnp.full((rows, rows), jnp.where(dev % 2 == 1, 0.0, NEG_BIG), F32)
    bias[pl.ds(2 * rows, 2 * rows), :] = jnp.zeros((2 * rows, rows), F32)

    def tile(t):
        return pl.ds(pl.multiple_of(t * 256, 256), 256)

    def project(n, store):
        w_copies[n].wait()
        if n + 2 < len(w_copies):
            w_copies[n + 2].start()

        def step(r, _):
            at = tile(r)
            store(at, dot(x_s[at, :], w_s[n]).astype(BF16))
            return 0

        lax.fori_loop(0, jnp.where(chip1, 4, 2), step, 0)

    def store_k(at, out):
        k_s[at, :] = out

    def store_v(at, out):
        vt_s[:, at] = out.T

    project(0, store_k)
    project(1, store_v)
    w_copies[2].wait()
    w_copies[4].start()
    qs[...] = dot(x_s[pl.ds(0, rows), :], w_s[2]).astype(BF16) * BF16(0.125)

    def chunk(j):
        return pl.ds(pl.multiple_of(j * CH, CH), CH)

    def head_cols(i):
        return pl.ds(pl.multiple_of(i * 128, 128), 128)

    def scores(i, j):
        k = k_s[chunk(j), head_cols(i)]
        return [dot_nt(k, q) + bias[chunk(j), :] for q in pair_queries(qs[:, head_cols(i)])]

    def values(i, j):
        return vt_s[head_cols(i), chunk(j)]

    attend_all(width // 128, jnp.where(chip1, 2, 1), scores, values, lambda i: None, at_s, (s0, s1), (mx0, mx1), m_s, l_s, acc_s)

    a_s[...] = at_s[...].T
    w_copies[3].wait()

    def project_o(t, _):
        cols = tile(t)
        hid_ref[:, cols] = (own_ref[:, cols].astype(F32) + dot(a_s[...], w_s[3, :, cols])).astype(BF16)
        return 0

    lax.fori_loop(0, tiles, project_o, 0)
    a_s[...] = rms(hid_ref[...], gc_ref[layer:layer + 1, :])
    w_copies[4].wait()

    def project_cq(t, _):
        cols = tile(t)
        q_ref[:, cols] = dot(a_s[...], w_s[4, :, cols]).astype(BF16) * BF16(0.125)
        return 0

    lax.fori_loop(0, tiles, project_cq, 0)


def self_attention(layer, dev, own, s1, s2, s3, gs, gc, wq, wk, wv, wo, wcq):
    rows, width = own.shape
    shape = jax.ShapeDtypeStruct((rows, width), BF16)
    flops = 2 * rows * width * width * 11 + 4 * rows * 4 * rows * width
    return pl.pallas_call(
        functools.partial(self_kernel, layer),
        in_specs=[SMEM] + [VMEM] * 6 + [ANY] * 5,
        out_specs=[VMEM, VMEM],
        out_shape=[shape, shape],
        scratch_shapes=[
            pltpu.VMEM((5, width, width), BF16),
            pltpu.VMEM((4 * rows, width), BF16),
            pltpu.VMEM((4 * rows, width), BF16),
            pltpu.VMEM((width, 4 * rows), BF16),
            pltpu.VMEM((rows, width), BF16),
            pltpu.VMEM((4 * rows, rows), F32),
            pltpu.VMEM((width, rows), BF16),
            pltpu.VMEM((rows, width), BF16),
            *attend_scratch(rows),
            pltpu.SemaphoreType.DMA((5,)),
        ],
        cost_estimate=pl.CostEstimate(flops=flops, bytes_accessed=10 * width * width, transcendentals=0),
        compiler_params=pltpu.CompilerParams(vmem_limit_bytes=VMEM_LIMIT),
        name="self_attention",
    )(dev, own, s1, s2, s3, gs, gc, wq, wk, wv, wo, wcq)


def cross_kernel(layer, planes, n_kv, lim_ref, q_ref, hid_ref, gm_ref, *refs):
    ks, vts = refs[:n_kv], refs[n_kv:2 * n_kv]
    (wco, wg, wu, wd, out_ref, kbuf, vbuf, at_s, a_s, x_s, acc_o, s0, s1, mx0, mx1, m_s, l_s, acc_s, mask, list_s,
     wo_s, wg_s, wu_s, wd_s, kv_sems, o_sem, w_sems) = refs[2 * n_kv:]
    rows, width = q_ref.shape
    pairs = width // 128
    steps = wg_s.shape[0]
    ff = wg_s.shape[2]

    def kv_copies(i, slot):
        cols = pl.ds(pl.multiple_of(i * 128, 128), 128)
        out, at = [], 0
        for n in range(n_kv):
            n_rows = ks[n].shape[1]
            out.append(pltpu.make_async_copy(ks[n].at[planes[n], :, cols], kbuf.at[slot, pl.ds(at, n_rows), :], kv_sems.at[slot, 0, n]))
            out.append(pltpu.make_async_copy(vts[n].at[planes[n], cols, :], vbuf.at[slot, :, pl.ds(at, n_rows)], kv_sems.at[slot, 1, n]))
            at += n_rows
        return out

    def w_copies(j):
        cols = pl.ds(pl.multiple_of(j * ff, ff), ff)
        return (pltpu.make_async_copy(wg.at[layer, :, cols], wg_s.at[j], w_sems.at[0, j]),
                pltpu.make_async_copy(wu.at[layer, :, cols], wu_s.at[j], w_sems.at[1, j]),
                pltpu.make_async_copy(wd.at[layer, cols, :], wd_s.at[j], w_sems.at[2, j]))

    for cp in kv_copies(0, 0):
        cp.start()
    o_copy = pltpu.make_async_copy(wco.at[layer], wo_s, o_sem)

    n_chunks, last = jnp.int32(0), jnp.int32(0)
    for c in range(lim_ref.shape[0]):
        lim = lim_ref[c]

        @pl.when(lim > 0)
        def _(c=c, at=n_chunks):
            list_s[at] = c

        n_chunks = n_chunks + (lim > 0).astype(jnp.int32)
        last = last + jnp.where(lim < CH, lim, 0)
    key = lax.broadcasted_iota(jnp.int32, (CH, 128), 0)
    lane = lax.broadcasted_iota(jnp.int32, (CH, 128), 1)
    mask[0] = jnp.zeros((CH, 128), BF16)
    mask[1] = jnp.where((key >= last) & (lane == 0), NEG_BIG, 0.0).astype(BF16)
    ones = (lax.broadcasted_iota(jnp.int32, (rows, 128), 1) == 0).astype(F32).astype(BF16)

    def enter(i):
        @pl.when(i + 1 < pairs)
        def _():
            for cp in kv_copies(i + 1, lax.rem(i + 1, 3)):
                cp.start()

        @pl.when(i == 0)
        def _():
            o_copy.start()

        @pl.when(i < steps)
        def _():
            for cp in w_copies(i):
                cp.start()

        for cp in kv_copies(i, lax.rem(i, 3)):
            cp.wait()

    def chunk(j):
        return pl.ds(pl.multiple_of(list_s[j] * CH, CH), CH)

    def scores(i, j):
        k = kbuf[lax.rem(i, 3), chunk(j), :]
        partial = (lim_ref[list_s[j]] < CH).astype(jnp.int32)
        cols = pl.ds(pl.multiple_of(i * 128, 128), 128)
        k = jnp.concatenate([k, mask[partial]], axis=1)
        return [dot_nt(k, jnp.concatenate([q, ones], axis=1)) for q in pair_queries(q_ref[:, cols])]

    def values(i, j):
        return vbuf[lax.rem(i, 3), :, chunk(j)]

    attend_all(pairs, n_chunks, scores, values, enter, at_s, (s0, s1), (mx0, mx1), m_s, l_s, acc_s)

    a_s[...] = at_s[...].T
    o_copy.wait()

    def project_o(t, _):
        cols = pl.ds(pl.multiple_of(t * 256, 256), 256)
        out_ref[:, cols] = (hid_ref[:, cols].astype(F32) + dot(a_s[...], wo_s[:, cols])).astype(BF16)
        return 0

    lax.fori_loop(0, width // 256, project_o, 0)
    x_s[...] = rms(out_ref[...], gm_ref[layer:layer + 1, :])
    acc_o[...] = jnp.zeros_like(acc_o)

    def mlp_step(j, _):
        for cp in w_copies(j):
            cp.wait()
        x = x_s[...]
        gate = dot(x, wg_s[j])
        up = dot(x, wu_s[j])
        act = (gate / (1.0 + jnp.exp(-gate)) * up).astype(BF16)
        acc_o[...] += dot(act, wd_s[j])
        return 0

    lax.fori_loop(0, steps, mlp_step, 0)
    out_ref[...] = (out_ref[...].astype(F32) + acc_o[...]).astype(BF16)


def cross_mlp(layer, lims, q, hid, gm, kvs, wco, wg, wu, wd):
    rows, width = q.shape
    steps = 10
    ff = wg.shape[2] // steps
    planes = tuple(plane for _, _, plane in kvs)
    ks, vts = [k for k, _, _ in kvs], [v for _, v, _ in kvs]
    total = sum(k.shape[1] for k in ks)
    n = len(kvs)
    flops = 2 * rows * width * (width + 3 * wg.shape[2]) + 4 * rows * 3072 * width
    return pl.pallas_call(
        functools.partial(cross_kernel, layer, planes, n),
        in_specs=[SMEM, VMEM, VMEM, VMEM] + [ANY] * (2 * n + 4),
        out_specs=VMEM,
        out_shape=jax.ShapeDtypeStruct((rows, width), BF16),
        scratch_shapes=[
            pltpu.VMEM((3, total, 128), BF16),
            pltpu.VMEM((3, 128, total), BF16),
            pltpu.VMEM((width, rows), BF16),
            pltpu.VMEM((rows, width), BF16),
            pltpu.VMEM((rows, width), BF16),
            pltpu.VMEM((rows, width), F32),
            *attend_scratch(rows),
            pltpu.VMEM((2, CH, 128), BF16),
            pltpu.SMEM((8,), jnp.int32),
            pltpu.VMEM((width, width), BF16),
            pltpu.VMEM((steps, width, ff), BF16),
            pltpu.VMEM((steps, width, ff), BF16),
            pltpu.VMEM((steps, ff, width), BF16),
            pltpu.SemaphoreType.DMA((3, 2, n)),
            pltpu.SemaphoreType.DMA,
            pltpu.SemaphoreType.DMA((3, steps)),
        ],
        cost_estimate=pl.CostEstimate(flops=flops, bytes_accessed=2 * width * (width + 3 * wg.shape[2]), transcendentals=0),
        compiler_params=pltpu.CompilerParams(vmem_limit_bytes=VMEM_LIMIT),
        name="cross_mlp",
    )(lims, q, hid, gm, *ks, *vts, wco, wg, wu, wd)


NONE = 1 << 20
BASES = (
    (0, 512, 1024, 1536, 2048, NONE, NONE, 2560),
    (1024, 1536, 0, 512, NONE, 2048, 2560, NONE),
    (2048, NONE, 2560, NONE, 0, 1024, 512, 1536),
    (2560, NONE, 2048, NONE, 1024, 0, 1536, 512),
)


def solution(mesh):
    row_spec = P(('dp', 'sp'), None)

    def local_step(hidden, memory, mem_len, norm_self, norm_cross, norm_mlp, self_q, self_k, self_v, self_o, cross_q, cross_k, cross_v, cross_o, mlp_gate, mlp_up, mlp_down):
        layers, width = norm_self.shape
        w_so = self_o.reshape(layers, width, width)
        w_co = cross_o.reshape(layers, width, width)
        dev = lax.axis_index('sp')
        dev_arr = dev.astype(jnp.int32).reshape(1)
        bases = jnp.array(BASES, jnp.int32)[dev]
        lims = jnp.clip(mem_len[0] - bases, 0, CH)
        is3 = (dev_arr == 3).astype(jnp.int32)

        def swap(x):
            return lax.ppermute(x, 'sp', [(0, 1), (1, 0), (2, 3), (3, 2)])

        def earlier_rows(h):
            s2 = lax.ppermute(h, 'sp', [(0, 2), (1, 3)])
            s1 = lax.ppermute(h, 'sp', [(0, 1), (2, 3)])
            s3 = lax.ppermute(s2, 'sp', [(2, 3), (3, 2)])
            return s1, s2, s3

        def program(hidden):
            blocks = earlier_rows(hidden)
            mem_a, mem_b = memory[:CH], memory[CH:]
            c2b = lax.ppermute(mem_b, 'sp', [(2, 3)])
            rem_a = lax.ppermute(mem_a, 'sp', [(0, 2), (1, 3), (2, 0)])
            rem_b = lax.ppermute(mem_b, 'sp', [(0, 2), (1, 3), (2, 1)])

            both = (0, layers)
            ka, va = kv_project(lims[0:2], is3, [memory, c2b], cross_k, cross_v, 2 * CH, both)
            kas, vas = swap(ka), swap(va)
            kvs = []
            for layer in range(layers):
                kvs.append([(ka, va, layer), (kas, vas, layer)])
            for layer in range(layers):
                for rem, at in ((rem_a, 4), (rem_b, 6)):
                    k, v = kv_project(lims[at:at + 1], is3, [rem], cross_k, cross_v, CH, (layer, 1))
                    kvs[layer] += [(k, v, 0), (swap(k), swap(v), 0)]

            for layer in range(layers):
                hidden, q = self_attention(layer, dev_arr, hidden, *blocks, norm_self, norm_cross, self_q, self_k, self_v, w_so, cross_q)
                hidden = cross_mlp(layer, lims, q, hidden, norm_mlp, kvs[layer], w_co, mlp_gate, mlp_up, mlp_down)
                if layer + 1 < layers:
                    blocks = earlier_rows(hidden)
            return hidden

        return program(hidden)

    return jax.shard_map(local_step, mesh=mesh, in_specs=(row_spec, row_spec, P('dp')) + (P(),) * 14, out_specs=row_spec, check_vma=False)
```

profile of v0, /device:TPU:7, one launch (start us, length us, event | category | flops | bytes accessed | tf_op | source)
XLA Modules:
  0.0 290.0 jit_solution(16732563091546214459)
XLA Ops:
  0.0 3.6 %fusion = (bf16[512,1280]{1,0:T(8,128)(2,1)}, bf16[512,1280]{1,0:T(8,128)(2,1)}) fusion(bf16[1024,1280]{1,0:T(8,128)(2,1)} %refs_0_.1), kind=kLoop, calls=%fused_computation.2 | loop fusion | bytes 5242880 | tf_op jit(solution)/shard_map/slice | solution.py:472
  3.6 1.3 collective-permute-start.3
  5.6 0.0 copy-start.8
  5.6 3.3 %collective-permute-done.3.refs_1_ = bf16[512,1280]{1,0:T(8,128)(2,1)} collective-permute-done((bf16[512,1280]{1,0:T(8,128)(2,1)}, bf16[512,1280]{1,0:T(8,128)(2,1)}, u32[]{:S(2)}, u32[]{:S(2)}) %collective-permute-start.3) | collective-permute-done | bytes 1310752 | tf_op jit(solution)/shard_map/ppermute | solution.py:473
  8.9 5.8 %kv_project.5 = (bf16[2,1024,1280]{2,1,0:T(8,128)(2,1)}, bf16[2,1280,1024]{2,1,0:T(8,128)(2,1)}) custom-call(s32[2]{0:T(128)S(1)} %slice_bitcast_fusion.lim_ref, s32[1]{0:T(128)S(6)} %convert_element_type.3.pick_ref, bf16[1024,1280]{1,0:T(8,128)(2,1)S(1)} %copy-done.2, bf16[512,1280]{1,0:T(8,128)(2,1)} %collective-permute-done.3.refs_1_, ...), custom_call_target="tpu_custom_call" | custom-call | flops 13421772800 | bytes 13107200 | tf_op jit(solution)/shard_map/kv_project/pallas_call | solution.py:98
  14.6 0.0 collective-permute-start.4
  14.7 0.5 collective-permute-start.9
  15.2 1.3 collective-permute-start.5
  16.5 1.3 collective-permute-start.7
  17.8 1.3 collective-permute-start.1
  19.1 0.7 fusion.1
  19.7 37.4 %collective-permute-done.5.refs_0_ = bf16[512,1280]{1,0:T(8,128)(2,1)S(1)} collective-permute-done((bf16[512,1280]{1,0:T(8,128)(2,1)S(1)}, bf16[512,1280]{1,0:T(8,128)(2,1)S(1)}, u32[]{:S(2)}, u32[]{:S(2)}) %collective-permute-start.5) | collective-permute-done | bytes 1310752 | tf_op jit(solution)/shard_map/ppermute | solution.py:474
  57.1 8.0 %kv_project.6 = (bf16[1,512,1280]{2,1,0:T(8,128)(2,1)S(1)}, bf16[1,1280,512]{2,1,0:T(8,128)(2,1)}) custom-call(s32[1]{0:T(128)} %bitcast.5.lim_ref, s32[1]{0:T(128)S(6)} %convert_element_type.3.pick_ref, bf16[512,1280]{1,0:T(8,128)(2,1)S(1)} %collective-permute-done.5.refs_0_, bf16[2,1280,1280]{2,1,0:T(8,128)(2,1)} %refs_1_.7, bf16[2,1280,1280]{2,1,0:T(8,128)(2,1)} %refs_2_.9), custom_call_target="tpu_custom_call" | custom-call | flops 3355443200 | bytes 6553600 | tf_op jit(solution)/shard_map/kv_project/pallas_call | solution.py:98
  65.1 3.0 %collective-permute-start.6 = (bf16[1,512,1280]{2,1,0:T(8,128)(2,1)S(1)}, bf16[1,512,1280]{2,1,0:T(8,128)(2,1)S(1)}, u32[]{:S(2)}, u32[]{:S(2)}) collective-permute-start(bf16[1,512,1280]{2,1,0:T(8,128)(2,1)S(1)} %get-tuple-element.22.refs_2_), channel_id=1, source_target_pairs={{0,1},{1,0},{2,3},{3,2},{4,5},{5,4},{6,7},{7,6}} | collective-permute-start | bytes 3932168 | tf_op jit(solution)/shard_map/ppermute | solution.py:462
  68.1 31.1 %collective-permute-done.1.s2_ref = bf16[256,1280]{1,0:T(8,128)(2,1)S(1)} collective-permute-done((bf16[256,1280]{1,0:T(8,128)(2,1)S(1)}, bf16[256,1280]{1,0:T(8,128)(2,1)S(1)}, u32[]{:S(2)}, u32[]{:S(2)}) %collective-permute-start.1) | collective-permute-done | bytes 655392 | tf_op jit(solution)/shard_map/ppermute | solution.py:465
  99.2 1.3 collective-permute-start
  100.5 0.0 collective-permute-done.7.refs_0_
  100.5 3.6 %collective-permute-start.2 = (bf16[256,1280]{1,0:T(8,128)(2,1)S(1)}, bf16[256,1280]{1,0:T(8,128)(2,1)S(1)}, u32[]{:S(2)}, u32[]{:S(2)}) collective-permute-start(bf16[256,1280]{1,0:T(8,128)(2,1)S(1)} %collective-permute-done.1.s2_ref), channel_id=1, source_target_pairs={{2,3},{3,2},{6,7},{7,6}} | collective-permute-start | bytes 1966088 | tf_op jit(solution)/shard_map/ppermute | solution.py:467
  104.2 7.9 %kv_project.7 = (bf16[1,512,1280]{2,1,0:T(8,128)(2,1)}, bf16[1,1280,512]{2,1,0:T(8,128)(2,1)}) custom-call(s32[1]{0:T(128)} %bitcast.6.lim_ref, s32[1]{0:T(128)S(6)} %convert_element_type.3.pick_ref, bf16[512,1280]{1,0:T(8,128)(2,1)S(1)} %collective-permute-done.7.refs_0_, bf16[2,1280,1280]{2,1,0:T(8,128)(2,1)} %refs_1_.7, bf16[2,1280,1280]{2,1,0:T(8,128)(2,1)} %refs_2_.9), custom_call_target="tpu_custom_call" | custom-call | flops 3355443200 | bytes 6553600 | tf_op jit(solution)/shard_map/kv_project/pallas_call | solution.py:98
  112.1 0.0 collective-permute-done.s1_ref
  112.1 0.0 copy-start.11
  112.2 0.0 collective-permute-start.8
  112.2 0.0 collective-permute-done.2.s3_ref
  112.2 0.5 collective-permute-start.10
  112.7 0.0 collective-permute-done.6.refs_3_
  112.7 1.1 copy-done.4
  113.8 0.1 collective-permute-start.11
  113.9 0.5 fusion.2.lim_ref
  114.5 26.4 %self_attention.2 = (bf16[256,1280]{1,0:T(8,128)(2,1)}, bf16[256,1280]{1,0:T(8,128)(2,1)}) custom-call(s32[1]{0:T(128)} %bitcast.2.dev_ref, bf16[256,1280]{1,0:T(8,128)(2,1)} %own_ref.1, bf16[256,1280]{1,0:T(8,128)(2,1)} %copy-done.11, bf16[256,1280]{1,0:T(8,128)(2,1)} %copy-done.9, bf16[256,1280]{1,0:T(8,128)(2,1)} %copy-done.12, bf16[2,1280]{1,0:T(2,128)(2,1)} %gs_ref.3, ...), custom_call_target="tpu_custom_call" | custom-call | flops 10569646080 | bytes 16384000 | tf_op jit(solution)/shard_map/self_attention/pallas_call | solution.py:274
  140.9 0.0 collective-permute-done.8.refs_5_
  140.9 0.0 collective-permute-done.11.refs_11_
  140.9 0.0 collective-permute-done.4.refs_1_
  140.9 41.0 %cross_mlp.2.own_ref = bf16[256,1280]{1,0:T(8,128)(2,1)} custom-call(s32[8]{0:T(128)} %fusion.2.lim_ref, bf16[256,1280]{1,0:T(8,128)(2,1)} %get-tuple-element.19.q_ref, bf16[256,1280]{1,0:T(8,128)(2,1)} %get-tuple-element.20.hid_ref, bf16[2,1280]{1,0:T(2,128)(2,1)} %gm_ref.3, bf16[2,1024,1280]{2,1,0:T(8,128)(2,1)} %get-tuple-element.21.refs_0_, ...), custom_call_target="tpu_custom_call" | custom-call | flops 14931722240 | bytes 42598400 | tf_op jit(solution)/shard_map/cross_mlp/pallas_call | solution.py:410
  181.9 1.3 collective-permute-start.13
  183.2 1.3 collective-permute-start.12
  184.5 15.4 %collective-permute-done.13.s2_ref = bf16[256,1280]{1,0:T(8,128)(2,1)S(1)} collective-permute-done((bf16[256,1280]{1,0:T(8,128)(2,1)}, bf16[256,1280]{1,0:T(8,128)(2,1)S(1)}, u32[]{:S(2)}, u32[]{:S(2)}) %collective-permute-start.13) | collective-permute-done | bytes 655392 | tf_op jit(solution)/shard_map/ppermute | solution.py:465
  199.9 3.1 %collective-permute-start.14 = (bf16[256,1280]{1,0:T(8,128)(2,1)S(1)}, bf16[256,1280]{1,0:T(8,128)(2,1)}, u32[]{:S(2)}, u32[]{:S(2)}) collective-permute-start(bf16[256,1280]{1,0:T(8,128)(2,1)S(1)} %collective-permute-done.13.s2_ref), channel_id=1, source_target_pairs={{2,3},{3,2},{6,7},{7,6}} | collective-permute-start | bytes 1966088 | tf_op jit(solution)/shard_map/ppermute | solution.py:467
  203.1 1.3 copy-done.1
  204.4 7.9 %kv_project.8 = (bf16[1,512,1280]{2,1,0:T(8,128)(2,1)}, bf16[1,1280,512]{2,1,0:T(8,128)(2,1)}) custom-call(s32[1]{0:T(128)} %bitcast.5.lim_ref, s32[1]{0:T(128)S(6)} %convert_element_type.3.pick_ref, bf16[512,1280]{1,0:T(8,128)(2,1)S(1)} %copy-done.1, bf16[2,1280,1280]{2,1,0:T(8,128)(2,1)} %refs_1_.7, bf16[2,1280,1280]{2,1,0:T(8,128)(2,1)} %refs_2_.9), custom_call_target="tpu_custom_call" | custom-call | flops 3355443200 | bytes 6553600 | tf_op jit(solution)/shard_map/kv_project/pallas_call | solution.py:98
  212.3 0.0 collective-permute-start.15
  212.4 8.0 %kv_project.9 = (bf16[1,512,1280]{2,1,0:T(8,128)(2,1)}, bf16[1,1280,512]{2,1,0:T(8,128)(2,1)}) custom-call(s32[1]{0:T(128)} %bitcast.6.lim_ref, s32[1]{0:T(128)S(6)} %convert_element_type.3.pick_ref, bf16[512,1280]{1,0:T(8,128)(2,1)S(1)} %collective-permute-done.7.refs_0_, bf16[2,1280,1280]{2,1,0:T(8,128)(2,1)} %refs_1_.7, bf16[2,1280,1280]{2,1,0:T(8,128)(2,1)} %refs_2_.9), custom_call_target="tpu_custom_call" | custom-call | flops 3355443200 | bytes 6553600 | tf_op jit(solution)/shard_map/kv_project/pallas_call | solution.py:98
  220.3 0.5 collective-permute-start.16
  220.8 0.0 collective-permute-start.17
  220.9 0.5 collective-permute-start.18
  221.3 26.4 %self_attention.3 = (bf16[256,1280]{1,0:T(8,128)(2,1)}, bf16[256,1280]{1,0:T(8,128)(2,1)}) custom-call(s32[1]{0:T(128)} %bitcast.2.dev_ref, bf16[256,1280]{1,0:T(8,128)(2,1)} %cross_mlp.2.own_ref, bf16[256,1280]{1,0:T(8,128)(2,1)} %collective-permute-done.12.s1_ref, bf16[256,1280]{1,0:T(8,128)(2,1)} %copy-done.10, ...), custom_call_target="tpu_custom_call" | custom-call | flops 10569646080 | bytes 16384000 | tf_op jit(solution)/shard_map/self_attention/pallas_call | solution.py:274
  247.7 0.0 collective-permute-done.16.refs_5_
  247.8 1.0 copy-done.5
  248.8 41.0 %cross_mlp.3 = bf16[256,1280]{1,0:T(8,128)(2,1)} custom-call(s32[8]{0:T(128)} %fusion.2.lim_ref, bf16[256,1280]{1,0:T(8,128)(2,1)} %get-tuple-element.27.q_ref, bf16[256,1280]{1,0:T(8,128)(2,1)} %get-tuple-element.28.hid_ref, bf16[2,1280]{1,0:T(2,128)(2,1)} %gm_ref.3, bf16[2,1024,1280]{2,1,0:T(8,128)(2,1)} %get-tuple-element.21.refs_0_, ...), custom_call_target="tpu_custom_call" | custom-call | flops 14931722240 | bytes 42598400 | tf_op jit(solution)/shard_map/cross_mlp/pallas_call | solution.py:410
  (30 shorter events, 0.1 us)
Async XLA Ops:
  0.0 5.5 %copy-start.7 = (s32[4,8]{1,0:T(4,128)S(1)}, s32[4,8]{1,0:T(4,128)}, u32[]{:S(2)}) copy-start(s32[4,8]{1,0:T(4,128)} %constant.14.clone) | copy-start | bytes 388
  0.0 8.9 %copy-start.2 = (bf16[1024,1280]{1,0:T(8,128)(2,1)S(1)}, bf16[1024,1280]{1,0:T(8,128)(2,1)}, u32[]{:S(2)}) copy-start(bf16[1024,1280]{1,0:T(8,128)(2,1)} %refs_0_.1) | copy-start | bytes 7864324
  3.6 5.3 %collective-permute-start.3 = (bf16[512,1280]{1,0:T(8,128)(2,1)}, bf16[512,1280]{1,0:T(8,128)(2,1)}, u32[]{:S(2)}, u32[]{:S(2)}) collective-permute-start(bf16[512,1280]{1,0:T(8,128)(2,1)} %get-tuple-element.34), channel_id=1, source_target_pairs={{2,3},{6,7}} | collective-permute-start | bytes 3932168 | tf_op jit(solution)/shard_map/ppermute | solution.py:473
  5.6 9.6 %copy-start.6 = (bf16[512,1280]{1,0:T(8,128)(2,1)S(1)}, bf16[512,1280]{1,0:T(8,128)(2,1)}, u32[]{:S(2)}) copy-start(bf16[512,1280]{1,0:T(8,128)(2,1)} %get-tuple-element.33) | copy-start | bytes 3932164
  5.6 12.2 %copy-start.8 = (bf16[256,1280]{1,0:T(8,128)(2,1)S(1)}, bf16[256,1280]{1,0:T(8,128)(2,1)}, u32[]{:S(2)}) copy-start(bf16[256,1280]{1,0:T(8,128)(2,1)} %own_ref.1) | copy-start | bytes 1966084
  14.6 126.3 %collective-permute-start.4 = (bf16[2,1024,1280]{2,1,0:T(8,128)(2,1)}, bf16[2,1024,1280]{2,1,0:T(8,128)(2,1)}, u32[]{:S(2)}, u32[]{:S(2)}) collective-permute-start(bf16[2,1024,1280]{2,1,0:T(8,128)(2,1)} %get-tuple-element.21.refs_0_), channel_id=1, source_target_pairs={{0,1},{1,0},{2,3},{3,2},{4,5},{5,4},{6,7},{7,6}} | collective-permute-start | bytes 15728648 | tf_op jit(solution)/shard_map/ppermute | solution.py:462
  14.7 126.2 %collective-permute-start.9 = (bf16[2,1280,1024]{2,1,0:T(8,128)(2,1)}, bf16[2,1280,1024]{2,1,0:T(8,128)(2,1)}, u32[]{:S(2)}, u32[]{:S(2)}) collective-permute-start(bf16[2,1280,1024]{2,1,0:T(8,128)(2,1)} %get-tuple-element.24.refs_6_), channel_id=1, source_target_pairs={{0,1},{1,0},{2,3},{3,2},{4,5},{5,4},{6,7},{7,6}} | collective-permute-start | bytes 15728648 | tf_op jit(solution)/shard_map/ppermute | solution.py:462
  15.2 41.9 %collective-permute-start.5 = (bf16[512,1280]{1,0:T(8,128)(2,1)S(1)}, bf16[512,1280]{1,0:T(8,128)(2,1)S(1)}, u32[]{:S(2)}, u32[]{:S(2)}) collective-permute-start(bf16[512,1280]{1,0:T(8,128)(2,1)S(1)} %copy-done.6), channel_id=1, source_target_pairs={{0,2},{1,3},{2,0},{4,6},{5,7},{6,4}} | collective-permute-start | bytes 3932168 | tf_op jit(solution)/shard_map/ppermute | solution.py:474
  16.5 84.1 %collective-permute-start.7 = (bf16[512,1280]{1,0:T(8,128)(2,1)}, bf16[512,1280]{1,0:T(8,128)(2,1)S(1)}, u32[]{:S(2)}, u32[]{:S(2)}) collective-permute-start(bf16[512,1280]{1,0:T(8,128)(2,1)} %get-tuple-element.34), channel_id=1, source_target_pairs={{0,2},{1,3},{2,1},{4,6},{5,7},{6,5}} | collective-permute-start | bytes 3932168 | tf_op jit(solution)/shard_map/ppermute | solution.py:475
  17.8 81.5 %collective-permute-start.1 = (bf16[256,1280]{1,0:T(8,128)(2,1)S(1)}, bf16[256,1280]{1,0:T(8,128)(2,1)S(1)}, u32[]{:S(2)}, u32[]{:S(2)}) collective-permute-start(bf16[256,1280]{1,0:T(8,128)(2,1)S(1)} %copy-done.8), channel_id=1, source_target_pairs={{0,2},{1,3},{4,6},{5,7}} | collective-permute-start | bytes 1966088 | tf_op jit(solution)/shard_map/ppermute | solution.py:465
  57.1 8.0 %copy-start = (bf16[512,1280]{1,0:T(8,128)(2,1)}, bf16[512,1280]{1,0:T(8,128)(2,1)S(1)}, u32[]{:S(2)}) copy-start(bf16[512,1280]{1,0:T(8,128)(2,1)S(1)} %collective-permute-done.5.refs_0_) | copy-start | bytes 3932164
  65.1 47.0 %copy-start.3 = (bf16[1,512,1280]{2,1,0:T(8,128)(2,1)}, bf16[1,512,1280]{2,1,0:T(8,128)(2,1)S(1)}, u32[]{:S(2)}) copy-start(bf16[1,512,1280]{2,1,0:T(8,128)(2,1)S(1)} %get-tuple-element.22.refs_2_) | copy-start | bytes 3932164
  65.1 47.6 %collective-permute-start.6 = (bf16[1,512,1280]{2,1,0:T(8,128)(2,1)S(1)}, bf16[1,512,1280]{2,1,0:T(8,128)(2,1)S(1)}, u32[]{:S(2)}, u32[]{:S(2)}) collective-permute-start(bf16[1,512,1280]{2,1,0:T(8,128)(2,1)S(1)} %get-tuple-element.22.refs_2_), channel_id=1, source_target_pairs={{0,1},{1,0},{2,3},{3,2},{4,5},{5,4},{6,7},{7,6}} | collective-permute-start | bytes 3932168 | tf_op jit(solution)/shard_map/ppermute | solution.py:462
  99.2 12.9 %copy-start.9 = (bf16[256,1280]{1,0:T(8,128)(2,1)}, bf16[256,1280]{1,0:T(8,128)(2,1)S(1)}, u32[]{:S(2)}) copy-start(bf16[256,1280]{1,0:T(8,128)(2,1)S(1)} %collective-permute-done.1.s2_ref) | copy-start | bytes 1966084
  99.2 12.9 %collective-permute-start = (bf16[256,1280]{1,0:T(8,128)(2,1)S(1)}, bf16[256,1280]{1,0:T(8,128)(2,1)S(1)}, u32[]{:S(2)}, u32[]{:S(2)}) collective-permute-start(bf16[256,1280]{1,0:T(8,128)(2,1)S(1)} %copy-done.8), channel_id=1, source_target_pairs={{0,1},{2,3},{4,5},{6,7}} | collective-permute-start | bytes 1966088 | tf_op jit(solution)/shard_map/ppermute | solution.py:466
  100.5 11.7 %collective-permute-start.2 = (bf16[256,1280]{1,0:T(8,128)(2,1)S(1)}, bf16[256,1280]{1,0:T(8,128)(2,1)S(1)}, u32[]{:S(2)}, u32[]{:S(2)}) collective-permute-start(bf16[256,1280]{1,0:T(8,128)(2,1)S(1)} %collective-permute-done.1.s2_ref), channel_id=1, source_target_pairs={{2,3},{3,2},{6,7},{7,6}} | collective-permute-start | bytes 1966088 | tf_op jit(solution)/shard_map/ppermute | solution.py:467
  112.1 2.3 copy-start.11
  112.2 28.7 %collective-permute-start.8 = (bf16[1,512,1280]{2,1,0:T(8,128)(2,1)}, bf16[1,512,1280]{2,1,0:T(8,128)(2,1)}, u32[]{:S(2)}, u32[]{:S(2)}) collective-permute-start(bf16[1,512,1280]{2,1,0:T(8,128)(2,1)} %get-tuple-element.23.refs_4_), channel_id=1, source_target_pairs={{0,1},{1,0},{2,3},{3,2},{4,5},{5,4},{6,7},{7,6}} | collective-permute-start | bytes 3932168 | tf_op jit(solution)/shard_map/ppermute | solution.py:462
  112.2 2.3 copy-start.12
  112.2 28.7 %collective-permute-start.10 = (bf16[1,1280,512]{2,1,0:T(8,128)(2,1)}, bf16[1,1280,512]{2,1,0:T(8,128)(2,1)}, u32[]{:S(2)}, u32[]{:S(2)}) collective-permute-start(bf16[1,1280,512]{2,1,0:T(8,128)(2,1)} %get-tuple-element.25.refs_8_), channel_id=1, source_target_pairs={{0,1},{1,0},{2,3},{3,2},{4,5},{5,4},{6,7},{7,6}} | collective-permute-start | bytes 3932168 | tf_op jit(solution)/shard_map/ppermute | solution.py:462
  112.7 1.1 copy-start.4
  113.8 27.1 %collective-permute-start.11 = (bf16[1,1280,512]{2,1,0:T(8,128)(2,1)}, bf16[1,1280,512]{2,1,0:T(8,128)(2,1)}, u32[]{:S(2)}, u32[]{:S(2)}) collective-permute-start(bf16[1,1280,512]{2,1,0:T(8,128)(2,1)} %get-tuple-element.26.refs_10_), channel_id=1, source_target_pairs={{0,1},{1,0},{2,3},{3,2},{4,5},{5,4},{6,7},{7,6}} | collective-permute-start | bytes 3932168 | tf_op jit(solution)/shard_map/ppermute | solution.py:462
  181.9 18.0 %collective-permute-start.13 = (bf16[256,1280]{1,0:T(8,128)(2,1)}, bf16[256,1280]{1,0:T(8,128)(2,1)S(1)}, u32[]{:S(2)}, u32[]{:S(2)}) collective-permute-start(bf16[256,1280]{1,0:T(8,128)(2,1)} %cross_mlp.2.own_ref), channel_id=1, source_target_pairs={{0,2},{1,3},{4,6},{5,7}} | collective-permute-start | bytes 1966088 | tf_op jit(solution)/shard_map/ppermute | solution.py:465
  183.2 37.6 %collective-permute-start.12 = (bf16[256,1280]{1,0:T(8,128)(2,1)}, bf16[256,1280]{1,0:T(8,128)(2,1)}, u32[]{:S(2)}, u32[]{:S(2)}) collective-permute-start(bf16[256,1280]{1,0:T(8,128)(2,1)} %cross_mlp.2.own_ref), channel_id=1, source_target_pairs={{0,1},{2,3},{4,5},{6,7}} | collective-permute-start | bytes 1966088 | tf_op jit(solution)/shard_map/ppermute | solution.py:466
  199.9 12.4 %copy-start.10 = (bf16[256,1280]{1,0:T(8,128)(2,1)}, bf16[256,1280]{1,0:T(8,128)(2,1)S(1)}, u32[]{:S(2)}) copy-start(bf16[256,1280]{1,0:T(8,128)(2,1)S(1)} %collective-permute-done.13.s2_ref) | copy-start | bytes 1966084
  199.9 21.4 %collective-permute-start.14 = (bf16[256,1280]{1,0:T(8,128)(2,1)S(1)}, bf16[256,1280]{1,0:T(8,128)(2,1)}, u32[]{:S(2)}, u32[]{:S(2)}) collective-permute-start(bf16[256,1280]{1,0:T(8,128)(2,1)S(1)} %collective-permute-done.13.s2_ref), channel_id=1, source_target_pairs={{2,3},{3,2},{6,7},{7,6}} | collective-permute-start | bytes 1966088 | tf_op jit(solution)/shard_map/ppermute | solution.py:467
  203.1 1.3 copy-start.1
  212.3 35.4 %collective-permute-start.15 = (bf16[1,512,1280]{2,1,0:T(8,128)(2,1)}, bf16[1,512,1280]{2,1,0:T(8,128)(2,1)}, u32[]{:S(2)}, u32[]{:S(2)}) collective-permute-start(bf16[1,512,1280]{2,1,0:T(8,128)(2,1)} %get-tuple-element.29.refs_2_), channel_id=1, source_target_pairs={{0,1},{1,0},{2,3},{3,2},{4,5},{5,4},{6,7},{7,6}} | collective-permute-start | bytes 3932168 | tf_op jit(solution)/shard_map/ppermute | solution.py:462
  220.3 27.4 %collective-permute-start.16 = (bf16[1,512,1280]{2,1,0:T(8,128)(2,1)}, bf16[1,512,1280]{2,1,0:T(8,128)(2,1)S(1)}, u32[]{:S(2)}, u32[]{:S(2)}) collective-permute-start(bf16[1,512,1280]{2,1,0:T(8,128)(2,1)} %get-tuple-element.30.refs_4_), channel_id=1, source_target_pairs={{0,1},{1,0},{2,3},{3,2},{4,5},{5,4},{6,7},{7,6}} | collective-permute-start | bytes 3932168 | tf_op jit(solution)/shard_map/ppermute | solution.py:462
  220.8 27.0 %collective-permute-start.17 = (bf16[1,1280,512]{2,1,0:T(8,128)(2,1)}, bf16[1,1280,512]{2,1,0:T(8,128)(2,1)}, u32[]{:S(2)}, u32[]{:S(2)}) collective-permute-start(bf16[1,1280,512]{2,1,0:T(8,128)(2,1)} %get-tuple-element.31.refs_8_), channel_id=1, source_target_pairs={{0,1},{1,0},{2,3},{3,2},{4,5},{5,4},{6,7},{7,6}} | collective-permute-start | bytes 3932168 | tf_op jit(solution)/shard_map/ppermute | solution.py:462
  220.9 26.9 %collective-permute-start.18 = (bf16[1,1280,512]{2,1,0:T(8,128)(2,1)}, bf16[1,1280,512]{2,1,0:T(8,128)(2,1)}, u32[]{:S(2)}, u32[]{:S(2)}) collective-permute-start(bf16[1,1280,512]{2,1,0:T(8,128)(2,1)} %get-tuple-element.32.refs_10_), channel_id=1, source_target_pairs={{0,1},{1,0},{2,3},{3,2},{4,5},{5,4},{6,7},{7,6}} | collective-permute-start | bytes 3932168 | tf_op jit(solution)/shard_map/ppermute | solution.py:462
  247.8 1.1 copy-start.5
where the time goes:
time: 290 us
  Pallas kernels  172 us (59%)
  waiting for transfers between devices  87.2 us (30%)
  starting transfers between devices  21 us (7%)
  local copies, waits for them, and re-layouts  7.79 us (3%)
    pallas_call x2, Pallas kernels, cross_mlp(): pl.pallas_call(functools.partial(cross_kernel, layer, planes, n), in_spec...  82 us
    pallas_call x2, Pallas kernels, self_attention(): pl.pallas_call(functools.partial(self_kernel, layer), in_specs=[SMEM] + [...  52.8 us
    ppermute x2, waiting for transfers between devices, earlier_rows(): s2 = lax.ppermute(h, 'sp', [(0, 2), (1, 3)])  46.5 us
    pallas_call x5, Pallas kernels, kv_project(): pl.pallas_call(functools.partial(kv_kernel, layers, len(srcs)), in_specs=...  37.5 us
    ppermute x1, waiting for transfers between devices, program(): rem_a = lax.ppermute(mem_a, 'sp', [(0, 2), (1, 3), (2, 0)])  37.4 us
    ppermute x2, starting transfers between devices, earlier_rows(): s3 = lax.ppermute(s2, 'sp', [(2, 3), (3, 2)])  6.77 us
  transfers between devices with their start and end apart: 19, of which 4 were waited for; matrix products, arithmetic and copies ran while one was open for 0% of the time, Pallas kernels for 29%

commit v1 on v0

--- a/solution.py
+++ b/solution.py
@@ -121,7 +121,9 @@
     return jnp.where(lane < 64, q, zero), jnp.where(lane < 64, zero, q)
 
 
-def attend_all(pairs, n_chunks, scores, values, enter, at_ref, s_refs, mx_refs, m_ref, l_ref, acc_ref):
+def attend_all(pairs, n_chunks, scores, values, enter, leave, scratch):
+    s_refs, mx_refs, (m_ref, l_ref, acc_ref) = scratch[:2], scratch[2:4], scratch[4:]
+
     def stage1(pair, j, buf):
         for h, s in enumerate(scores(pair, j)):
             s_refs[buf][h] = s
@@ -130,13 +132,13 @@
     def stage2(pair, j, buf):
         vt = values(pair, j)
         for h in range(2):
-            m_old = m_ref[h:h + 1, :]
+            m_old = m_ref[pair, h:h + 1, :]
             m_new = jnp.maximum(m_old, mx_refs[buf][h:h + 1, :])
             p = jnp.exp(s_refs[buf][h] - m_new)
             alpha = jnp.exp(m_old - m_new)
-            m_ref[h:h + 1, :] = m_new
-            l_ref[h:h + 1, :] = l_ref[h:h + 1, :] * alpha + jnp.sum(p, axis=0, keepdims=True)
-            acc_ref[h] = acc_ref[h] * alpha + dot(vt[h * 64:(h + 1) * 64, :], p.astype(BF16))
+            m_ref[pair, h:h + 1, :] = m_new
+            l_ref[pair, h:h + 1, :] = l_ref[pair, h:h + 1, :] * alpha + jnp.sum(p, axis=0, keepdims=True)
+            acc_ref[pair, h] = acc_ref[pair, h] * alpha + dot(vt[h * 64:(h + 1) * 64, :], p.astype(BF16))
 
     def advance(pair, j):
         wrap = j + 1 == n_chunks
@@ -150,12 +152,6 @@
         for buf in range(2):
             pair_next, j_next = advance(pair, j)
 
-            @pl.when(j == 0)
-            def _():
-                m_ref[...] = jnp.full_like(m_ref, -jnp.inf)
-                l_ref[...] = jnp.zeros_like(l_ref)
-                acc_ref[...] = jnp.zeros_like(acc_ref)
-
             @pl.when((j_next == 0) & (pair_next < pairs))
             def _(pair_next=pair_next):
                 enter(pair_next)
@@ -165,9 +161,7 @@
 
             @pl.when(j_next == 0)
             def _(pair=pair):
-                for h in range(2):
-                    rows = pl.ds(pl.multiple_of(pair * 128 + h * 64, 64), 64)
-                    at_ref[rows, :] = (acc_ref[h] / l_ref[h:h + 1, :]).astype(BF16)
+                leave(pair)
 
             pair, j = pair_next, j_next
         return pair, j
@@ -175,78 +169,165 @@
     lax.fori_loop(0, pairs * n_chunks // 2, step, (jnp.int32(0), jnp.int32(0)))
 
 
-def attend_scratch(rows):
-    return [pltpu.VMEM((2, CH, rows), F32)] * 2 + [pltpu.VMEM((2, rows), F32)] * 4 + [pltpu.VMEM((2, 64, rows), F32)]
-
-
-def self_kernel(layer, dev_ref, own_ref, s1_ref, s2_ref, s3_ref, gs_ref, gc_ref, wq, wk, wv, wo, wcq, hid_ref, q_ref,
-                w_s, x_s, k_s, vt_s, qs, bias, at_s, a_s, s0, s1, mx0, mx1, m_s, l_s, acc_s, sems):
+def attend_reset(scratch):
+    m_ref, l_ref, acc_ref = scratch[4:]
+    m_ref[...] = jnp.full_like(m_ref, -jnp.inf)
+    l_ref[...] = jnp.zeros_like(l_ref)
+    acc_ref[...] = jnp.zeros_like(acc_ref)
+
+
+def attend_finish(pair, at_ref, scratch):
+    l_ref, acc_ref = scratch[5:]
+    for h in range(2):
+        rows = pl.ds(pl.multiple_of(pair * 128 + h * 64, 64), 64)
+        at_ref[rows, :] = (acc_ref[pair, h] / l_ref[pair, h:h + 1, :]).astype(BF16)
+
+
+def attend_scratch(pairs, rows):
+    return [
+        pltpu.VMEM((2, CH, rows), F32),
+        pltpu.VMEM((2, CH, rows), F32),
+        pltpu.VMEM((2, rows), F32),
+        pltpu.VMEM((2, rows), F32),
+        pltpu.VMEM((pairs, 2, rows), F32),
+        pltpu.VMEM((pairs, 2, rows), F32),
+        pltpu.VMEM((pairs, 2, 64, rows), F32),
+    ]
+
+
+def self_kernel(layer, far_given, *refs):
+    own_ref, refs = refs[0], refs[1:]
+    if far_given:
+        s2, refs = refs[0], refs[1:]
+    gs_ref, gc_ref, wq, wk, wv, wo, wcq, hid_ref, q_ref, w_s, x_s, k_s, vt_s, qs, bias, at_s, a_s, s1, s3 = refs[:19]
+    refs = refs[19:]
+    if not far_given:
+        s2, refs = refs[0], refs[1:]
+    scratch, (sems, near_sems, far_sems, fwd_sems) = refs[:7], refs[7:]
     rows, width = own_ref.shape
     tiles = width // 256
-    dev = dev_ref[0]
+    parts = far_sems.shape[1]
+    dev = lax.axis_index("sp")
+    odd = lax.rem(dev, 2)
     chip1 = dev >= 2
+    sibling = dev + 1 - 2 * odd
+    across = lax.rem(dev + 2, 4)
 
     w_copies = [pltpu.make_async_copy(src.at[layer], w_s.at[n], sems.at[n]) for n, src in enumerate((wk, wv, wq, wo, wcq))]
     w_copies[0].start()
     w_copies[1].start()
 
+    barrier = pltpu.get_barrier_semaphore()
+    for other in (sibling, across):
+        pl.semaphore_signal(barrier, inc=1, device_id={"sp": other}, device_id_type=pl.DeviceIdType.MESH)
+    pl.semaphore_wait(barrier, 2)
+
+    def send(src, dst, sem, other):
+        return pltpu.make_async_remote_copy(src_ref=src, dst_ref=dst, send_sem=sem.at[0], recv_sem=sem.at[1],
+                                            device_id={"sp": other}, device_id_type=pl.DeviceIdType.MESH)
+
+    def part(i):
+        return pl.ds(i * (rows // parts), rows // parts)
+
+    near = send(own_ref, s1, near_sems, sibling)
+    far = [send(own_ref.at[part(i)], s2.at[part(i)], far_sems.at[:, i], across) for i in range(parts)]
+    fwd = [send(s2.at[part(i)], s3.at[part(i)], fwd_sems.at[:, i], sibling) for i in range(parts)]
+
+    if not far_given:
+        @pl.when(jnp.logical_not(chip1))
+        def _():
+            for cp in far:
+                cp.start()
+
+    @pl.when(odd == 0)
+    def _():
+        near.start()
+
+    if far_given:
+        @pl.when(chip1)
+        def _():
+            for cp in fwd:
+                cp.start()
+
     gain = gs_ref[layer:layer + 1, :]
     x_s[pl.ds(0, rows), :] = rms(own_ref[...], gain)
-    x_s[pl.ds(rows, rows), :] = rms(s1_ref[...], gain)
-
-    @pl.when(chip1)
-    def _():
-        x_s[pl.ds(2 * rows, rows), :] = rms(s2_ref[...], gain)
-        x_s[pl.ds(3 * rows, rows), :] = rms(s3_ref[...], gain)
-
     key = lax.broadcasted_iota(jnp.int32, (rows, rows), 0)
     query = lax.broadcasted_iota(jnp.int32, (rows, rows), 1)
     bias[pl.ds(0, rows), :] = jnp.where(key <= query, 0.0, NEG_BIG)
-    bias[pl.ds(rows, rows), :] = jnp.full((rows, rows), jnp.where(dev % 2 == 1, 0.0, NEG_BIG), F32)
-    bias[pl.ds(2 * rows, 2 * rows), :] = jnp.zeros((2 * rows, rows), F32)
+    bias[pl.ds(rows, rows), :] = jnp.full((rows, rows), jnp.where(odd == 1, 0.0, NEG_BIG), F32)
+    attend_reset(scratch)
+
+    @pl.when(odd == 1)
+    def _():
+        near.wait_recv()
+        x_s[pl.ds(rows, rows), :] = rms(s1[...], gain)
+
+    @pl.when(odd == 0)
+    def _():
+        x_s[pl.ds(rows, rows), :] = jnp.zeros((rows, width), BF16)
 
     def tile(t):
         return pl.ds(pl.multiple_of(t * 256, 256), 256)
 
-    def project(n, store):
-        w_copies[n].wait()
-        if n + 2 < len(w_copies):
-            w_copies[n + 2].start()
-
+    def project(n, first):
         def step(r, _):
-            at = tile(r)
-            store(at, dot(x_s[at, :], w_s[n]).astype(BF16))
+            at = tile(first + r)
+            out = dot(x_s[at, :], w_s[n]).astype(BF16)
+            if n == 0:
+                k_s[at, :] = out
+            else:
+                vt_s[:, at] = out.T
             return 0
 
-        lax.fori_loop(0, jnp.where(chip1, 4, 2), step, 0)
-
-    def store_k(at, out):
-        k_s[at, :] = out
-
-    def store_v(at, out):
-        vt_s[:, at] = out.T
-
-    project(0, store_k)
-    project(1, store_v)
+        lax.fori_loop(0, 2, step, 0)
+
+    def head_cols(i):
+        return pl.ds(pl.multiple_of(i * 128, 128), 128)
+
+    def attend(half, add):
+        at = pl.ds(half * CH, CH)
+
+        def scores(i, j):
+            k = k_s[at, head_cols(i)]
+            return [add(dot_nt(k, q)) for q in pair_queries(qs[:, head_cols(i)])]
+
+        attend_all(width // 128, 1, scores, lambda i, j: vt_s[head_cols(i), at], lambda i: None, lambda i: None, scratch)
+
+    w_copies[0].wait()
+    w_copies[2].start()
+    project(0, 0)
+    w_copies[1].wait()
+    w_copies[3].start()
+    project(1, 0)
     w_copies[2].wait()
     w_copies[4].start()
-    qs[...] = dot(x_s[pl.ds(0, rows), :], w_s[2]).astype(BF16) * BF16(0.125)
-
-    def chunk(j):
-        return pl.ds(pl.multiple_of(j * CH, CH), CH)
-
-    def head_cols(i):
-        return pl.ds(pl.multiple_of(i * 128, 128), 128)
-
-    def scores(i, j):
-        k = k_s[chunk(j), head_cols(i)]
-        return [dot_nt(k, q) + bias[chunk(j), :] for q in pair_queries(qs[:, head_cols(i)])]
-
-    def values(i, j):
-        return vt_s[head_cols(i), chunk(j)]
-
-    attend_all(width // 128, jnp.where(chip1, 2, 1), scores, values, lambda i: None, at_s, (s0, s1), (mx0, mx1), m_s, l_s, acc_s)
-
+
+    def project_q(t, _):
+        qs[:, tile(t)] = dot(x_s[pl.ds(0, rows), :], w_s[2, :, tile(t)]).astype(BF16) * BF16(0.125)
+        return 0
+
+    lax.fori_loop(0, tiles, project_q, 0)
+    attend(0, lambda s: s + bias[...])
+
+    @pl.when(chip1)
+    def _():
+        if not far_given:
+            for i in range(parts):
+                far[i].wait_recv()
+                fwd[i].start()
+        x_s[pl.ds(2 * rows, rows), :] = rms(s2[...], gain)
+        for cp in fwd:
+            cp.wait_recv()
+        x_s[pl.ds(3 * rows, rows), :] = rms(s3[...], gain)
+        project(0, 2)
+        project(1, 2)
+        attend(1, lambda s: s)
+
+    def finish(i, _):
+        attend_finish(i, at_s, scratch)
+        return 0
+
+    lax.fori_loop(0, width // 128, finish, 0)
     a_s[...] = at_s[...].T
     w_copies[3].wait()
 
@@ -266,14 +347,32 @@
 
     lax.fori_loop(0, tiles, project_cq, 0)
 
-
-def self_attention(layer, dev, own, s1, s2, s3, gs, gc, wq, wk, wv, wo, wcq):
+    @pl.when(odd == 0)
+    def _():
+        near.wait_send()
+
+    @pl.when(chip1)
+    def _():
+        for cp in fwd:
+            cp.wait_send()
+
+    if not far_given:
+        @pl.when(jnp.logical_not(chip1))
+        def _():
+            for cp in far:
+                cp.wait_send()
+
+
+def self_attention(layer, own, far, gs, gc, wq, wk, wv, wo, wcq):
     rows, width = own.shape
+    far_given = far is not None
+    parts = 1 if far_given else 4
     shape = jax.ShapeDtypeStruct((rows, width), BF16)
     flops = 2 * rows * width * width * 11 + 4 * rows * 4 * rows * width
+    block = pltpu.VMEM((rows, width), BF16)
     return pl.pallas_call(
-        functools.partial(self_kernel, layer),
-        in_specs=[SMEM] + [VMEM] * 6 + [ANY] * 5,
+        functools.partial(self_kernel, layer, far_given),
+        in_specs=[VMEM] * (4 if far_given else 3) + [ANY] * 5,
         out_specs=[VMEM, VMEM],
         out_shape=[shape, shape],
         scratch_shapes=[
@@ -281,23 +380,30 @@
             pltpu.VMEM((4 * rows, width), BF16),
             pltpu.VMEM((4 * rows, width), BF16),
             pltpu.VMEM((width, 4 * rows), BF16),
-            pltpu.VMEM((rows, width), BF16),
-            pltpu.VMEM((4 * rows, rows), F32),
+            block,
+            pltpu.VMEM((2 * rows, rows), F32),
             pltpu.VMEM((width, rows), BF16),
-            pltpu.VMEM((rows, width), BF16),
-            *attend_scratch(rows),
+            block,
+            block,
+            block,
+            *([] if far_given else [block]),
+            *attend_scratch(width // 128, rows),
             pltpu.SemaphoreType.DMA((5,)),
+            pltpu.SemaphoreType.DMA((2,)),
+            pltpu.SemaphoreType.DMA((2, parts)),
+            pltpu.SemaphoreType.DMA((2, parts)),
         ],
         cost_estimate=pl.CostEstimate(flops=flops, bytes_accessed=10 * width * width, transcendentals=0),
-        compiler_params=pltpu.CompilerParams(vmem_limit_bytes=VMEM_LIMIT),
+        compiler_params=pltpu.CompilerParams(vmem_limit_bytes=VMEM_LIMIT, collective_id=layer, has_side_effects=True),
         name="self_attention",
-    )(dev, own, s1, s2, s3, gs, gc, wq, wk, wv, wo, wcq)
+    )(own, *([far] if far_given else []), gs, gc, wq, wk, wv, wo, wcq)
 
 
 def cross_kernel(layer, planes, n_kv, lim_ref, q_ref, hid_ref, gm_ref, *refs):
     ks, vts = refs[:n_kv], refs[n_kv:2 * n_kv]
-    (wco, wg, wu, wd, out_ref, kbuf, vbuf, at_s, a_s, x_s, acc_o, s0, s1, mx0, mx1, m_s, l_s, acc_s, mask, list_s,
-     wo_s, wg_s, wu_s, wd_s, kv_sems, o_sem, w_sems) = refs[2 * n_kv:]
+    (wco, wg, wu, wd, out_ref, kbuf, vbuf, at_s, a_s, x_s, acc_o, mask, list_s, wo_s, wg_s, wu_s, wd_s,
+     kv_sems, o_sem, w_sems) = refs[2 * n_kv:-7]
+    scratch = refs[-7:]
     rows, width = q_ref.shape
     pairs = width // 128
     steps = wg_s.shape[0]
@@ -370,7 +476,8 @@
     def values(i, j):
         return vbuf[lax.rem(i, 3), :, chunk(j)]
 
-    attend_all(pairs, n_chunks, scores, values, enter, at_s, (s0, s1), (mx0, mx1), m_s, l_s, acc_s)
+    attend_reset(scratch)
+    attend_all(pairs, n_chunks, scores, values, enter, lambda i: attend_finish(i, at_s, scratch), scratch)
 
     a_s[...] = at_s[...].T
     o_copy.wait()
@@ -400,6 +507,7 @@
 
 def cross_mlp(layer, lims, q, hid, gm, kvs, wco, wg, wu, wd):
     rows, width = q.shape
+    pairs = width // 128
     steps = 10
     ff = wg.shape[2] // steps
     planes = tuple(plane for _, _, plane in kvs)
@@ -419,7 +527,6 @@
             pltpu.VMEM((rows, width), BF16),
             pltpu.VMEM((rows, width), BF16),
             pltpu.VMEM((rows, width), F32),
-            *attend_scratch(rows),
             pltpu.VMEM((2, CH, 128), BF16),
             pltpu.SMEM((8,), jnp.int32),
             pltpu.VMEM((width, width), BF16),
@@ -429,6 +536,7 @@
             pltpu.SemaphoreType.DMA((3, 2, n)),
             pltpu.SemaphoreType.DMA,
             pltpu.SemaphoreType.DMA((3, steps)),
+            *attend_scratch(pairs, rows),
         ],
         cost_estimate=pl.CostEstimate(flops=flops, bytes_accessed=2 * width * (width + 3 * wg.shape[2]), transcendentals=0),
         compiler_params=pltpu.CompilerParams(vmem_limit_bytes=VMEM_LIMIT),
@@ -461,14 +569,8 @@
         def swap(x):
             return lax.ppermute(x, 'sp', [(0, 1), (1, 0), (2, 3), (3, 2)])
 
-        def earlier_rows(h):
-            s2 = lax.ppermute(h, 'sp', [(0, 2), (1, 3)])
-            s1 = lax.ppermute(h, 'sp', [(0, 1), (2, 3)])
-            s3 = lax.ppermute(s2, 'sp', [(2, 3), (3, 2)])
-            return s1, s2, s3
-
         def program(hidden):
-            blocks = earlier_rows(hidden)
+            far = lax.ppermute(hidden, 'sp', [(0, 2), (1, 3)])
             mem_a, mem_b = memory[:CH], memory[CH:]
             c2b = lax.ppermute(mem_b, 'sp', [(2, 3)])
             rem_a = lax.ppermute(mem_a, 'sp', [(0, 2), (1, 3), (2, 0)])
@@ -486,10 +588,9 @@
                     kvs[layer] += [(k, v, 0), (swap(k), swap(v), 0)]
 
             for layer in range(layers):
-                hidden, q = self_attention(layer, dev_arr, hidden, *blocks, norm_self, norm_cross, self_q, self_k, self_v, w_so, cross_q)
+                hidden, q = self_attention(layer, hidden, far, norm_self, norm_cross, self_q, self_k, self_v, w_so, cross_q)
                 hidden = cross_mlp(layer, lims, q, hidden, norm_mlp, kvs[layer], w_co, mlp_gate, mlp_up, mlp_down)
-                if layer + 1 < layers:
-                    blocks = earlier_rows(hidden)
+                far = None
             return hidden
 
         return program(hidden)

time: 290 us -> 265 us (0.914)
  waiting for transfers between devices: 87.2 us -> 60.2 us
  Pallas kernels: 172 us -> 180 us
  starting transfers between devices: 21 us -> 14.5 us
    ppermute x6 -> x1, waiting for transfers between devices: 46.5 us -> 3.23 us  [program(): far = lax.ppermute(hidden, 'sp', [(0, 2), (1, 3)])]
    ppermute x1, waiting for transfers between devices: 0.01 us -> 15.1 us  [program(): rem_b = lax.ppermute(mem_b, 'sp', [(0, 2), (1, 3), (2, 1)])]
    ppermute x6 -> x1, starting transfers between devices: 11.9 us -> 1.28 us  [program(): far = lax.ppermute(hidden, 'sp', [(0, 2), (1, 3)])]
    pallas_call x2, Pallas kernels: 52.8 us -> 61.1 us  [self_attention(): pl.pallas_call(functools.partial(self_kernel, layer, far_given), in_specs...]
    ppermute x10, starting transfers between devices: 5.18 us -> 9.38 us  [swap(): return lax.ppermute(x, 'sp', [(0, 1), (1, 0), (2, 3), (3, 2)])]
  transfers between devices with their start and end apart: 19 -> 14, of which waited for: 4 -> 4; matrix products, arithmetic and copies ran while one was open for 0% -> 0% of each run, Pallas kernels for 29% -> 51%
where the time goes in v1:
time: 265 us; the launch traced here: 264 us
  Pallas kernels  180 us (68%)
  waiting for transfers between devices  60.2 us (23%)
  starting transfers between devices  14.5 us (5%)
  local copies, waits for them, and re-layouts  7.63 us (3%)
    pallas_call x2, Pallas kernels, cross_mlp(): pl.pallas_call(functools.partial(cross_kernel, layer, planes, n), in_spec...  81.6 us
    pallas_call x2, Pallas kernels, self_attention(): pl.pallas_call(functools.partial(self_kernel, layer, far_given), in_specs...  61.1 us
    ppermute x1, waiting for transfers between devices, program(): rem_a = lax.ppermute(mem_a, 'sp', [(0, 2), (1, 3), (2, 0)])  38.6 us
    pallas_call x5, Pallas kernels, kv_project(): pl.pallas_call(functools.partial(kv_kernel, layers, len(srcs)), in_specs=...  37.6 us
    ppermute x1, waiting for transfers between devices, program(): rem_b = lax.ppermute(mem_b, 'sp', [(0, 2), (1, 3), (2, 1)])  15.1 us
    ppermute x10, starting transfers between devices, swap(): return lax.ppermute(x, 'sp', [(0, 1), (1, 0), (2, 3), (3, 2)])  9.38 us
  transfers between devices with their start and end apart: 14, of which 4 were waited for; matrix products, arithmetic and copies ran while one was open for 0% of the time, Pallas kernels for 51%

profile of v1, /device:TPU:7, one launch (start us, length us, event | category | flops | bytes accessed | tf_op | source)
XLA Modules:
  0.0 264.3 jit_solution(970670624971513393)
XLA Ops:
  0.0 3.5 %fusion = (bf16[512,1280]{1,0:T(8,128)(2,1)}, bf16[512,1280]{1,0:T(8,128)(2,1)}) fusion(bf16[1024,1280]{1,0:T(8,128)(2,1)} %refs_0_.3), kind=kLoop, calls=%fused_computation.2 | loop fusion | bytes 5242880 | tf_op jit(solution)/shard_map/slice | solution.py:574
  3.5 1.3 collective-permute-start.1
  5.5 0.0 copy-done.7
  5.5 3.3 %collective-permute-done.1.refs_1_ = bf16[512,1280]{1,0:T(8,128)(2,1)} collective-permute-done((bf16[512,1280]{1,0:T(8,128)(2,1)}, bf16[512,1280]{1,0:T(8,128)(2,1)}, u32[]{:S(2)}, u32[]{:S(2)}) %collective-permute-start.1) | collective-permute-done | bytes 1310752 | tf_op jit(solution)/shard_map/ppermute | solution.py:575
  8.8 5.8 %kv_project.5 = (bf16[2,1024,1280]{2,1,0:T(8,128)(2,1)}, bf16[2,1280,1024]{2,1,0:T(8,128)(2,1)}) custom-call(s32[2]{0:T(128)S(1)} %slice_bitcast_fusion.lim_ref, s32[1]{0:T(128)} %bitcast.4.pick_ref, bf16[1024,1280]{1,0:T(8,128)(2,1)S(1)} %copy-done.2, bf16[512,1280]{1,0:T(8,128)(2,1)} %collective-permute-done.1.refs_1_, bf16[2,1280,1280]{2,1,0:T(8,128)(2,1)} %refs_1_.9, ...), custom_call_target="tpu_custom_call" | custom-call | flops 13421772800 | bytes 13107200 | tf_op jit(solution)/shard_map/kv_project/pallas_call | solution.py:98
  14.6 0.0 collective-permute-start.2
  14.6 0.5 collective-permute-start.7
  15.1 1.3 collective-permute-start.3
  16.4 1.3 collective-permute-start.5
  17.7 0.7 fusion.1
  18.4 38.6 %collective-permute-done.3.refs_0_ = bf16[512,1280]{1,0:T(8,128)(2,1)S(1)} collective-permute-done((bf16[512,1280]{1,0:T(8,128)(2,1)S(1)}, bf16[512,1280]{1,0:T(8,128)(2,1)S(1)}, u32[]{:S(2)}, u32[]{:S(2)}) %collective-permute-start.3) | collective-permute-done | bytes 1310752 | tf_op jit(solution)/shard_map/ppermute | solution.py:576
  57.0 8.1 %kv_project.6 = (bf16[1,512,1280]{2,1,0:T(8,128)(2,1)S(1)}, bf16[1,1280,512]{2,1,0:T(8,128)(2,1)}) custom-call(s32[1]{0:T(128)} %bitcast.5.lim_ref, s32[1]{0:T(128)} %bitcast.4.pick_ref, bf16[512,1280]{1,0:T(8,128)(2,1)S(1)} %collective-permute-done.3.refs_0_, bf16[2,1280,1280]{2,1,0:T(8,128)(2,1)} %refs_1_.9, bf16[2,1280,1280]{2,1,0:T(8,128)(2,1)} %refs_2_.13), custom_call_target="tpu_custom_call" | custom-call | flops 3355443200 | bytes 6553600 | tf_op jit(solution)/shard_map/kv_project/pallas_call | solution.py:98
  65.1 0.0 copy-done
  65.1 0.0 copy-start.3
  65.1 3.0 %collective-permute-start.4 = (bf16[1,512,1280]{2,1,0:T(8,128)(2,1)S(1)}, bf16[1,512,1280]{2,1,0:T(8,128)(2,1)S(1)}, u32[]{:S(2)}, u32[]{:S(2)}) collective-permute-start(bf16[1,512,1280]{2,1,0:T(8,128)(2,1)S(1)} %get-tuple-element.22.refs_2_), channel_id=1, source_target_pairs={{0,1},{1,0},{2,3},{3,2},{4,5},{5,4},{6,7},{7,6}} | collective-permute-start | bytes 3932168 | tf_op jit(solution)/shard_map/ppermute | solution.py:570
  68.1 1.3 collective-permute-start
  69.4 0.6 fusion.2.lim_ref
  70.0 15.1 %collective-permute-done.5.refs_0_ = bf16[512,1280]{1,0:T(8,128)(2,1)S(1)} collective-permute-done((bf16[512,1280]{1,0:T(8,128)(2,1)}, bf16[512,1280]{1,0:T(8,128)(2,1)S(1)}, u32[]{:S(2)}, u32[]{:S(2)}) %collective-permute-start.5) | collective-permute-done | bytes 1310752 | tf_op jit(solution)/shard_map/ppermute | solution.py:577
  85.1 7.8 %kv_project.7 = (bf16[1,512,1280]{2,1,0:T(8,128)(2,1)}, bf16[1,1280,512]{2,1,0:T(8,128)(2,1)}) custom-call(s32[1]{0:T(128)} %bitcast.6.lim_ref, s32[1]{0:T(128)} %bitcast.4.pick_ref, bf16[512,1280]{1,0:T(8,128)(2,1)S(1)} %collective-permute-done.5.refs_0_, bf16[2,1280,1280]{2,1,0:T(8,128)(2,1)} %refs_1_.9, bf16[2,1280,1280]{2,1,0:T(8,128)(2,1)} %refs_2_.13), custom_call_target="tpu_custom_call" | custom-call | flops 3355443200 | bytes 6553600 | tf_op jit(solution)/shard_map/kv_project/pallas_call | solution.py:98
  92.9 3.0 %collective-permute-start.6 = (bf16[1,512,1280]{2,1,0:T(8,128)(2,1)}, bf16[1,512,1280]{2,1,0:T(8,128)(2,1)}, u32[]{:S(2)}, u32[]{:S(2)}) collective-permute-start(bf16[1,512,1280]{2,1,0:T(8,128)(2,1)} %get-tuple-element.23.refs_4_), channel_id=1, source_target_pairs={{0,1},{1,0},{2,3},{3,2},{4,5},{5,4},{6,7},{7,6}} | collective-permute-start | bytes 3932168 | tf_op jit(solution)/shard_map/ppermute | solution.py:570
  95.9 3.2 %collective-permute-done.refs_1_ = bf16[256,1280]{1,0:T(8,128)(2,1)S(1)} collective-permute-done((bf16[256,1280]{1,0:T(8,128)(2,1)S(1)}, bf16[256,1280]{1,0:T(8,128)(2,1)S(1)}, u32[]{:S(2)}, u32[]{:S(2)}) %collective-permute-start) | collective-permute-done | bytes 655392 | tf_op jit(solution)/shard_map/ppermute | solution.py:573
  99.1 1.7 collective-permute-start.8
  100.8 0.0 collective-permute-done.4.refs_3_
  100.8 1.1 copy-done.4
  101.9 0.0 copy-done.9
  101.9 0.2 collective-permute-start.9
  102.1 28.4 %self_attention.2 = (bf16[256,1280]{1,0:T(8,128)(2,1)}, bf16[256,1280]{1,0:T(8,128)(2,1)}) custom-call(bf16[256,1280]{1,0:T(8,128)(2,1)} %refs_0_.2, bf16[256,1280]{1,0:T(8,128)(2,1)} %copy-done.9, bf16[2,1280]{1,0:T(2,128)(2,1)} %refs_1_.7, bf16[2,1280]{1,0:T(2,128)(2,1)} %refs_2_.11, bf16[2,1280,1280]{2,1,0:T(8,128)(2,1)} %refs_3_.5, ...), custom_call_target="tpu_custom_call" | custom-call | flops 10569646080 | bytes 16384000 | tf_op jit(solution)/shard_map/self_attention/pallas_call | solution.py:373
  130.5 0.0 copy-start.1
  130.5 1.3 copy-done.1
  131.8 8.0 %kv_project.8 = (bf16[1,512,1280]{2,1,0:T(8,128)(2,1)}, bf16[1,1280,512]{2,1,0:T(8,128)(2,1)}) custom-call(s32[1]{0:T(128)} %bitcast.5.lim_ref, s32[1]{0:T(128)} %bitcast.4.pick_ref, bf16[512,1280]{1,0:T(8,128)(2,1)S(1)} %copy-done.1, bf16[2,1280,1280]{2,1,0:T(8,128)(2,1)} %refs_1_.9, bf16[2,1280,1280]{2,1,0:T(8,128)(2,1)} %refs_2_.13), custom_call_target="tpu_custom_call" | custom-call | flops 3355443200 | bytes 6553600 | tf_op jit(solution)/shard_map/kv_project/pallas_call | solution.py:98
  139.8 7.9 %kv_project.9 = (bf16[1,512,1280]{2,1,0:T(8,128)(2,1)}, bf16[1,1280,512]{2,1,0:T(8,128)(2,1)}) custom-call(s32[1]{0:T(128)} %bitcast.6.lim_ref, s32[1]{0:T(128)} %bitcast.4.pick_ref, bf16[512,1280]{1,0:T(8,128)(2,1)S(1)} %collective-permute-done.5.refs_0_, bf16[2,1280,1280]{2,1,0:T(8,128)(2,1)} %refs_1_.9, bf16[2,1280,1280]{2,1,0:T(8,128)(2,1)} %refs_2_.13), custom_call_target="tpu_custom_call" | custom-call | flops 3355443200 | bytes 6553600 | tf_op jit(solution)/shard_map/kv_project/pallas_call | solution.py:98
  147.7 0.0 collective-permute-done.6.refs_5_
  147.7 0.0 collective-permute-start.10
  147.7 0.0 collective-permute-done.8.refs_9_
  147.7 0.5 collective-permute-start.11
  148.2 0.0 collective-permute-done.9.refs_11_
  148.2 0.0 collective-permute-start.12
  148.3 0.0 collective-permute-done.2.refs_1_
  148.3 0.5 collective-permute-start.13
  148.7 0.0 collective-permute-done.7.refs_7_
  148.7 40.9 %cross_mlp.2.refs_0_ = bf16[256,1280]{1,0:T(8,128)(2,1)} custom-call(s32[8]{0:T(128)} %fusion.2.lim_ref, bf16[256,1280]{1,0:T(8,128)(2,1)} %get-tuple-element.19.q_ref, bf16[256,1280]{1,0:T(8,128)(2,1)} %get-tuple-element.20.hid_ref, bf16[2,1280]{1,0:T(2,128)(2,1)} %gm_ref.3, bf16[2,1024,1280]{2,1,0:T(8,128)(2,1)} %get-tuple-element.21.refs_0_, ...), custom_call_target="tpu_custom_call" | custom-call | flops 14931722240 | bytes 42598400 | tf_op jit(solution)/shard_map/cross_mlp/pallas_call | solution.py:518
  189.7 32.7 %self_attention.3 = (bf16[256,1280]{1,0:T(8,128)(2,1)}, bf16[256,1280]{1,0:T(8,128)(2,1)}) custom-call(bf16[256,1280]{1,0:T(8,128)(2,1)} %cross_mlp.2.refs_0_, bf16[2,1280]{1,0:T(2,128)(2,1)} %refs_1_.7, bf16[2,1280]{1,0:T(2,128)(2,1)} %refs_2_.11, bf16[2,1280,1280]{2,1,0:T(8,128)(2,1)} %refs_3_.5, bf16[2,1280,1280]{2,1,0:T(8,128)(2,1)} %refs_4_.3, ...), custom_call_target="tpu_custom_call" | custom-call | flops 10569646080 | bytes 16384000 | tf_op jit(solution)/shard_map/self_attention/pallas_call | solution.py:373
  222.4 0.0 collective-permute-done.10.refs_3_
  222.4 0.0 collective-permute-done.11.refs_5_
  222.4 0.0 collective-permute-done.12.refs_9_
  222.4 0.0 collective-permute-done.13.refs_11_
  222.5 1.0 copy-done.5
  223.5 40.7 %cross_mlp.3 = bf16[256,1280]{1,0:T(8,128)(2,1)} custom-call(s32[8]{0:T(128)} %fusion.2.lim_ref, bf16[256,1280]{1,0:T(8,128)(2,1)} %get-tuple-element.27.q_ref, bf16[256,1280]{1,0:T(8,128)(2,1)} %get-tuple-element.28.hid_ref, bf16[2,1280]{1,0:T(2,128)(2,1)} %gm_ref.3, bf16[2,1024,1280]{2,1,0:T(8,128)(2,1)} %get-tuple-element.21.refs_0_, ...), custom_call_target="tpu_custom_call" | custom-call | flops 14931722240 | bytes 42598400 | tf_op jit(solution)/shard_map/cross_mlp/pallas_call | solution.py:518
  (14 shorter events, 0.0 us)
Async XLA Ops:
  0.0 5.5 %copy-start.7 = (s32[4,8]{1,0:T(4,128)S(1)}, s32[4,8]{1,0:T(4,128)}, u32[]{:S(2)}) copy-start(s32[4,8]{1,0:T(4,128)} %constant.15.clone) | copy-start | bytes 388
  0.0 8.8 %copy-start.2 = (bf16[1024,1280]{1,0:T(8,128)(2,1)S(1)}, bf16[1024,1280]{1,0:T(8,128)(2,1)}, u32[]{:S(2)}) copy-start(bf16[1024,1280]{1,0:T(8,128)(2,1)} %refs_0_.3) | copy-start | bytes 7864324
  3.5 5.3 %collective-permute-start.1 = (bf16[512,1280]{1,0:T(8,128)(2,1)}, bf16[512,1280]{1,0:T(8,128)(2,1)}, u32[]{:S(2)}, u32[]{:S(2)}) collective-permute-start(bf16[512,1280]{1,0:T(8,128)(2,1)} %get-tuple-element.34), channel_id=1, source_target_pairs={{2,3},{6,7}} | collective-permute-start | bytes 3932168 | tf_op jit(solution)/shard_map/ppermute | solution.py:575
  8.8 6.3 %copy-start.6 = (bf16[512,1280]{1,0:T(8,128)(2,1)S(1)}, bf16[512,1280]{1,0:T(8,128)(2,1)}, u32[]{:S(2)}) copy-start(bf16[512,1280]{1,0:T(8,128)(2,1)} %get-tuple-element.33) | copy-start | bytes 3932164
  14.6 133.7 %collective-permute-start.2 = (bf16[2,1024,1280]{2,1,0:T(8,128)(2,1)}, bf16[2,1024,1280]{2,1,0:T(8,128)(2,1)}, u32[]{:S(2)}, u32[]{:S(2)}) collective-permute-start(bf16[2,1024,1280]{2,1,0:T(8,128)(2,1)} %get-tuple-element.21.refs_0_), channel_id=1, source_target_pairs={{0,1},{1,0},{2,3},{3,2},{4,5},{5,4},{6,7},{7,6}} | collective-permute-start | bytes 15728648 | tf_op jit(solution)/shard_map/ppermute | solution.py:570
  14.6 134.1 %collective-permute-start.7 = (bf16[2,1280,1024]{2,1,0:T(8,128)(2,1)}, bf16[2,1280,1024]{2,1,0:T(8,128)(2,1)}, u32[]{:S(2)}, u32[]{:S(2)}) collective-permute-start(bf16[2,1280,1024]{2,1,0:T(8,128)(2,1)} %get-tuple-element.24.refs_6_), channel_id=1, source_target_pairs={{0,1},{1,0},{2,3},{3,2},{4,5},{5,4},{6,7},{7,6}} | collective-permute-start | bytes 15728648 | tf_op jit(solution)/shard_map/ppermute | solution.py:570
  15.1 41.9 %collective-permute-start.3 = (bf16[512,1280]{1,0:T(8,128)(2,1)S(1)}, bf16[512,1280]{1,0:T(8,128)(2,1)S(1)}, u32[]{:S(2)}, u32[]{:S(2)}) collective-permute-start(bf16[512,1280]{1,0:T(8,128)(2,1)S(1)} %copy-done.6), channel_id=1, source_target_pairs={{0,2},{1,3},{2,0},{4,6},{5,7},{6,4}} | collective-permute-start | bytes 3932168 | tf_op jit(solution)/shard_map/ppermute | solution.py:576
  16.4 68.7 %collective-permute-start.5 = (bf16[512,1280]{1,0:T(8,128)(2,1)}, bf16[512,1280]{1,0:T(8,128)(2,1)S(1)}, u32[]{:S(2)}, u32[]{:S(2)}) collective-permute-start(bf16[512,1280]{1,0:T(8,128)(2,1)} %get-tuple-element.34), channel_id=1, source_target_pairs={{0,2},{1,3},{2,1},{4,6},{5,7},{6,5}} | collective-permute-start | bytes 3932168 | tf_op jit(solution)/shard_map/ppermute | solution.py:577
  57.0 8.1 %copy-start = (bf16[512,1280]{1,0:T(8,128)(2,1)}, bf16[512,1280]{1,0:T(8,128)(2,1)S(1)}, u32[]{:S(2)}) copy-start(bf16[512,1280]{1,0:T(8,128)(2,1)S(1)} %collective-permute-done.3.refs_0_) | copy-start | bytes 3932164
  57.0 11.1 %copy-start.8 = (bf16[256,1280]{1,0:T(8,128)(2,1)S(1)}, bf16[256,1280]{1,0:T(8,128)(2,1)}, u32[]{:S(2)}) copy-start(bf16[256,1280]{1,0:T(8,128)(2,1)} %refs_0_.2) | copy-start | bytes 1966084
  65.1 27.8 %copy-start.3 = (bf16[1,512,1280]{2,1,0:T(8,128)(2,1)}, bf16[1,512,1280]{2,1,0:T(8,128)(2,1)S(1)}, u32[]{:S(2)}) copy-start(bf16[1,512,1280]{2,1,0:T(8,128)(2,1)S(1)} %get-tuple-element.22.refs_2_) | copy-start | bytes 3932164
  65.1 35.7 %collective-permute-start.4 = (bf16[1,512,1280]{2,1,0:T(8,128)(2,1)S(1)}, bf16[1,512,1280]{2,1,0:T(8,128)(2,1)S(1)}, u32[]{:S(2)}, u32[]{:S(2)}) collective-permute-start(bf16[1,512,1280]{2,1,0:T(8,128)(2,1)S(1)} %get-tuple-element.22.refs_2_), channel_id=1, source_target_pairs={{0,1},{1,0},{2,3},{3,2},{4,5},{5,4},{6,7},{7,6}} | collective-permute-start | bytes 3932168 | tf_op jit(solution)/shard_map/ppermute | solution.py:570
  68.1 31.0 %collective-permute-start = (bf16[256,1280]{1,0:T(8,128)(2,1)S(1)}, bf16[256,1280]{1,0:T(8,128)(2,1)S(1)}, u32[]{:S(2)}, u32[]{:S(2)}) collective-permute-start(bf16[256,1280]{1,0:T(8,128)(2,1)S(1)} %copy-done.8), channel_id=1, source_target_pairs={{0,2},{1,3},{4,6},{5,7}} | collective-permute-start | bytes 1966088 | tf_op jit(solution)/shard_map/ppermute | solution.py:573
  92.9 54.8 %collective-permute-start.6 = (bf16[1,512,1280]{2,1,0:T(8,128)(2,1)}, bf16[1,512,1280]{2,1,0:T(8,128)(2,1)}, u32[]{:S(2)}, u32[]{:S(2)}) collective-permute-start(bf16[1,512,1280]{2,1,0:T(8,128)(2,1)} %get-tuple-element.23.refs_4_), channel_id=1, source_target_pairs={{0,1},{1,0},{2,3},{3,2},{4,5},{5,4},{6,7},{7,6}} | collective-permute-start | bytes 3932168 | tf_op jit(solution)/shard_map/ppermute | solution.py:570
  99.1 2.8 %copy-start.9 = (bf16[256,1280]{1,0:T(8,128)(2,1)}, bf16[256,1280]{1,0:T(8,128)(2,1)S(1)}, u32[]{:S(2)}) copy-start(bf16[256,1280]{1,0:T(8,128)(2,1)S(1)} %collective-permute-done.refs_1_) | copy-start | bytes 1966084
  99.1 48.6 %collective-permute-start.8 = (bf16[1,1280,512]{2,1,0:T(8,128)(2,1)}, bf16[1,1280,512]{2,1,0:T(8,128)(2,1)}, u32[]{:S(2)}, u32[]{:S(2)}) collective-permute-start(bf16[1,1280,512]{2,1,0:T(8,128)(2,1)} %get-tuple-element.25.refs_8_), channel_id=1, source_target_pairs={{0,1},{1,0},{2,3},{3,2},{4,5},{5,4},{6,7},{7,6}} | collective-permute-start | bytes 3932168 | tf_op jit(solution)/shard_map/ppermute | solution.py:570
  100.8 1.1 copy-start.4
  101.9 46.4 %collective-permute-start.9 = (bf16[1,1280,512]{2,1,0:T(8,128)(2,1)}, bf16[1,1280,512]{2,1,0:T(8,128)(2,1)}, u32[]{:S(2)}, u32[]{:S(2)}) collective-permute-start(bf16[1,1280,512]{2,1,0:T(8,128)(2,1)} %get-tuple-element.26.refs_10_), channel_id=1, source_target_pairs={{0,1},{1,0},{2,3},{3,2},{4,5},{5,4},{6,7},{7,6}} | collective-permute-start | bytes 3932168 | tf_op jit(solution)/shard_map/ppermute | solution.py:570
  130.5 1.3 copy-start.1
  147.7 74.7 %collective-permute-start.10 = (bf16[1,512,1280]{2,1,0:T(8,128)(2,1)}, bf16[1,512,1280]{2,1,0:T(8,128)(2,1)S(1)}, u32[]{:S(2)}, u32[]{:S(2)}) collective-permute-start(bf16[1,512,1280]{2,1,0:T(8,128)(2,1)} %get-tuple-element.29.refs_2_), channel_id=1, source_target_pairs={{0,1},{1,0},{2,3},{3,2},{4,5},{5,4},{6,7},{7,6}} | collective-permute-start | bytes 3932168 | tf_op jit(solution)/shard_map/ppermute | solution.py:570
  147.7 74.7 %collective-permute-start.11 = (bf16[1,512,1280]{2,1,0:T(8,128)(2,1)}, bf16[1,512,1280]{2,1,0:T(8,128)(2,1)}, u32[]{:S(2)}, u32[]{:S(2)}) collective-permute-start(bf16[1,512,1280]{2,1,0:T(8,128)(2,1)} %get-tuple-element.30.refs_4_), channel_id=1, source_target_pairs={{0,1},{1,0},{2,3},{3,2},{4,5},{5,4},{6,7},{7,6}} | collective-permute-start | bytes 3932168 | tf_op jit(solution)/shard_map/ppermute | solution.py:570
  148.2 74.2 %collective-permute-start.12 = (bf16[1,1280,512]{2,1,0:T(8,128)(2,1)}, bf16[1,1280,512]{2,1,0:T(8,128)(2,1)}, u32[]{:S(2)}, u32[]{:S(2)}) collective-permute-start(bf16[1,1280,512]{2,1,0:T(8,128)(2,1)} %get-tuple-element.31.refs_8_), channel_id=1, source_target_pairs={{0,1},{1,0},{2,3},{3,2},{4,5},{5,4},{6,7},{7,6}} | collective-permute-start | bytes 3932168 | tf_op jit(solution)/shard_map/ppermute | solution.py:570
  148.3 74.2 %collective-permute-start.13 = (bf16[1,1280,512]{2,1,0:T(8,128)(2,1)}, bf16[1,1280,512]{2,1,0:T(8,128)(2,1)}, u32[]{:S(2)}, u32[]{:S(2)}) collective-permute-start(bf16[1,1280,512]{2,1,0:T(8,128)(2,1)} %get-tuple-element.32.refs_10_), channel_id=1, source_target_pairs={{0,1},{1,0},{2,3},{3,2},{4,5},{5,4},{6,7},{7,6}} | collective-permute-start | bytes 3932168 | tf_op jit(solution)/shard_map/ppermute | solution.py:570
  222.4 1.1 copy-start.5

commit v2 on v1

--- a/solution.py
+++ b/solution.py
@@ -218,9 +218,10 @@
     w_copies[1].start()
 
     barrier = pltpu.get_barrier_semaphore()
-    for other in (sibling, across):
+    others = (sibling,) if far_given else (sibling, across)
+    for other in others:
         pl.semaphore_signal(barrier, inc=1, device_id={"sp": other}, device_id_type=pl.DeviceIdType.MESH)
-    pl.semaphore_wait(barrier, 2)
+    pl.semaphore_wait(barrier, len(others))
 
     def send(src, dst, sem, other):
         return pltpu.make_async_remote_copy(src_ref=src, dst_ref=dst, send_sem=sem.at[0], recv_sem=sem.at[1],
@@ -253,8 +254,9 @@
     x_s[pl.ds(0, rows), :] = rms(own_ref[...], gain)
     key = lax.broadcasted_iota(jnp.int32, (rows, rows), 0)
     query = lax.broadcasted_iota(jnp.int32, (rows, rows), 1)
-    bias[pl.ds(0, rows), :] = jnp.where(key <= query, 0.0, NEG_BIG)
-    bias[pl.ds(rows, rows), :] = jnp.full((rows, rows), jnp.where(odd == 1, 0.0, NEG_BIG), F32)
+    bias[0, pl.ds(0, rows), :] = jnp.where(key <= query, 0.0, NEG_BIG)
+    bias[0, pl.ds(rows, rows), :] = jnp.full((rows, rows), jnp.where(odd == 1, 0.0, NEG_BIG), F32)
+    bias[1] = jnp.zeros((2 * rows, rows), F32)
     attend_reset(scratch)
 
     @pl.when(odd == 1)
@@ -269,59 +271,66 @@
     def tile(t):
         return pl.ds(pl.multiple_of(t * 256, 256), 256)
 
-    def project(n, first):
-        def step(r, _):
-            at = tile(first + r)
-            out = dot(x_s[at, :], w_s[n]).astype(BF16)
-            if n == 0:
-                k_s[at, :] = out
-            else:
-                vt_s[:, at] = out.T
-            return 0
-
-        lax.fori_loop(0, 2, step, 0)
-
     def head_cols(i):
         return pl.ds(pl.multiple_of(i * 128, 128), 128)
 
-    def attend(half, add):
-        at = pl.ds(half * CH, CH)
+    def phase(half, _):
+        at = pl.ds(pl.multiple_of(half * CH, CH), CH)
+
+        @pl.when(half == 0)
+        def _():
+            w_copies[0].wait()
+            w_copies[2].start()
+
+        @pl.when(half == 1)
+        def _():
+            if not far_given:
+                for i in range(parts):
+                    far[i].wait_recv()
+                    fwd[i].start()
+            x_s[pl.ds(2 * rows, rows), :] = rms(s2[...], gain)
+            for cp in fwd:
+                cp.wait_recv()
+            x_s[pl.ds(3 * rows, rows), :] = rms(s3[...], gain)
+
+        def project_k(r, _):
+            rows_at = tile(2 * half + r)
+            k_s[rows_at, :] = dot(x_s[rows_at, :], w_s[0]).astype(BF16)
+            return 0
+
+        lax.fori_loop(0, 2, project_k, 0)
+
+        @pl.when(half == 0)
+        def _():
+            w_copies[1].wait()
+            w_copies[3].start()
+
+        def project_v(r, _):
+            rows_at = tile(2 * half + r)
+            vt_s[:, rows_at] = dot(x_s[rows_at, :], w_s[1]).astype(BF16).T
+            return 0
+
+        lax.fori_loop(0, 2, project_v, 0)
+
+        @pl.when(half == 0)
+        def _():
+            w_copies[2].wait()
+            w_copies[4].start()
+
+            def project_q(t, _):
+                qs[:, tile(t)] = dot(x_s[pl.ds(0, rows), :], w_s[2, :, tile(t)]).astype(BF16) * BF16(0.125)
+                return 0
+
+            lax.fori_loop(0, tiles, project_q, 0)
 
         def scores(i, j):
             k = k_s[at, head_cols(i)]
-            return [add(dot_nt(k, q)) for q in pair_queries(qs[:, head_cols(i)])]
+            return [dot_nt(k, q) + bias[half] for q in pair_queries(qs[:, head_cols(i)])]
 
         attend_all(width // 128, 1, scores, lambda i, j: vt_s[head_cols(i), at], lambda i: None, lambda i: None, scratch)
-
-    w_copies[0].wait()
-    w_copies[2].start()
-    project(0, 0)
-    w_copies[1].wait()
-    w_copies[3].start()
-    project(1, 0)
-    w_copies[2].wait()
-    w_copies[4].start()
-
-    def project_q(t, _):
-        qs[:, tile(t)] = dot(x_s[pl.ds(0, rows), :], w_s[2, :, tile(t)]).astype(BF16) * BF16(0.125)
         return 0
 
-    lax.fori_loop(0, tiles, project_q, 0)
-    attend(0, lambda s: s + bias[...])
-
-    @pl.when(chip1)
-    def _():
-        if not far_given:
-            for i in range(parts):
-                far[i].wait_recv()
-                fwd[i].start()
-        x_s[pl.ds(2 * rows, rows), :] = rms(s2[...], gain)
-        for cp in fwd:
-            cp.wait_recv()
-        x_s[pl.ds(3 * rows, rows), :] = rms(s3[...], gain)
-        project(0, 2)
-        project(1, 2)
-        attend(1, lambda s: s)
+    lax.fori_loop(0, jnp.where(chip1, 2, 1), phase, 0)
 
     def finish(i, _):
         attend_finish(i, at_s, scratch)
@@ -381,7 +390,7 @@
             pltpu.VMEM((4 * rows, width), BF16),
             pltpu.VMEM((width, 4 * rows), BF16),
             block,
-            pltpu.VMEM((2 * rows, rows), F32),
+            pltpu.VMEM((2, 2 * rows, rows), F32),
             pltpu.VMEM((width, rows), BF16),
             block,
             block,
@@ -399,15 +408,25 @@
     )(own, *([far] if far_given else []), gs, gc, wq, wk, wv, wo, wcq)
 
 
-def cross_kernel(layer, planes, n_kv, lim_ref, q_ref, hid_ref, gm_ref, *refs):
-    ks, vts = refs[:n_kv], refs[n_kv:2 * n_kv]
-    (wco, wg, wu, wd, out_ref, kbuf, vbuf, at_s, a_s, x_s, acc_o, mask, list_s, wo_s, wg_s, wu_s, wd_s,
-     kv_sems, o_sem, w_sems) = refs[2 * n_kv:-7]
-    scratch = refs[-7:]
+def cross_kernel(layer, planes, n_kv, state_in, mlp, lim_ref, q_ref, *refs):
+    def take(n):
+        nonlocal refs
+        head, refs = refs[:n], refs[n:]
+        return head
+
+    ks, vts = take(n_kv), take(n_kv)
+    state = take(3) if state_in else None
+    if mlp:
+        hid_ref, gm_ref, wco, wg, wu, wd, out_ref = take(7)
+    else:
+        outs = take(3)
+    scratch = take(7)
+    kbuf, vbuf, mask, list_s, kv_sems = take(5)
+    if mlp:
+        at_s, a_s, x_s, acc_o, wo_s, wg_s, wu_s, wd_s, o_sem, w_sems = take(10)
+        steps, ff = wg_s.shape[0], wg_s.shape[2]
     rows, width = q_ref.shape
     pairs = width // 128
-    steps = wg_s.shape[0]
-    ff = wg_s.shape[2]
 
     def kv_copies(i, slot):
         cols = pl.ds(pl.multiple_of(i * 128, 128), 128)
@@ -419,17 +438,31 @@
             at += n_rows
         return out
 
-    def w_copies(j):
-        cols = pl.ds(pl.multiple_of(j * ff, ff), ff)
-        return (pltpu.make_async_copy(wg.at[layer, :, cols], wg_s.at[j], w_sems.at[0, j]),
-                pltpu.make_async_copy(wu.at[layer, :, cols], wu_s.at[j], w_sems.at[1, j]),
-                pltpu.make_async_copy(wd.at[layer, cols, :], wd_s.at[j], w_sems.at[2, j]))
-
     for cp in kv_copies(0, 0):
         cp.start()
-    o_copy = pltpu.make_async_copy(wco.at[layer], wo_s, o_sem)
+    if mlp:
+        o_copy = pltpu.make_async_copy(wco.at[layer], wo_s, o_sem)
+
+        def w_copies(j):
+            cols = pl.ds(pl.multiple_of(j * ff, ff), ff)
+            return (pltpu.make_async_copy(wg.at[layer, :, cols], wg_s.at[j], w_sems.at[0, j]),
+                    pltpu.make_async_copy(wu.at[layer, :, cols], wu_s.at[j], w_sems.at[1, j]),
+                    pltpu.make_async_copy(wd.at[layer, cols, :], wd_s.at[j], w_sems.at[2, j]))
+
+        def start_weights(j):
+            for cp in w_copies(j):
+                cp.start()
+
+        o_copy.start()
+
+    if state_in:
+        for src, dst in zip(state, scratch[4:]):
+            dst[...] = src[...]
+    else:
+        attend_reset(scratch)
 
     n_chunks, last = jnp.int32(0), jnp.int32(0)
+    list_s[0] = 0
     for c in range(lim_ref.shape[0]):
         lim = lim_ref[c]
 
@@ -451,14 +484,10 @@
             for cp in kv_copies(i + 1, lax.rem(i + 1, 3)):
                 cp.start()
 
-        @pl.when(i == 0)
-        def _():
-            o_copy.start()
-
-        @pl.when(i < steps)
-        def _():
-            for cp in w_copies(i):
-                cp.start()
+        if mlp:
+            @pl.when(i < steps)
+            def _():
+                start_weights(i)
 
         for cp in kv_copies(i, lax.rem(i, 3)):
             cp.wait()
@@ -476,9 +505,28 @@
     def values(i, j):
         return vbuf[lax.rem(i, 3), :, chunk(j)]
 
-    attend_reset(scratch)
-    attend_all(pairs, n_chunks, scores, values, enter, lambda i: attend_finish(i, at_s, scratch), scratch)
-
+    @pl.when(n_chunks > 0)
+    def _():
+        attend_all(pairs, n_chunks, scores, values, enter, lambda i: None, scratch)
+
+    @pl.when(n_chunks == 0)
+    def _():
+        for cp in kv_copies(0, 0):
+            cp.wait()
+        if mlp:
+            for j in range(steps):
+                start_weights(j)
+
+    if not mlp:
+        for src, dst in zip(scratch[4:], outs):
+            dst[...] = src[...]
+        return
+
+    def finish(i, _):
+        attend_finish(i, at_s, scratch)
+        return 0
+
+    lax.fori_loop(0, pairs, finish, 0)
     a_s[...] = at_s[...].T
     o_copy.wait()
 
@@ -505,43 +553,60 @@
     out_ref[...] = (out_ref[...].astype(F32) + acc_o[...]).astype(BF16)
 
 
-def cross_mlp(layer, lims, q, hid, gm, kvs, wco, wg, wu, wd):
+def cross(layer, lims, q, kvs, state=None, after=None):
     rows, width = q.shape
     pairs = width // 128
-    steps = 10
-    ff = wg.shape[2] // steps
     planes = tuple(plane for _, _, plane in kvs)
     ks, vts = [k for k, _, _ in kvs], [v for _, v, _ in kvs]
     total = sum(k.shape[1] for k in ks)
     n = len(kvs)
-    flops = 2 * rows * width * (width + 3 * wg.shape[2]) + 4 * rows * 3072 * width
-    return pl.pallas_call(
-        functools.partial(cross_kernel, layer, planes, n),
-        in_specs=[SMEM, VMEM, VMEM, VMEM] + [ANY] * (2 * n + 4),
-        out_specs=VMEM,
-        out_shape=jax.ShapeDtypeStruct((rows, width), BF16),
-        scratch_shapes=[
-            pltpu.VMEM((3, total, 128), BF16),
-            pltpu.VMEM((3, 128, total), BF16),
+    operands, specs = [lims, q, *ks, *vts], [SMEM, VMEM] + [ANY] * (2 * n)
+    if state is not None:
+        operands, specs = operands + list(state), specs + [VMEM] * 3
+    scratch = attend_scratch(pairs, rows) + [
+        pltpu.VMEM((3, total, 128), BF16),
+        pltpu.VMEM((3, 128, total), BF16),
+        pltpu.VMEM((2, CH, 128), BF16),
+        pltpu.SMEM((8,), jnp.int32),
+        pltpu.SemaphoreType.DMA((3, 2, n)),
+    ]
+    flops = 4 * rows * min(total, 3072) * width
+    if after is None:
+        out_shape = [jax.ShapeDtypeStruct((pairs, 2, rows), F32)] * 2 + [jax.ShapeDtypeStruct((pairs, 2, 64, rows), F32)]
+        out_specs = [VMEM] * 3
+        moved = 8 * total * width
+        limit = 32 * 1024 * 1024
+    else:
+        _, _, _, wg, _, _ = after
+        operands, specs = operands + list(after), specs + [VMEM] * 2 + [ANY] * 4
+        out_shape, out_specs = jax.ShapeDtypeStruct((rows, width), BF16), VMEM
+        steps = 10
+        ff = wg.shape[2] // steps
+        scratch += [
             pltpu.VMEM((width, rows), BF16),
             pltpu.VMEM((rows, width), BF16),
             pltpu.VMEM((rows, width), BF16),
             pltpu.VMEM((rows, width), F32),
-            pltpu.VMEM((2, CH, 128), BF16),
-            pltpu.SMEM((8,), jnp.int32),
             pltpu.VMEM((width, width), BF16),
             pltpu.VMEM((steps, width, ff), BF16),
             pltpu.VMEM((steps, width, ff), BF16),
             pltpu.VMEM((steps, ff, width), BF16),
-            pltpu.SemaphoreType.DMA((3, 2, n)),
             pltpu.SemaphoreType.DMA,
             pltpu.SemaphoreType.DMA((3, steps)),
-            *attend_scratch(pairs, rows),
-        ],
-        cost_estimate=pl.CostEstimate(flops=flops, bytes_accessed=2 * width * (width + 3 * wg.shape[2]), transcendentals=0),
-        compiler_params=pltpu.CompilerParams(vmem_limit_bytes=VMEM_LIMIT),
-        name="cross_mlp",
-    )(lims, q, hid, gm, *ks, *vts, wco, wg, wu, wd)
+        ]
+        flops += 2 * rows * width * (width + 3 * wg.shape[2])
+        moved = 2 * width * (width + 3 * wg.shape[2])
+        limit = VMEM_LIMIT
+    return pl.pallas_call(
+        functools.partial(cross_kernel, layer, planes, n, state is not None, after is not None),
+        in_specs=specs,
+        out_specs=out_specs,
+        out_shape=out_shape,
+        scratch_shapes=scratch,
+        cost_estimate=pl.CostEstimate(flops=flops, bytes_accessed=moved, transcendentals=0),
+        compiler_params=pltpu.CompilerParams(vmem_limit_bytes=limit),
+        name="cross_attention" if after is None else "cross_mlp",
+    )(*operands)
 
 
 NONE = 1 << 20
@@ -589,7 +654,12 @@
 
             for layer in range(layers):
                 hidden, q = self_attention(layer, hidden, far, norm_self, norm_cross, self_q, self_k, self_v, w_so, cross_q)
-                hidden = cross_mlp(layer, lims, q, hidden, norm_mlp, kvs[layer], w_co, mlp_gate, mlp_up, mlp_down)
+                after = (hidden, norm_mlp, w_co, mlp_gate, mlp_up, mlp_down)
+                if layer == 0:
+                    state = cross(layer, lims[:6], q, kvs[layer][:4])
+                    hidden = cross(layer, lims[6:], q, kvs[layer][4:], state, after)
+                else:
+                    hidden = cross(layer, lims, q, kvs[layer], None, after)
                 far = None
             return hidden
 

time: 265 us -> 282 us (1.064)
  Pallas kernels: 180 us -> 189 us
  local copies, waits for them, and re-layouts: 7.63 us -> 16.4 us
    unnamed x20 -> x48, local copies, waits for them, and re-layouts: 3.43 us -> 11.6 us
    pallas_call x2 -> x3, Pallas kernels: 81.6 us -> 87.9 us  [cross(): pl.pallas_call(functools.partial(cross_kernel, layer, planes, n, state is...]
  transfers between devices with their start and end apart: 14 -> 14, of which waited for: 4 -> 4; matrix products, arithmetic and copies ran while one was open for 0% -> 1% of each run, Pallas kernels for 51% -> 50%
where the time goes in v2:
time: 282 us; the launch traced here: 281 us
  Pallas kernels  189 us (67%)
  waiting for transfers between devices  60.3 us (21%)
  local copies, waits for them, and re-layouts  16.4 us (6%)
  starting transfers between devices  14.3 us (5%)
    pallas_call x3, Pallas kernels, cross(): pl.pallas_call(functools.partial(cross_kernel, layer, planes, n, state is...  87.9 us
    pallas_call x2, Pallas kernels, self_attention(): pl.pallas_call(functools.partial(self_kernel, layer, far_given), in_specs...  63.3 us
    ppermute x1, waiting for transfers between devices, program(): rem_a = lax.ppermute(mem_a, 'sp', [(0, 2), (1, 3), (2, 0)])  39.2 us
    pallas_call x5, Pallas kernels, kv_project(): pl.pallas_call(functools.partial(kv_kernel, layers, len(srcs)), in_specs=...  37.3 us
    ppermute x1, waiting for transfers between devices, program(): rem_b = lax.ppermute(mem_b, 'sp', [(0, 2), (1, 3), (2, 1)])  15.1 us
    unnamed x48, local copies, waits for them, and re-layouts  11.6 us
    ppermute x10, starting transfers between devices, swap(): return lax.ppermute(x, 'sp', [(0, 1), (1, 0), (2, 3), (3, 2)])  9.19 us
  transfers between devices with their start and end apart: 14, of which 4 were waited for; matrix products, arithmetic and copies ran while one was open for 1% of the time, Pallas kernels for 50%

profile of v2, /device:TPU:7, one launch (start us, length us, event | category | flops | bytes accessed | tf_op | source)
XLA Modules:
  0.0 281.2 jit_solution(6158293132340839583)
XLA Ops:
  0.0 3.5 %fusion = (bf16[512,1280]{1,0:T(8,128)(2,1)}, bf16[512,1280]{1,0:T(8,128)(2,1)}) fusion(bf16[1024,1280]{1,0:T(8,128)(2,1)} %refs_0_.3), kind=kLoop, calls=%fused_computation.4 | loop fusion | bytes 5242880 | tf_op jit(solution)/shard_map/slice | solution.py:639
  3.5 1.3 collective-permute-start.4
  5.5 0.6 slice_bitcast_fusion
  6.2 2.6 collective-permute-done.4.refs_1_
  8.8 5.8 %kv_project.6 = (bf16[2,1024,1280]{2,1,0:T(8,128)(2,1)}, bf16[2,1280,1024]{2,1,0:T(8,128)(2,1)}) custom-call(s32[2]{0:T(128)S(1)} %get-tuple-element.43.lim_ref, s32[1]{0:T(128)} %bitcast.5.pick_ref, bf16[1024,1280]{1,0:T(8,128)(2,1)S(1)} %copy-done.5, bf16[512,1280]{1,0:T(8,128)(2,1)} %collective-permute-done.4.refs_1_, bf16[2,1280,1280]{2,1,0:T(8,128)(2,1)} %refs_1_.9, ...), custom_call_target="tpu_custom_call" | custom-call | flops 13421772800 | bytes 13107200 | tf_op jit(solution)/shard_map/kv_project/pallas_call | solution.py:98
  14.6 0.0 collective-permute-start.5
  14.6 0.5 collective-permute-start.8
  15.1 1.3 collective-permute-start.6
  16.4 1.3 collective-permute-start.1
  17.7 0.6 fusion.1
  18.4 39.2 %collective-permute-done.6.refs_0_ = bf16[512,1280]{1,0:T(8,128)(2,1)S(1)} collective-permute-done((bf16[512,1280]{1,0:T(8,128)(2,1)S(1)}, bf16[512,1280]{1,0:T(8,128)(2,1)S(1)}, u32[]{:S(2)}, u32[]{:S(2)}) %collective-permute-start.6) | collective-permute-done | bytes 1310752 | tf_op jit(solution)/shard_map/ppermute | solution.py:641
  57.6 8.1 %kv_project.7 = (bf16[1,512,1280]{2,1,0:T(8,128)(2,1)S(1)}, bf16[1,1280,512]{2,1,0:T(8,128)(2,1)}) custom-call(s32[1]{0:T(128)} %bitcast.8.lim_ref, s32[1]{0:T(128)} %bitcast.5.pick_ref, bf16[512,1280]{1,0:T(8,128)(2,1)S(1)} %collective-permute-done.6.refs_0_, bf16[2,1280,1280]{2,1,0:T(8,128)(2,1)} %refs_1_.9, bf16[2,1280,1280]{2,1,0:T(8,128)(2,1)} %refs_2_.13), custom_call_target="tpu_custom_call" | custom-call | flops 3355443200 | bytes 6553600 | tf_op jit(solution)/shard_map/kv_project/pallas_call | solution.py:98
  65.7 3.0 %collective-permute-start.7 = (bf16[1,512,1280]{2,1,0:T(8,128)(2,1)S(1)}, bf16[1,512,1280]{2,1,0:T(8,128)(2,1)S(1)}, u32[]{:S(2)}, u32[]{:S(2)}) collective-permute-start(bf16[1,512,1280]{2,1,0:T(8,128)(2,1)S(1)} %get-tuple-element.26.refs_2_), channel_id=1, source_target_pairs={{0,1},{1,0},{2,3},{3,2},{4,5},{5,4},{6,7},{7,6}} | collective-permute-start | bytes 3932168 | tf_op jit(solution)/shard_map/ppermute | solution.py:635
  68.7 1.3 collective-permute-start
  70.0 0.5 fusion.2.lim_ref
  70.5 15.1 %collective-permute-done.1.refs_0_ = bf16[512,1280]{1,0:T(8,128)(2,1)S(1)} collective-permute-done((bf16[512,1280]{1,0:T(8,128)(2,1)}, bf16[512,1280]{1,0:T(8,128)(2,1)S(1)}, u32[]{:S(2)}, u32[]{:S(2)}) %collective-permute-start.1) | collective-permute-done | bytes 1310752 | tf_op jit(solution)/shard_map/ppermute | solution.py:642
  85.7 3.0 %collective-permute-start.9 = (bf16[1,1280,512]{2,1,0:T(8,128)(2,1)}, bf16[1,1280,512]{2,1,0:T(8,128)(2,1)}, u32[]{:S(2)}, u32[]{:S(2)}) collective-permute-start(bf16[1,1280,512]{2,1,0:T(8,128)(2,1)} %get-tuple-element.28.refs_6_), channel_id=1, source_target_pairs={{0,1},{1,0},{2,3},{3,2},{4,5},{5,4},{6,7},{7,6}} | collective-permute-start | bytes 3932168 | tf_op jit(solution)/shard_map/ppermute | solution.py:635
  88.6 7.8 %kv_project.5 = (bf16[1,512,1280]{2,1,0:T(8,128)(2,1)}, bf16[1,1280,512]{2,1,0:T(8,128)(2,1)}) custom-call(s32[1]{0:T(128)} %bitcast.4.lim_ref, s32[1]{0:T(128)} %bitcast.5.pick_ref, bf16[512,1280]{1,0:T(8,128)(2,1)S(1)} %collective-permute-done.1.refs_0_, bf16[2,1280,1280]{2,1,0:T(8,128)(2,1)} %refs_1_.9, bf16[2,1280,1280]{2,1,0:T(8,128)(2,1)} %refs_2_.13), custom_call_target="tpu_custom_call" | custom-call | flops 3355443200 | bytes 6553600 | tf_op jit(solution)/shard_map/kv_project/pallas_call | solution.py:98
  96.5 3.2 %collective-permute-done.refs_1_ = bf16[256,1280]{1,0:T(8,128)(2,1)S(1)} collective-permute-done((bf16[256,1280]{1,0:T(8,128)(2,1)S(1)}, bf16[256,1280]{1,0:T(8,128)(2,1)S(1)}, u32[]{:S(2)}, u32[]{:S(2)}) %collective-permute-start) | collective-permute-done | bytes 655392 | tf_op jit(solution)/shard_map/ppermute | solution.py:638
  99.7 1.7 collective-permute-start.2
  101.4 1.1 copy-done.10
  102.5 0.0 collective-permute-start.3
  102.5 29.8 %self_attention.2 = (bf16[256,1280]{1,0:T(8,128)(2,1)}, bf16[256,1280]{1,0:T(8,128)(2,1)}) custom-call(bf16[256,1280]{1,0:T(8,128)(2,1)} %refs_0_.2, bf16[256,1280]{1,0:T(8,128)(2,1)} %copy-done.19, bf16[2,1280]{1,0:T(2,128)(2,1)} %refs_1_.7, bf16[2,1280]{1,0:T(2,128)(2,1)} %refs_2_.11, bf16[2,1280,1280]{2,1,0:T(8,128)(2,1)} %refs_3_.5, ...), custom_call_target="tpu_custom_call" | custom-call | flops 10569646080 | bytes 16384000 | tf_op jit(solution)/shard_map/self_attention/pallas_call | solution.py:382
  132.3 1.3 copy-done.3
  133.6 7.5 %kv_project.9 = (bf16[1,512,1280]{2,1,0:T(8,128)(2,1)S(1)}, bf16[1,1280,512]{2,1,0:T(8,128)(2,1)S(1)}) custom-call(s32[1]{0:T(128)} %bitcast.4.lim_ref, s32[1]{0:T(128)} %bitcast.5.pick_ref, bf16[512,1280]{1,0:T(8,128)(2,1)S(1)} %copy-done.3, bf16[2,1280,1280]{2,1,0:T(8,128)(2,1)} %refs_1_.9, bf16[2,1280,1280]{2,1,0:T(8,128)(2,1)} %refs_2_.13), custom_call_target="tpu_custom_call" | custom-call | flops 3355443200 | bytes 6553600 | tf_op jit(solution)/shard_map/kv_project/pallas_call | solution.py:98
  141.1 1.1 copy-done.6
  142.2 1.1 copy-done.7
  143.3 8.1 %kv_project.8 = (bf16[1,512,1280]{2,1,0:T(8,128)(2,1)}, bf16[1,1280,512]{2,1,0:T(8,128)(2,1)}) custom-call(s32[1]{0:T(128)} %bitcast.8.lim_ref, s32[1]{0:T(128)} %bitcast.5.pick_ref, bf16[512,1280]{1,0:T(8,128)(2,1)S(1)} %copy-done.1, bf16[2,1280,1280]{2,1,0:T(8,128)(2,1)} %refs_1_.9, bf16[2,1280,1280]{2,1,0:T(8,128)(2,1)} %refs_2_.13), custom_call_target="tpu_custom_call" | custom-call | flops 3355443200 | bytes 6553600 | tf_op jit(solution)/shard_map/kv_project/pallas_call | solution.py:98
  151.4 0.0 collective-permute-start.11
  151.4 0.0 collective-permute-done.5.refs_1_
  151.5 0.5 collective-permute-start.13
  151.9 0.0 collective-permute-done.8.refs_5_.refs_7_
  151.9 0.0 collective-permute-start.10
  152.0 1.1 copy-done.4
  153.1 1.3 copy-done.9
  154.4 1.3 copy-done.11
  155.7 12.3 %cross_attention.1 = (f32[10,2,256]{2,1,0:T(2,128)S(1)}, f32[10,2,256]{2,1,0:T(2,128)S(1)}, f32[10,2,64,256]{3,2,1,0:T(8,128)S(1)}) custom-call(s32[6]{0:T(128)S(1)} %slice_bitcast_fusion.1.lim_ref, bf16[256,1280]{1,0:T(8,128)(2,1)S(1)} %copy-done.4, bf16[2,1024,1280]{2,1,0:T(8,128)(2,1)S(1)} %bitcast.17, ...), custom_call_target="tpu_custom_call" | custom-call | flops 4026531840 | bytes 31457280 | tf_op jit(solution)/shard_map/cross_attention/pallas_call | solution.py:600
  168.1 1.0 copy-done.12
  169.1 0.6 copy-done.13
  169.7 0.6 copy-done.14
  170.3 0.5 collective-permute-start.12
  170.8 0.0 collective-permute-done.3.refs_3_
  170.8 34.4 %cross_mlp.2.refs_0_ = bf16[256,1280]{1,0:T(8,128)(2,1)} custom-call(s32[2]{0:T(128)} %get-tuple-element.44.lim_ref, bf16[256,1280]{1,0:T(8,128)(2,1)} %get-tuple-element.22.q_ref, bf16[1,512,1280]{2,1,0:T(8,128)(2,1)} %get-tuple-element.23.refs_0_, bf16[1,512,1280]{2,1,0:T(8,128)(2,1)} %collective-permute-done.2.refs_1_, ...), custom_call_target="tpu_custom_call" | custom-call | flops 12247367680 | bytes 42598400 | tf_op jit(solution)/shard_map/cross_mlp/pallas_call | solution.py:600
  205.2 33.5 %self_attention.3 = (bf16[256,1280]{1,0:T(8,128)(2,1)}, bf16[256,1280]{1,0:T(8,128)(2,1)}) custom-call(bf16[256,1280]{1,0:T(8,128)(2,1)} %cross_mlp.2.refs_0_, bf16[2,1280]{1,0:T(2,128)(2,1)} %refs_1_.7, bf16[2,1280]{1,0:T(2,128)(2,1)} %refs_2_.11, bf16[2,1280,1280]{2,1,0:T(8,128)(2,1)} %refs_3_.5, bf16[2,1280,1280]{2,1,0:T(8,128)(2,1)} %refs_4_.3, ...), custom_call_target="tpu_custom_call" | custom-call | flops 10569646080 | bytes 16384000 | tf_op jit(solution)/shard_map/self_attention/pallas_call | solution.py:382
  238.7 0.0 collective-permute-done.11.refs_5_
  238.7 0.0 collective-permute-done.10.refs_3_
  238.8 1.1 copy-done.15
  239.8 41.2 %cross_mlp.3 = bf16[256,1280]{1,0:T(8,128)(2,1)} custom-call(s32[8]{0:T(128)} %fusion.2.lim_ref, bf16[256,1280]{1,0:T(8,128)(2,1)} %get-tuple-element.33.q_ref, bf16[2,1024,1280]{2,1,0:T(8,128)(2,1)} %get-tuple-element.25.refs_0_, bf16[2,1024,1280]{2,1,0:T(8,128)(2,1)} %collective-permute-done.5.refs_1_, bf16[1,512,1280]{2,1,0:T(8,128)(2,1)} %get-tuple-element.34.refs_2_, ...), custom_call_target="tpu_custom_call" | custom-call | flops 14931722240 | bytes 42598400 | tf_op jit(solution)/shard_map/cross_mlp/pallas_call | solution.py:600
  (46 shorter events, 0.1 us)
Async XLA Ops:
  0.0 5.5 %copy-start.17 = (s32[4,8]{1,0:T(4,128)S(1)}, s32[4,8]{1,0:T(4,128)}, u32[]{:S(2)}) copy-start(s32[4,8]{1,0:T(4,128)} %constant.15.clone) | copy-start | bytes 388
  0.0 8.8 %copy-start.5 = (bf16[1024,1280]{1,0:T(8,128)(2,1)S(1)}, bf16[1024,1280]{1,0:T(8,128)(2,1)}, u32[]{:S(2)}) copy-start(bf16[1024,1280]{1,0:T(8,128)(2,1)} %refs_0_.3) | copy-start | bytes 7864324
  3.5 5.3 %collective-permute-start.4 = (bf16[512,1280]{1,0:T(8,128)(2,1)}, bf16[512,1280]{1,0:T(8,128)(2,1)}, u32[]{:S(2)}, u32[]{:S(2)}) collective-permute-start(bf16[512,1280]{1,0:T(8,128)(2,1)} %get-tuple-element.40), channel_id=1, source_target_pairs={{2,3},{6,7}} | collective-permute-start | bytes 3932168 | tf_op jit(solution)/shard_map/ppermute | solution.py:640
  8.8 6.3 %copy-start.16 = (bf16[512,1280]{1,0:T(8,128)(2,1)S(1)}, bf16[512,1280]{1,0:T(8,128)(2,1)}, u32[]{:S(2)}) copy-start(bf16[512,1280]{1,0:T(8,128)(2,1)} %get-tuple-element.39) | copy-start | bytes 3932164
  14.6 136.9 %collective-permute-start.5 = (bf16[2,1024,1280]{2,1,0:T(8,128)(2,1)}, bf16[2,1024,1280]{2,1,0:T(8,128)(2,1)}, u32[]{:S(2)}, u32[]{:S(2)}) collective-permute-start(bf16[2,1024,1280]{2,1,0:T(8,128)(2,1)} %get-tuple-element.25.refs_0_), channel_id=1, source_target_pairs={{0,1},{1,0},{2,3},{3,2},{4,5},{5,4},{6,7},{7,6}} | collective-permute-start | bytes 15728648 | tf_op jit(solution)/shard_map/ppermute | solution.py:635
  14.6 137.3 %collective-permute-start.8 = (bf16[2,1280,1024]{2,1,0:T(8,128)(2,1)}, bf16[2,1280,1024]{2,1,0:T(8,128)(2,1)}, u32[]{:S(2)}, u32[]{:S(2)}) collective-permute-start(bf16[2,1280,1024]{2,1,0:T(8,128)(2,1)} %get-tuple-element.27.refs_4_.refs_6_), channel_id=1, source_target_pairs={{0,1},{1,0},{2,3},{3,2},{4,5},{5,4},{6,7},{7,6}} | collective-permute-start | bytes 15728648 | tf_op jit(solution)/shard_map/ppermute | solution.py:635
  15.1 42.5 %collective-permute-start.6 = (bf16[512,1280]{1,0:T(8,128)(2,1)S(1)}, bf16[512,1280]{1,0:T(8,128)(2,1)S(1)}, u32[]{:S(2)}, u32[]{:S(2)}) collective-permute-start(bf16[512,1280]{1,0:T(8,128)(2,1)S(1)} %copy-done.16), channel_id=1, source_target_pairs={{0,2},{1,3},{2,0},{4,6},{5,7},{6,4}} | collective-permute-start | bytes 3932168 | tf_op jit(solution)/shard_map/ppermute | solution.py:641
  16.4 69.3 %collective-permute-start.1 = (bf16[512,1280]{1,0:T(8,128)(2,1)}, bf16[512,1280]{1,0:T(8,128)(2,1)S(1)}, u32[]{:S(2)}, u32[]{:S(2)}) collective-permute-start(bf16[512,1280]{1,0:T(8,128)(2,1)} %get-tuple-element.40), channel_id=1, source_target_pairs={{0,2},{1,3},{2,1},{4,6},{5,7},{6,5}} | collective-permute-start | bytes 3932168 | tf_op jit(solution)/shard_map/ppermute | solution.py:642
  57.6 8.1 %copy-start = (bf16[512,1280]{1,0:T(8,128)(2,1)}, bf16[512,1280]{1,0:T(8,128)(2,1)S(1)}, u32[]{:S(2)}) copy-start(bf16[512,1280]{1,0:T(8,128)(2,1)S(1)} %collective-permute-done.6.refs_0_) | copy-start | bytes 3932164
  57.6 11.1 %copy-start.18 = (bf16[256,1280]{1,0:T(8,128)(2,1)S(1)}, bf16[256,1280]{1,0:T(8,128)(2,1)}, u32[]{:S(2)}) copy-start(bf16[256,1280]{1,0:T(8,128)(2,1)} %refs_0_.2) | copy-start | bytes 1966084
  65.7 30.8 %copy-start.8 = (bf16[1,512,1280]{2,1,0:T(8,128)(2,1)}, bf16[1,512,1280]{2,1,0:T(8,128)(2,1)S(1)}, u32[]{:S(2)}) copy-start(bf16[1,512,1280]{2,1,0:T(8,128)(2,1)S(1)} %get-tuple-element.26.refs_2_) | copy-start | bytes 3932164
  65.7 35.7 %collective-permute-start.7 = (bf16[1,512,1280]{2,1,0:T(8,128)(2,1)S(1)}, bf16[1,512,1280]{2,1,0:T(8,128)(2,1)S(1)}, u32[]{:S(2)}, u32[]{:S(2)}) collective-permute-start(bf16[1,512,1280]{2,1,0:T(8,128)(2,1)S(1)} %get-tuple-element.26.refs_2_), channel_id=1, source_target_pairs={{0,1},{1,0},{2,3},{3,2},{4,5},{5,4},{6,7},{7,6}} | collective-permute-start | bytes 3932168 | tf_op jit(solution)/shard_map/ppermute | solution.py:635
  68.7 31.0 %collective-permute-start = (bf16[256,1280]{1,0:T(8,128)(2,1)S(1)}, bf16[256,1280]{1,0:T(8,128)(2,1)S(1)}, u32[]{:S(2)}, u32[]{:S(2)}) collective-permute-start(bf16[256,1280]{1,0:T(8,128)(2,1)S(1)} %copy-done.18), channel_id=1, source_target_pairs={{0,2},{1,3},{4,6},{5,7}} | collective-permute-start | bytes 1966088 | tf_op jit(solution)/shard_map/ppermute | solution.py:638
  85.7 10.8 %copy-start.2 = (bf16[512,1280]{1,0:T(8,128)(2,1)}, bf16[512,1280]{1,0:T(8,128)(2,1)S(1)}, u32[]{:S(2)}) copy-start(bf16[512,1280]{1,0:T(8,128)(2,1)S(1)} %collective-permute-done.1.refs_0_) | copy-start | bytes 3932164
  85.7 65.7 %collective-permute-start.9 = (bf16[1,1280,512]{2,1,0:T(8,128)(2,1)}, bf16[1,1280,512]{2,1,0:T(8,128)(2,1)}, u32[]{:S(2)}, u32[]{:S(2)}) collective-permute-start(bf16[1,1280,512]{2,1,0:T(8,128)(2,1)} %get-tuple-element.28.refs_6_), channel_id=1, source_target_pairs={{0,1},{1,0},{2,3},{3,2},{4,5},{5,4},{6,7},{7,6}} | collective-permute-start | bytes 3932168 | tf_op jit(solution)/shard_map/ppermute | solution.py:635
  99.7 2.8 copy-start.19
  99.7 70.6 %collective-permute-start.2 = (bf16[1,512,1280]{2,1,0:T(8,128)(2,1)}, bf16[1,512,1280]{2,1,0:T(8,128)(2,1)}, u32[]{:S(2)}, u32[]{:S(2)}) collective-permute-start(bf16[1,512,1280]{2,1,0:T(8,128)(2,1)} %get-tuple-element.23.refs_0_), channel_id=1, source_target_pairs={{0,1},{1,0},{2,3},{3,2},{4,5},{5,4},{6,7},{7,6}} | collective-permute-start | bytes 3932168 | tf_op jit(solution)/shard_map/ppermute | solution.py:635
  101.4 1.1 copy-start.10
  102.5 68.4 %collective-permute-start.3 = (bf16[1,1280,512]{2,1,0:T(8,128)(2,1)}, bf16[1,1280,512]{2,1,0:T(8,128)(2,1)}, u32[]{:S(2)}, u32[]{:S(2)}) collective-permute-start(bf16[1,1280,512]{2,1,0:T(8,128)(2,1)} %get-tuple-element.24.refs_2_), channel_id=1, source_target_pairs={{0,1},{1,0},{2,3},{3,2},{4,5},{5,4},{6,7},{7,6}} | collective-permute-start | bytes 3932168 | tf_op jit(solution)/shard_map/ppermute | solution.py:635
  132.3 1.3 copy-start.3
  133.6 9.6 %copy-start.1 = (bf16[512,1280]{1,0:T(8,128)(2,1)S(1)}, bf16[512,1280]{1,0:T(8,128)(2,1)}, u32[]{:S(2)}) copy-start(bf16[512,1280]{1,0:T(8,128)(2,1)} %copy-done) | copy-start | bytes 3932164
  133.6 18.3 %slice-start = ((s8[5242880]{0:T(1024)(128)(4,1)}), s8[4194304]{0:T(1024)(128)(4,1)S(1)}, s32[]{:S(2)}) async-start(s8[5242880]{0:T(1024)(128)(4,1)} %bitcast.16), calls=%async_computation | async-start | bytes 8388608
  133.6 18.3 %slice-start.2 = ((s8[5242880]{0:T(1024)(128)(4,1)}), s8[4194304]{0:T(1024)(128)(4,1)S(1)}, s32[]{:S(2)}) async-start(s8[5242880]{0:T(1024)(128)(4,1)} %bitcast.18), calls=%async_computation.2 | async-start | bytes 8388608
  141.1 1.1 copy-start.6
  142.2 1.1 copy-start.7
  143.3 8.7 %slice-start.1 = ((s8[5242880]{0:T(1024)(128)(4,1)}), s8[1048576]{0:T(1024)(128)(4,1)S(1)}, s32[]{:S(2)}) async-start(s8[5242880]{0:T(1024)(128)(4,1)} %bitcast.16), calls=%async_computation.1 | async-start | bytes 2097152
  143.3 8.7 %slice-start.3 = ((s8[5242880]{0:T(1024)(128)(4,1)}), s8[1048576]{0:T(1024)(128)(4,1)S(1)}, s32[]{:S(2)}) async-start(s8[5242880]{0:T(1024)(128)(4,1)} %bitcast.18), calls=%async_computation.3 | async-start | bytes 2097152
  151.4 87.3 %collective-permute-start.11 = (bf16[1,512,1280]{2,1,0:T(8,128)(2,1)}, bf16[1,512,1280]{2,1,0:T(8,128)(2,1)}, u32[]{:S(2)}, u32[]{:S(2)}) collective-permute-start(bf16[1,512,1280]{2,1,0:T(8,128)(2,1)} %copy-done.6), channel_id=1, source_target_pairs={{0,1},{1,0},{2,3},{3,2},{4,5},{5,4},{6,7},{7,6}} | collective-permute-start | bytes 3932168 | tf_op jit(solution)/shard_map/ppermute | solution.py:635
  151.5 87.3 %collective-permute-start.13 = (bf16[1,1280,512]{2,1,0:T(8,128)(2,1)}, bf16[1,1280,512]{2,1,0:T(8,128)(2,1)}, u32[]{:S(2)}, u32[]{:S(2)}) collective-permute-start(bf16[1,1280,512]{2,1,0:T(8,128)(2,1)} %copy-done.7), channel_id=1, source_target_pairs={{0,1},{1,0},{2,3},{3,2},{4,5},{5,4},{6,7},{7,6}} | collective-permute-start | bytes 3932168 | tf_op jit(solution)/shard_map/ppermute | solution.py:635
  151.9 86.8 %collective-permute-start.10 = (bf16[1,512,1280]{2,1,0:T(8,128)(2,1)}, bf16[1,512,1280]{2,1,0:T(8,128)(2,1)}, u32[]{:S(2)}, u32[]{:S(2)}) collective-permute-start(bf16[1,512,1280]{2,1,0:T(8,128)(2,1)} %get-tuple-element.34.refs_2_), channel_id=1, source_target_pairs={{0,1},{1,0},{2,3},{3,2},{4,5},{5,4},{6,7},{7,6}} | collective-permute-start | bytes 3932168 | tf_op jit(solution)/shard_map/ppermute | solution.py:635
  152.0 1.1 copy-start.4
  153.1 1.3 copy-start.9
  154.4 1.3 copy-start.11
  168.1 1.1 copy-start.12
  169.1 0.6 copy-start.13
  169.7 0.6 copy-start.14
  170.3 68.4 %collective-permute-start.12 = (bf16[1,1280,512]{2,1,0:T(8,128)(2,1)}, bf16[1,1280,512]{2,1,0:T(8,128)(2,1)S(1)}, u32[]{:S(2)}, u32[]{:S(2)}) collective-permute-start(bf16[1,1280,512]{2,1,0:T(8,128)(2,1)} %get-tuple-element.36.refs_8_), channel_id=1, source_target_pairs={{0,1},{1,0},{2,3},{3,2},{4,5},{5,4},{6,7},{7,6}} | collective-permute-start | bytes 3932168 | tf_op jit(solution)/shard_map/ppermute | solution.py:635
  238.8 1.1 copy-start.15

commit v3 on v2

--- a/solution.py
+++ b/solution.py
@@ -13,6 +13,8 @@
 F32 = jnp.float32
 BF16 = jnp.bfloat16
 CH = 512
+HEADS = 4
+GW = HEADS * 64
 VMEM_LIMIT = 62 * 1024 * 1024
 ANY = pl.BlockSpec(memory_space=pl.ANY)
 SMEM = pl.BlockSpec(memory_space=pltpu.SMEM)
@@ -27,10 +29,6 @@
 
 def dot(a, b):
     return jnp.dot(a, b, preferred_element_type=F32)
-
-
-def dot_nt(a, b):
-    return lax.dot_general(a, b, (((1,), (1,)), ((), ())), preferred_element_type=F32)
 
 
 def kv_kernel(layers, n_src, lim_ref, pick_ref, *refs):
@@ -115,58 +113,68 @@
     )(lims, pick, *srcs, wk, wv)
 
 
-def pair_queries(q):
-    lane = lax.broadcasted_iota(jnp.int32, q.shape, 1)
-    zero = jnp.zeros_like(q)
-    return jnp.where(lane < 64, q, zero), jnp.where(lane < 64, zero, q)
-
-
-def attend_all(pairs, n_chunks, scores, values, enter, leave, scratch):
+def head_queries(qt, extra=None):
+    row = lax.broadcasted_iota(jnp.int32, (128, qt.shape[1]), 0)
+    out = []
+    for h in range(HEADS):
+        pair = qt[h // 2 * 128:(h // 2 + 1) * 128, :]
+        q = jnp.where((row < 64) == (h % 2 == 0), pair, jnp.zeros_like(pair))
+        out.append(q if extra is None else jnp.concatenate([q, extra], axis=0))
+    return out
+
+
+def attend_all(groups, n_chunks, scores, values, enter, leave, scratch):
     s_refs, mx_refs, (m_ref, l_ref, acc_ref) = scratch[:2], scratch[2:4], scratch[4:]
-
-    def stage1(pair, j, buf):
-        for h, s in enumerate(scores(pair, j)):
+    total = groups * n_chunks
+
+    def stage1(group, j, buf):
+        for h, s in enumerate(scores(group, j)):
             s_refs[buf][h] = s
             mx_refs[buf][h:h + 1, :] = jnp.max(s, axis=0, keepdims=True)
 
-    def stage2(pair, j, buf):
-        vt = values(pair, j)
-        for h in range(2):
-            m_old = m_ref[pair, h:h + 1, :]
+    def stage2(group, j, buf):
+        vt = values(group, j)
+        for h in range(HEADS):
+            m_old = m_ref[group, h:h + 1, :]
             m_new = jnp.maximum(m_old, mx_refs[buf][h:h + 1, :])
             p = jnp.exp(s_refs[buf][h] - m_new)
             alpha = jnp.exp(m_old - m_new)
-            m_ref[pair, h:h + 1, :] = m_new
-            l_ref[pair, h:h + 1, :] = l_ref[pair, h:h + 1, :] * alpha + jnp.sum(p, axis=0, keepdims=True)
-            acc_ref[pair, h] = acc_ref[pair, h] * alpha + dot(vt[h * 64:(h + 1) * 64, :], p.astype(BF16))
-
-    def advance(pair, j):
+            m_ref[group, h:h + 1, :] = m_new
+            l_ref[group, h:h + 1, :] = l_ref[group, h:h + 1, :] * alpha + jnp.sum(p, axis=0, keepdims=True)
+            acc_ref[group, h] = acc_ref[group, h] * alpha + dot(vt[h * 64:(h + 1) * 64, :], p.astype(BF16))
+
+    def advance(group, j):
         wrap = j + 1 == n_chunks
-        return jnp.where(wrap, pair + 1, pair), jnp.where(wrap, 0, j + 1)
+        return jnp.where(wrap, group + 1, group), jnp.where(wrap, 0, j + 1)
 
     enter(0)
     stage1(0, 0, 0)
 
-    def step(_, now):
-        pair, j = now
-        for buf in range(2):
-            pair_next, j_next = advance(pair, j)
-
-            @pl.when((j_next == 0) & (pair_next < pairs))
-            def _(pair_next=pair_next):
-                enter(pair_next)
-
-            stage1(jnp.minimum(pair_next, pairs - 1), j_next, 1 - buf)
-            stage2(pair, j, buf)
-
-            @pl.when(j_next == 0)
-            def _(pair=pair):
-                leave(pair)
-
-            pair, j = pair_next, j_next
-        return pair, j
-
-    lax.fori_loop(0, pairs * n_chunks // 2, step, (jnp.int32(0), jnp.int32(0)))
+    def item(group, j, buf):
+        group_next, j_next = advance(group, j)
+
+        @pl.when((j_next == 0) & (group_next < groups))
+        def _():
+            enter(group_next)
+
+        stage1(jnp.minimum(group_next, groups - 1), j_next, 1 - buf)
+        stage2(group, j, buf)
+
+        @pl.when(j_next == 0)
+        def _():
+            leave(group)
+
+    def step(u, now):
+        item(*now, 0)
+        now = advance(*now)
+
+        @pl.when(2 * u + 1 < total)
+        def _():
+            item(*now, 1)
+
+        return advance(*now)
+
+    lax.fori_loop(0, (total + 1) // 2, step, (jnp.int32(0), jnp.int32(0)))
 
 
 def attend_reset(scratch):
@@ -176,22 +184,22 @@
     acc_ref[...] = jnp.zeros_like(acc_ref)
 
 
-def attend_finish(pair, at_ref, scratch):
+def attend_finish(group, at_ref, scratch):
     l_ref, acc_ref = scratch[5:]
-    for h in range(2):
-        rows = pl.ds(pl.multiple_of(pair * 128 + h * 64, 64), 64)
-        at_ref[rows, :] = (acc_ref[pair, h] / l_ref[pair, h:h + 1, :]).astype(BF16)
-
-
-def attend_scratch(pairs, rows):
+    for h in range(HEADS):
+        rows = pl.ds(pl.multiple_of(group * HEADS * 64 + h * 64, 64), 64)
+        at_ref[rows, :] = (acc_ref[group, h] / l_ref[group, h:h + 1, :]).astype(BF16)
+
+
+def attend_scratch(groups, rows):
     return [
-        pltpu.VMEM((2, CH, rows), F32),
-        pltpu.VMEM((2, CH, rows), F32),
-        pltpu.VMEM((2, rows), F32),
-        pltpu.VMEM((2, rows), F32),
-        pltpu.VMEM((pairs, 2, rows), F32),
-        pltpu.VMEM((pairs, 2, rows), F32),
-        pltpu.VMEM((pairs, 2, 64, rows), F32),
+        pltpu.VMEM((HEADS, CH, rows), F32),
+        pltpu.VMEM((HEADS, CH, rows), F32),
+        pltpu.VMEM((HEADS, rows), F32),
+        pltpu.VMEM((HEADS, rows), F32),
+        pltpu.VMEM((groups, HEADS, rows), F32),
+        pltpu.VMEM((groups, HEADS, rows), F32),
+        pltpu.VMEM((groups, HEADS, 64, rows), F32),
     ]
 
 
@@ -272,7 +280,7 @@
         return pl.ds(pl.multiple_of(t * 256, 256), 256)
 
     def head_cols(i):
-        return pl.ds(pl.multiple_of(i * 128, 128), 128)
+        return pl.ds(pl.multiple_of(i * GW, GW), GW)
 
     def phase(half, _):
         at = pl.ds(pl.multiple_of(half * CH, CH), CH)
@@ -318,16 +326,16 @@
             w_copies[4].start()
 
             def project_q(t, _):
-                qs[:, tile(t)] = dot(x_s[pl.ds(0, rows), :], w_s[2, :, tile(t)]).astype(BF16) * BF16(0.125)
+                qs[tile(t), :] = (dot(x_s[pl.ds(0, rows), :], w_s[2, :, tile(t)]).astype(BF16) * BF16(0.125)).T
                 return 0
 
             lax.fori_loop(0, tiles, project_q, 0)
 
         def scores(i, j):
             k = k_s[at, head_cols(i)]
-            return [dot_nt(k, q) + bias[half] for q in pair_queries(qs[:, head_cols(i)])]
-
-        attend_all(width // 128, 1, scores, lambda i, j: vt_s[head_cols(i), at], lambda i: None, lambda i: None, scratch)
+            return [dot(k[:, h // 2 * 128:(h // 2 + 1) * 128], q) + bias[half] for h, q in enumerate(head_queries(qs[head_cols(i), :]))]
+
+        attend_all(width // GW, 1, scores, lambda i, j: vt_s[head_cols(i), at], lambda i: None, lambda i: None, scratch)
         return 0
 
     lax.fori_loop(0, jnp.where(chip1, 2, 1), phase, 0)
@@ -336,7 +344,7 @@
         attend_finish(i, at_s, scratch)
         return 0
 
-    lax.fori_loop(0, width // 128, finish, 0)
+    lax.fori_loop(0, width // GW, finish, 0)
     a_s[...] = at_s[...].T
     w_copies[3].wait()
 
@@ -351,7 +359,7 @@
 
     def project_cq(t, _):
         cols = tile(t)
-        q_ref[:, cols] = dot(a_s[...], w_s[4, :, cols]).astype(BF16) * BF16(0.125)
+        q_ref[cols, :] = (dot(a_s[...], w_s[4, :, cols]).astype(BF16) * BF16(0.125)).T
         return 0
 
     lax.fori_loop(0, tiles, project_cq, 0)
@@ -383,20 +391,20 @@
         functools.partial(self_kernel, layer, far_given),
         in_specs=[VMEM] * (4 if far_given else 3) + [ANY] * 5,
         out_specs=[VMEM, VMEM],
-        out_shape=[shape, shape],
+        out_shape=[shape, jax.ShapeDtypeStruct((width, rows), BF16)],
         scratch_shapes=[
             pltpu.VMEM((5, width, width), BF16),
             pltpu.VMEM((4 * rows, width), BF16),
             pltpu.VMEM((4 * rows, width), BF16),
             pltpu.VMEM((width, 4 * rows), BF16),
-            block,
+            pltpu.VMEM((width, rows), BF16),
             pltpu.VMEM((2, 2 * rows, rows), F32),
             pltpu.VMEM((width, rows), BF16),
             block,
             block,
             block,
             *([] if far_given else [block]),
-            *attend_scratch(width // 128, rows),
+            *attend_scratch(width // GW, rows),
             pltpu.SemaphoreType.DMA((5,)),
             pltpu.SemaphoreType.DMA((2,)),
             pltpu.SemaphoreType.DMA((2, parts)),
@@ -408,28 +416,24 @@
     )(own, *([far] if far_given else []), gs, gc, wq, wk, wv, wo, wcq)
 
 
-def cross_kernel(layer, planes, n_kv, state_in, mlp, lim_ref, q_ref, *refs):
+def cross_kernel(layer, planes, n_kv, lim_ref, q_ref, *refs):
     def take(n):
         nonlocal refs
         head, refs = refs[:n], refs[n:]
         return head
 
     ks, vts = take(n_kv), take(n_kv)
-    state = take(3) if state_in else None
-    if mlp:
-        hid_ref, gm_ref, wco, wg, wu, wd, out_ref = take(7)
-    else:
-        outs = take(3)
+    hid_ref, gm_ref, wco, wg, wu, wd, out_ref = take(7)
     scratch = take(7)
     kbuf, vbuf, mask, list_s, kv_sems = take(5)
-    if mlp:
-        at_s, a_s, x_s, acc_o, wo_s, wg_s, wu_s, wd_s, o_sem, w_sems = take(10)
-        steps, ff = wg_s.shape[0], wg_s.shape[2]
-    rows, width = q_ref.shape
-    pairs = width // 128
-
-    def kv_copies(i, slot):
-        cols = pl.ds(pl.multiple_of(i * 128, 128), 128)
+    at_s, a_s, x_s, acc_o, wo_s, wg_s, wu_s, wd_s, o_sem, w_sems = take(10)
+    steps, ff = wg_s.shape[0], wg_s.shape[2]
+    width, rows = q_ref.shape
+    groups = width // GW
+
+    def kv_copies(i):
+        slot = lax.rem(i, 2)
+        cols = pl.ds(pl.multiple_of(i * GW, GW), GW)
         out, at = [], 0
         for n in range(n_kv):
             n_rows = ks[n].shape[1]
@@ -438,28 +442,18 @@
             at += n_rows
         return out
 
-    for cp in kv_copies(0, 0):
-        cp.start()
-    if mlp:
-        o_copy = pltpu.make_async_copy(wco.at[layer], wo_s, o_sem)
-
-        def w_copies(j):
-            cols = pl.ds(pl.multiple_of(j * ff, ff), ff)
-            return (pltpu.make_async_copy(wg.at[layer, :, cols], wg_s.at[j], w_sems.at[0, j]),
-                    pltpu.make_async_copy(wu.at[layer, :, cols], wu_s.at[j], w_sems.at[1, j]),
-                    pltpu.make_async_copy(wd.at[layer, cols, :], wd_s.at[j], w_sems.at[2, j]))
-
-        def start_weights(j):
-            for cp in w_copies(j):
-                cp.start()
-
-        o_copy.start()
-
-    if state_in:
-        for src, dst in zip(state, scratch[4:]):
-            dst[...] = src[...]
-    else:
-        attend_reset(scratch)
+    for i in range(2):
+        for cp in kv_copies(i):
+            cp.start()
+    o_copy = pltpu.make_async_copy(wco.at[layer], wo_s, o_sem)
+
+    def w_copies(j):
+        cols = pl.ds(pl.multiple_of(j * ff, ff), ff)
+        return (pltpu.make_async_copy(wg.at[layer, :, cols], wg_s.at[j], w_sems.at[0, j]),
+                pltpu.make_async_copy(wu.at[layer, :, cols], wu_s.at[j], w_sems.at[1, j]),
+                pltpu.make_async_copy(wd.at[layer, cols, :], wd_s.at[j], w_sems.at[2, j]))
+
+    attend_reset(scratch)
 
     n_chunks, last = jnp.int32(0), jnp.int32(0)
     list_s[0] = 0
@@ -476,57 +470,46 @@
     lane = lax.broadcasted_iota(jnp.int32, (CH, 128), 1)
     mask[0] = jnp.zeros((CH, 128), BF16)
     mask[1] = jnp.where((key >= last) & (lane == 0), NEG_BIG, 0.0).astype(BF16)
-    ones = (lax.broadcasted_iota(jnp.int32, (rows, 128), 1) == 0).astype(F32).astype(BF16)
+    ones = (lax.broadcasted_iota(jnp.int32, (128, rows), 0) == 0).astype(F32).astype(BF16)
 
     def enter(i):
-        @pl.when(i + 1 < pairs)
-        def _():
-            for cp in kv_copies(i + 1, lax.rem(i + 1, 3)):
+        for cp in kv_copies(i):
+            cp.wait()
+
+        @pl.when(i == 0)
+        def _():
+            o_copy.start()
+
+        for j in range(2):
+            for cp in w_copies(2 * i + j):
                 cp.start()
 
-        if mlp:
-            @pl.when(i < steps)
-            def _():
-                start_weights(i)
-
-        for cp in kv_copies(i, lax.rem(i, 3)):
-            cp.wait()
+    def leave(i):
+        @pl.when(i + 2 < groups)
+        def _():
+            for cp in kv_copies(i + 2):
+                cp.start()
 
     def chunk(j):
         return pl.ds(pl.multiple_of(list_s[j] * CH, CH), CH)
 
     def scores(i, j):
-        k = kbuf[lax.rem(i, 3), chunk(j), :]
         partial = (lim_ref[list_s[j]] < CH).astype(jnp.int32)
-        cols = pl.ds(pl.multiple_of(i * 128, 128), 128)
-        k = jnp.concatenate([k, mask[partial]], axis=1)
-        return [dot_nt(k, jnp.concatenate([q, ones], axis=1)) for q in pair_queries(q_ref[:, cols])]
+        k = kbuf[lax.rem(i, 2), chunk(j), :]
+        ks = [jnp.concatenate([k[:, p * 128:(p + 1) * 128], mask[partial]], axis=1) for p in range(HEADS // 2)]
+        queries = head_queries(q_ref[pl.ds(pl.multiple_of(i * GW, GW), GW), :], ones)
+        return [dot(ks[h // 2], q) for h, q in enumerate(queries)]
 
     def values(i, j):
-        return vbuf[lax.rem(i, 3), :, chunk(j)]
-
-    @pl.when(n_chunks > 0)
-    def _():
-        attend_all(pairs, n_chunks, scores, values, enter, lambda i: None, scratch)
-
-    @pl.when(n_chunks == 0)
-    def _():
-        for cp in kv_copies(0, 0):
-            cp.wait()
-        if mlp:
-            for j in range(steps):
-                start_weights(j)
-
-    if not mlp:
-        for src, dst in zip(scratch[4:], outs):
-            dst[...] = src[...]
-        return
+        return vbuf[lax.rem(i, 2), :, chunk(j)]
+
+    attend_all(groups, n_chunks, scores, values, enter, leave, scratch)
 
     def finish(i, _):
         attend_finish(i, at_s, scratch)
         return 0
 
-    lax.fori_loop(0, pairs, finish, 0)
+    lax.fori_loop(0, groups, finish, 0)
     a_s[...] = at_s[...].T
     o_copy.wait()
 
@@ -553,36 +536,26 @@
     out_ref[...] = (out_ref[...].astype(F32) + acc_o[...]).astype(BF16)
 
 
-def cross(layer, lims, q, kvs, state=None, after=None):
-    rows, width = q.shape
-    pairs = width // 128
+def cross_mlp(layer, lims, q, kvs, hid, gm, wco, wg, wu, wd):
+    width, rows = q.shape
+    groups = width // GW
     planes = tuple(plane for _, _, plane in kvs)
     ks, vts = [k for k, _, _ in kvs], [v for _, v, _ in kvs]
     total = sum(k.shape[1] for k in ks)
     n = len(kvs)
-    operands, specs = [lims, q, *ks, *vts], [SMEM, VMEM] + [ANY] * (2 * n)
-    if state is not None:
-        operands, specs = operands + list(state), specs + [VMEM] * 3
-    scratch = attend_scratch(pairs, rows) + [
-        pltpu.VMEM((3, total, 128), BF16),
-        pltpu.VMEM((3, 128, total), BF16),
-        pltpu.VMEM((2, CH, 128), BF16),
-        pltpu.SMEM((8,), jnp.int32),
-        pltpu.SemaphoreType.DMA((3, 2, n)),
-    ]
-    flops = 4 * rows * min(total, 3072) * width
-    if after is None:
-        out_shape = [jax.ShapeDtypeStruct((pairs, 2, rows), F32)] * 2 + [jax.ShapeDtypeStruct((pairs, 2, 64, rows), F32)]
-        out_specs = [VMEM] * 3
-        moved = 8 * total * width
-        limit = 32 * 1024 * 1024
-    else:
-        _, _, _, wg, _, _ = after
-        operands, specs = operands + list(after), specs + [VMEM] * 2 + [ANY] * 4
-        out_shape, out_specs = jax.ShapeDtypeStruct((rows, width), BF16), VMEM
-        steps = 10
-        ff = wg.shape[2] // steps
-        scratch += [
+    steps = 2 * groups
+    ff = wg.shape[2] // steps
+    return pl.pallas_call(
+        functools.partial(cross_kernel, layer, planes, n),
+        in_specs=[SMEM, VMEM] + [ANY] * (2 * n) + [VMEM] * 2 + [ANY] * 4,
+        out_specs=VMEM,
+        out_shape=jax.ShapeDtypeStruct((rows, width), BF16),
+        scratch_shapes=attend_scratch(groups, rows) + [
+            pltpu.VMEM((2, total, GW), BF16),
+            pltpu.VMEM((2, GW, total), BF16),
+            pltpu.VMEM((2, CH, 128), BF16),
+            pltpu.SMEM((8,), jnp.int32),
+            pltpu.SemaphoreType.DMA((2, 2, n)),
             pltpu.VMEM((width, rows), BF16),
             pltpu.VMEM((rows, width), BF16),
             pltpu.VMEM((rows, width), BF16),
@@ -593,20 +566,13 @@
             pltpu.VMEM((steps, ff, width), BF16),
             pltpu.SemaphoreType.DMA,
             pltpu.SemaphoreType.DMA((3, steps)),
-        ]
-        flops += 2 * rows * width * (width + 3 * wg.shape[2])
-        moved = 2 * width * (width + 3 * wg.shape[2])
-        limit = VMEM_LIMIT
-    return pl.pallas_call(
-        functools.partial(cross_kernel, layer, planes, n, state is not None, after is not None),
-        in_specs=specs,
-        out_specs=out_specs,
-        out_shape=out_shape,
-        scratch_shapes=scratch,
-        cost_estimate=pl.CostEstimate(flops=flops, bytes_accessed=moved, transcendentals=0),
-        compiler_params=pltpu.CompilerParams(vmem_limit_bytes=limit),
-        name="cross_attention" if after is None else "cross_mlp",
-    )(*operands)
+        ],
+        cost_estimate=pl.CostEstimate(
+            flops=4 * rows * 3072 * width + 2 * rows * width * (width + 3 * wg.shape[2]),
+            bytes_accessed=2 * width * (width + 3 * wg.shape[2]), transcendentals=0),
+        compiler_params=pltpu.CompilerParams(vmem_limit_bytes=VMEM_LIMIT),
+        name="cross_mlp",
+    )(lims, q, *ks, *vts, hid, gm, wco, wg, wu, wd)
 
 
 NONE = 1 << 20
@@ -644,22 +610,17 @@
             both = (0, layers)
             ka, va = kv_project(lims[0:2], is3, [memory, c2b], cross_k, cross_v, 2 * CH, both)
             kas, vas = swap(ka), swap(va)
+            kb, vb = kv_project(lims[4:5], is3, [rem_a], cross_k, cross_v, CH, both)
+            kbs, vbs = swap(kb), swap(vb)
             kvs = []
             for layer in range(layers):
-                kvs.append([(ka, va, layer), (kas, vas, layer)])
-            for layer in range(layers):
-                for rem, at in ((rem_a, 4), (rem_b, 6)):
-                    k, v = kv_project(lims[at:at + 1], is3, [rem], cross_k, cross_v, CH, (layer, 1))
-                    kvs[layer] += [(k, v, 0), (swap(k), swap(v), 0)]
+                kc, vc = kv_project(lims[6:7], is3, [rem_b], cross_k, cross_v, CH, (layer, 1))
+                kcs, vcs = swap(kc), swap(vc)
+                kvs.append([(ka, va, layer), (kas, vas, layer), (kb, vb, layer), (kbs, vbs, layer), (kc, vc, 0), (kcs, vcs, 0)])
 
             for layer in range(layers):
                 hidden, q = self_attention(layer, hidden, far, norm_self, norm_cross, self_q, self_k, self_v, w_so, cross_q)
-                after = (hidden, norm_mlp, w_co, mlp_gate, mlp_up, mlp_down)
-                if layer == 0:
-                    state = cross(layer, lims[:6], q, kvs[layer][:4])
-                    hidden = cross(layer, lims[6:], q, kvs[layer][4:], state, after)
-                else:
-                    hidden = cross(layer, lims, q, kvs[layer], None, after)
+                hidden = cross_mlp(layer, lims, q, kvs[layer], hidden, norm_mlp, w_co, mlp_gate, mlp_up, mlp_down)
                 far = None
             return hidden
 

time: 282 us -> 265 us (0.940)
  local copies, waits for them, and re-layouts: 16.4 us -> 6.24 us
  starting transfers between devices: 14.3 us -> 7.72 us
  Pallas kernels: 189 us -> 185 us
  waiting for transfers between devices: 60.3 us -> 63.5 us
    ppermute x1, waiting for transfers between devices: 15.1 us -> 39.5 us  [program(): rem_b = lax.ppermute(mem_b, 'sp', [(0, 2), (1, 3), (2, 1)])]
    ppermute x1, waiting for transfers between devices: 39.2 us -> 19.7 us  [program(): rem_a = lax.ppermute(mem_a, 'sp', [(0, 2), (1, 3), (2, 0)])]
    unnamed x48 -> x16, local copies, waits for them, and re-layouts: 11.6 us -> 2.14 us
    ppermute x10 -> x8, starting transfers between devices: 9.19 us -> 2.58 us  [swap(): return lax.ppermute(x, 'sp', [(0, 1), (1, 0), (2, 3), (3, 2)])]
    pallas_call x3 -> x2, Pallas kernels: 87.9 us -> 84.4 us  [cross_mlp(): pl.pallas_call(functools.partial(cross_kernel, layer, planes, n), in_spec...]
    pallas_call x2, Pallas kernels: 63.3 us -> 66.8 us  [self_attention(): pl.pallas_call(functools.partial(self_kernel, layer, far_given), in_specs...]
    pallas_call x5 -> x4, Pallas kernels: 37.3 us -> 34 us  [kv_project(): pl.pallas_call(functools.partial(kv_kernel, layers, len(srcs)), in_specs=...]
  transfers between devices with their start and end apart: 14 -> 12, of which waited for: 4 -> 4; matrix products, arithmetic and copies ran while one was open for 1% -> 0% of each run, Pallas kernels for 50% -> 52%
where the time goes in v3:
time: 265 us; the launch traced here: 264 us
  Pallas kernels  185 us (70%)
  waiting for transfers between devices  63.5 us (24%)
  starting transfers between devices  7.72 us (3%)
  local copies, waits for them, and re-layouts  6.24 us (2%)
    pallas_call x2, Pallas kernels, cross_mlp(): pl.pallas_call(functools.partial(cross_kernel, layer, planes, n), in_spec...  84.4 us
    pallas_call x2, Pallas kernels, self_attention(): pl.pallas_call(functools.partial(self_kernel, layer, far_given), in_specs...  66.8 us
    ppermute x1, waiting for transfers between devices, program(): rem_b = lax.ppermute(mem_b, 'sp', [(0, 2), (1, 3), (2, 1)])  39.5 us
    pallas_call x4, Pallas kernels, kv_project(): pl.pallas_call(functools.partial(kv_kernel, layers, len(srcs)), in_specs=...  34 us
    ppermute x1, waiting for transfers between devices, program(): rem_a = lax.ppermute(mem_a, 'sp', [(0, 2), (1, 3), (2, 0)])  19.7 us
  transfers between devices with their start and end apart: 12, of which 4 were waited for; matrix products, arithmetic and copies ran while one was open for 0% of the time, Pallas kernels for 52%

profile of v3, /device:TPU:7, one launch (start us, length us, event | category | flops | bytes accessed | tf_op | source)
XLA Modules:
  0.0 264.3 jit_solution(13925163018161558440)
XLA Ops:
  0.0 0.0 copy-start.5
  0.0 0.0 copy-start
  0.0 3.5 %fusion = (bf16[512,1280]{1,0:T(8,128)(2,1)}, bf16[512,1280]{1,0:T(8,128)(2,1)}) fusion(bf16[1024,1280]{1,0:T(8,128)(2,1)} %refs_0_.3), kind=kLoop, calls=%fused_computation.2 | loop fusion | bytes 5242880 | tf_op jit(solution)/shard_map/slice | solution.py:605
  3.5 1.3 collective-permute-start.1
  5.5 0.0 copy-done.5
  5.5 3.3 %collective-permute-done.1.refs_1_ = bf16[512,1280]{1,0:T(8,128)(2,1)} collective-permute-done((bf16[512,1280]{1,0:T(8,128)(2,1)}, bf16[512,1280]{1,0:T(8,128)(2,1)}, u32[]{:S(2)}, u32[]{:S(2)}) %collective-permute-start.1) | collective-permute-done | bytes 1310752 | tf_op jit(solution)/shard_map/ppermute | solution.py:606
  8.8 0.0 copy-done
  8.8 0.0 copy-start.4
  8.8 5.8 %kv_project.4 = (bf16[2,1024,1280]{2,1,0:T(8,128)(2,1)}, bf16[2,1280,1024]{2,1,0:T(8,128)(2,1)}) custom-call(s32[2]{0:T(128)S(1)} %slice_bitcast_fusion.lim_ref, s32[1]{0:T(128)} %bitcast.4.pick_ref, bf16[1024,1280]{1,0:T(8,128)(2,1)S(1)} %copy-done, bf16[512,1280]{1,0:T(8,128)(2,1)} %collective-permute-done.1.refs_1_, bf16[2,1280,1280]{2,1,0:T(8,128)(2,1)} %refs_1_.7, ...), custom_call_target="tpu_custom_call" | custom-call | flops 13421772800 | bytes 13107200 | tf_op jit(solution)/shard_map/kv_project/pallas_call | solution.py:96
  14.6 0.0 collective-permute-start.2
  14.7 0.5 collective-permute-start.7
  15.1 1.3 collective-permute-start.5
  16.4 0.0 copy-done.4
  16.4 1.3 collective-permute-start.3
  17.7 0.0 copy-done.6
  17.8 1.3 collective-permute-start
  19.1 0.6 fusion.1
  19.6 39.5 %collective-permute-done.5.refs_0_ = bf16[512,1280]{1,0:T(8,128)(2,1)S(1)} collective-permute-done((bf16[512,1280]{1,0:T(8,128)(2,1)}, bf16[512,1280]{1,0:T(8,128)(2,1)S(1)}, u32[]{:S(2)}, u32[]{:S(2)}) %collective-permute-start.5) | collective-permute-done | bytes 1310752 | tf_op jit(solution)/shard_map/ppermute | solution.py:608
  59.1 7.9 %kv_project.6 = (bf16[1,512,1280]{2,1,0:T(8,128)(2,1)S(1)}, bf16[1,1280,512]{2,1,0:T(8,128)(2,1)}) custom-call(s32[1]{0:T(128)} %bitcast.6.lim_ref, s32[1]{0:T(128)} %bitcast.4.pick_ref, bf16[512,1280]{1,0:T(8,128)(2,1)S(1)} %collective-permute-done.5.refs_0_, bf16[2,1280,1280]{2,1,0:T(8,128)(2,1)} %refs_1_.7, bf16[2,1280,1280]{2,1,0:T(8,128)(2,1)} %refs_2_.11), custom_call_target="tpu_custom_call" | custom-call | flops 3355443200 | bytes 6553600 | tf_op jit(solution)/shard_map/kv_project/pallas_call | solution.py:96
  67.1 0.0 copy-start.1
  67.1 0.5 collective-permute-start.6
  67.5 19.7 %collective-permute-done.3.refs_0_ = bf16[512,1280]{1,0:T(8,128)(2,1)S(1)} collective-permute-done((bf16[512,1280]{1,0:T(8,128)(2,1)S(1)}, bf16[512,1280]{1,0:T(8,128)(2,1)S(1)}, u32[]{:S(2)}, u32[]{:S(2)}) %collective-permute-start.3) | collective-permute-done | bytes 1310752 | tf_op jit(solution)/shard_map/ppermute | solution.py:607
  87.2 12.4 %kv_project.5 = (bf16[2,512,1280]{2,1,0:T(8,128)(2,1)}, bf16[2,1280,512]{2,1,0:T(8,128)(2,1)}) custom-call(s32[1]{0:T(128)} %bitcast.5.lim_ref, s32[1]{0:T(128)} %bitcast.4.pick_ref, bf16[512,1280]{1,0:T(8,128)(2,1)S(1)} %collective-permute-done.3.refs_0_, bf16[2,1280,1280]{2,1,0:T(8,128)(2,1)} %refs_1_.7, bf16[2,1280,1280]{2,1,0:T(8,128)(2,1)} %refs_2_.11), custom_call_target="tpu_custom_call" | custom-call | flops 6710886400 | bytes 13107200 | tf_op jit(solution)/shard_map/kv_project/pallas_call | solution.py:96
  99.7 0.0 copy-done.1
  99.7 0.5 collective-permute-start.4
  100.2 1.1 collective-permute-done.refs_1_
  101.3 0.4 collective-permute-start.8
  101.7 0.0 collective-permute-done.6.refs_5_
  101.7 1.1 copy-done.2
  102.8 0.2 collective-permute-start.9
  102.9 0.5 fusion.2.lim_ref
  103.4 0.0 copy-done.7
  103.4 33.3 %self_attention.2 = (bf16[256,1280]{1,0:T(8,128)(2,1)}, bf16[1280,256]{1,0:T(8,128)(2,1)}) custom-call(bf16[256,1280]{1,0:T(8,128)(2,1)} %refs_0_.2, bf16[256,1280]{1,0:T(8,128)(2,1)} %copy-done.7, bf16[2,1280]{1,0:T(2,128)(2,1)} %refs_1_.6, bf16[2,1280]{1,0:T(2,128)(2,1)} %refs_2_.10, bf16[2,1280,1280]{2,1,0:T(8,128)(2,1)} %refs_3_.5, ...), custom_call_target="tpu_custom_call" | custom-call | flops 10569646080 | bytes 16384000 | tf_op jit(solution)/shard_map/self_attention/pallas_call | solution.py:390
  136.7 7.8 %kv_project.7 = (bf16[1,512,1280]{2,1,0:T(8,128)(2,1)}, bf16[1,1280,512]{2,1,0:T(8,128)(2,1)}) custom-call(s32[1]{0:T(128)} %bitcast.6.lim_ref, s32[1]{0:T(128)} %bitcast.4.pick_ref, bf16[512,1280]{1,0:T(8,128)(2,1)S(1)} %collective-permute-done.5.refs_0_, bf16[2,1280,1280]{2,1,0:T(8,128)(2,1)} %refs_1_.7, bf16[2,1280,1280]{2,1,0:T(8,128)(2,1)} %refs_2_.11), custom_call_target="tpu_custom_call" | custom-call | flops 3355443200 | bytes 6553600 | tf_op jit(solution)/shard_map/kv_project/pallas_call | solution.py:96
  144.6 0.0 collective-permute-done.9.refs_11_
  144.6 0.0 collective-permute-start.10
  144.6 0.0 collective-permute-done.4.refs_3_
  144.6 0.5 collective-permute-start.11
  145.1 0.0 collective-permute-done.8.refs_9_
  145.1 0.0 collective-permute-done.2.refs_1_
  145.1 0.0 collective-permute-done.7.refs_7_
  145.1 42.3 %cross_mlp.2.refs_0_ = bf16[256,1280]{1,0:T(8,128)(2,1)} custom-call(s32[8]{0:T(128)} %fusion.2.lim_ref, bf16[1280,256]{1,0:T(8,128)(2,1)} %get-tuple-element.17.q_ref, bf16[2,1024,1280]{2,1,0:T(8,128)(2,1)} %get-tuple-element.18.refs_0_, bf16[2,1024,1280]{2,1,0:T(8,128)(2,1)} %collective-permute-done.2.refs_1_, ...), custom_call_target="tpu_custom_call" | custom-call | flops 14931722240 | bytes 42598400 | tf_op jit(solution)/shard_map/cross_mlp/pallas_call | solution.py:548
  187.4 33.5 %self_attention.3 = (bf16[256,1280]{1,0:T(8,128)(2,1)}, bf16[1280,256]{1,0:T(8,128)(2,1)}) custom-call(bf16[256,1280]{1,0:T(8,128)(2,1)} %cross_mlp.2.refs_0_, bf16[2,1280]{1,0:T(2,128)(2,1)} %refs_1_.6, bf16[2,1280]{1,0:T(2,128)(2,1)} %refs_2_.10, bf16[2,1280,1280]{2,1,0:T(8,128)(2,1)} %refs_3_.5, bf16[2,1280,1280]{2,1,0:T(8,128)(2,1)} %refs_4_.3, ...), custom_call_target="tpu_custom_call" | custom-call | flops 10569646080 | bytes 16384000 | tf_op jit(solution)/shard_map/self_attention/pallas_call | solution.py:390
  221.0 0.0 collective-permute-done.10.refs_5_
  221.0 0.0 copy-start.3
  221.0 0.0 collective-permute-done.11.refs_11_
  221.0 1.0 copy-done.3
  222.1 42.1 %cross_mlp.3 = bf16[256,1280]{1,0:T(8,128)(2,1)} custom-call(s32[8]{0:T(128)} %fusion.2.lim_ref, bf16[1280,256]{1,0:T(8,128)(2,1)} %get-tuple-element.25.q_ref, bf16[2,1024,1280]{2,1,0:T(8,128)(2,1)} %get-tuple-element.18.refs_0_, bf16[2,1024,1280]{2,1,0:T(8,128)(2,1)} %collective-permute-done.2.refs_1_, bf16[2,512,1280]{2,1,0:T(8,128)(2,1)} %get-tuple-element.19.refs_2_, ...), custom_call_target="tpu_custom_call" | custom-call | flops 14931722240 | bytes 42598400 | tf_op jit(solution)/shard_map/cross_mlp/pallas_call | solution.py:548
  (5 shorter events, 0.0 us)
Async XLA Ops:
  0.0 5.5 %copy-start.5 = (s32[4,8]{1,0:T(4,128)S(1)}, s32[4,8]{1,0:T(4,128)}, u32[]{:S(2)}) copy-start(s32[4,8]{1,0:T(4,128)} %constant.15.clone) | copy-start | bytes 388
  0.0 8.8 %copy-start = (bf16[1024,1280]{1,0:T(8,128)(2,1)S(1)}, bf16[1024,1280]{1,0:T(8,128)(2,1)}, u32[]{:S(2)}) copy-start(bf16[1024,1280]{1,0:T(8,128)(2,1)} %refs_0_.3) | copy-start | bytes 7864324
  3.5 5.3 %collective-permute-start.1 = (bf16[512,1280]{1,0:T(8,128)(2,1)}, bf16[512,1280]{1,0:T(8,128)(2,1)}, u32[]{:S(2)}, u32[]{:S(2)}) collective-permute-start(bf16[512,1280]{1,0:T(8,128)(2,1)} %get-tuple-element.30), channel_id=1, source_target_pairs={{2,3},{6,7}} | collective-permute-start | bytes 3932168 | tf_op jit(solution)/shard_map/ppermute | solution.py:606
  8.8 7.6 %copy-start.4 = (bf16[512,1280]{1,0:T(8,128)(2,1)S(1)}, bf16[512,1280]{1,0:T(8,128)(2,1)}, u32[]{:S(2)}) copy-start(bf16[512,1280]{1,0:T(8,128)(2,1)} %get-tuple-element.29) | copy-start | bytes 3932164
  8.8 9.0 %copy-start.6 = (bf16[256,1280]{1,0:T(8,128)(2,1)S(1)}, bf16[256,1280]{1,0:T(8,128)(2,1)}, u32[]{:S(2)}) copy-start(bf16[256,1280]{1,0:T(8,128)(2,1)} %refs_0_.2) | copy-start | bytes 1966084
  14.6 130.5 %collective-permute-start.2 = (bf16[2,1024,1280]{2,1,0:T(8,128)(2,1)}, bf16[2,1024,1280]{2,1,0:T(8,128)(2,1)}, u32[]{:S(2)}, u32[]{:S(2)}) collective-permute-start(bf16[2,1024,1280]{2,1,0:T(8,128)(2,1)} %get-tuple-element.18.refs_0_), channel_id=1, source_target_pairs={{0,1},{1,0},{2,3},{3,2},{4,5},{5,4},{6,7},{7,6}} | collective-permute-start | bytes 15728648 | tf_op jit(solution)/shard_map/ppermute | solution.py:601
  14.7 130.5 %collective-permute-start.7 = (bf16[2,1280,1024]{2,1,0:T(8,128)(2,1)}, bf16[2,1280,1024]{2,1,0:T(8,128)(2,1)}, u32[]{:S(2)}, u32[]{:S(2)}) collective-permute-start(bf16[2,1280,1024]{2,1,0:T(8,128)(2,1)} %get-tuple-element.21.refs_6_), channel_id=1, source_target_pairs={{0,1},{1,0},{2,3},{3,2},{4,5},{5,4},{6,7},{7,6}} | collective-permute-start | bytes 15728648 | tf_op jit(solution)/shard_map/ppermute | solution.py:601
  15.1 44.0 %collective-permute-start.5 = (bf16[512,1280]{1,0:T(8,128)(2,1)}, bf16[512,1280]{1,0:T(8,128)(2,1)S(1)}, u32[]{:S(2)}, u32[]{:S(2)}) collective-permute-start(bf16[512,1280]{1,0:T(8,128)(2,1)} %get-tuple-element.30), channel_id=1, source_target_pairs={{0,2},{1,3},{2,1},{4,6},{5,7},{6,5}} | collective-permute-start | bytes 3932168 | tf_op jit(solution)/shard_map/ppermute | solution.py:608
  16.4 70.8 %collective-permute-start.3 = (bf16[512,1280]{1,0:T(8,128)(2,1)S(1)}, bf16[512,1280]{1,0:T(8,128)(2,1)S(1)}, u32[]{:S(2)}, u32[]{:S(2)}) collective-permute-start(bf16[512,1280]{1,0:T(8,128)(2,1)S(1)} %copy-done.4), channel_id=1, source_target_pairs={{0,2},{1,3},{2,0},{4,6},{5,7},{6,4}} | collective-permute-start | bytes 3932168 | tf_op jit(solution)/shard_map/ppermute | solution.py:607
  17.8 83.5 %collective-permute-start = (bf16[256,1280]{1,0:T(8,128)(2,1)S(1)}, bf16[256,1280]{1,0:T(8,128)(2,1)S(1)}, u32[]{:S(2)}, u32[]{:S(2)}) collective-permute-start(bf16[256,1280]{1,0:T(8,128)(2,1)S(1)} %copy-done.6), channel_id=1, source_target_pairs={{0,2},{1,3},{4,6},{5,7}} | collective-permute-start | bytes 1966088 | tf_op jit(solution)/shard_map/ppermute | solution.py:604
  67.1 32.6 %copy-start.1 = (bf16[1,512,1280]{2,1,0:T(8,128)(2,1)}, bf16[1,512,1280]{2,1,0:T(8,128)(2,1)S(1)}, u32[]{:S(2)}) copy-start(bf16[1,512,1280]{2,1,0:T(8,128)(2,1)S(1)} %get-tuple-element.20.refs_4_) | copy-start | bytes 3932164
  67.1 34.6 %collective-permute-start.6 = (bf16[1,512,1280]{2,1,0:T(8,128)(2,1)S(1)}, bf16[1,512,1280]{2,1,0:T(8,128)(2,1)S(1)}, u32[]{:S(2)}, u32[]{:S(2)}) collective-permute-start(bf16[1,512,1280]{2,1,0:T(8,128)(2,1)S(1)} %get-tuple-element.20.refs_4_), channel_id=1, source_target_pairs={{0,1},{1,0},{2,3},{3,2},{4,5},{5,4},{6,7},{7,6}} | collective-permute-start | bytes 3932168 | tf_op jit(solution)/shard_map/ppermute | solution.py:601
  99.7 44.9 %collective-permute-start.4 = (bf16[2,512,1280]{2,1,0:T(8,128)(2,1)}, bf16[2,512,1280]{2,1,0:T(8,128)(2,1)}, u32[]{:S(2)}, u32[]{:S(2)}) collective-permute-start(bf16[2,512,1280]{2,1,0:T(8,128)(2,1)} %get-tuple-element.19.refs_2_), channel_id=1, source_target_pairs={{0,1},{1,0},{2,3},{3,2},{4,5},{5,4},{6,7},{7,6}} | collective-permute-start | bytes 7864328 | tf_op jit(solution)/shard_map/ppermute | solution.py:601
  101.3 2.2 copy-start.7
  101.3 43.9 %collective-permute-start.8 = (bf16[2,1280,512]{2,1,0:T(8,128)(2,1)}, bf16[2,1280,512]{2,1,0:T(8,128)(2,1)}, u32[]{:S(2)}, u32[]{:S(2)}) collective-permute-start(bf16[2,1280,512]{2,1,0:T(8,128)(2,1)} %get-tuple-element.22.refs_8_), channel_id=1, source_target_pairs={{0,1},{1,0},{2,3},{3,2},{4,5},{5,4},{6,7},{7,6}} | collective-permute-start | bytes 7864328 | tf_op jit(solution)/shard_map/ppermute | solution.py:601
  101.7 1.1 copy-start.2
  102.8 41.8 %collective-permute-start.9 = (bf16[1,1280,512]{2,1,0:T(8,128)(2,1)}, bf16[1,1280,512]{2,1,0:T(8,128)(2,1)}, u32[]{:S(2)}, u32[]{:S(2)}) collective-permute-start(bf16[1,1280,512]{2,1,0:T(8,128)(2,1)} %get-tuple-element.23.refs_10_), channel_id=1, source_target_pairs={{0,1},{1,0},{2,3},{3,2},{4,5},{5,4},{6,7},{7,6}} | collective-permute-start | bytes 3932168 | tf_op jit(solution)/shard_map/ppermute | solution.py:601
  144.6 76.4 %collective-permute-start.10 = (bf16[1,512,1280]{2,1,0:T(8,128)(2,1)}, bf16[1,512,1280]{2,1,0:T(8,128)(2,1)S(1)}, u32[]{:S(2)}, u32[]{:S(2)}) collective-permute-start(bf16[1,512,1280]{2,1,0:T(8,128)(2,1)} %get-tuple-element.26.refs_4_), channel_id=1, source_target_pairs={{0,1},{1,0},{2,3},{3,2},{4,5},{5,4},{6,7},{7,6}} | collective-permute-start | bytes 3932168 | tf_op jit(solution)/shard_map/ppermute | solution.py:601
  144.6 76.4 %collective-permute-start.11 = (bf16[1,1280,512]{2,1,0:T(8,128)(2,1)}, bf16[1,1280,512]{2,1,0:T(8,128)(2,1)}, u32[]{:S(2)}, u32[]{:S(2)}) collective-permute-start(bf16[1,1280,512]{2,1,0:T(8,128)(2,1)} %get-tuple-element.27.refs_10_), channel_id=1, source_target_pairs={{0,1},{1,0},{2,3},{3,2},{4,5},{5,4},{6,7},{7,6}} | collective-permute-start | bytes 3932168 | tf_op jit(solution)/shard_map/ppermute | solution.py:601
  221.0 1.1 copy-start.3

commit v4 on v3

--- a/solution.py
+++ b/solution.py
@@ -48,28 +48,34 @@
             def _():
                 go(pltpu.make_async_copy(srcs[1], mem.at[pl.ds(0, CH)], sem))
 
-    w_copies = []
+    def w_copy(i, v):
+        return pltpu.make_async_copy((wk, wv)[v].at[lo + i], w_s.at[2 * i + v], w_sems.at[2 * i + v])
+
+    w_copy(0, 0).start()
+    from_src(lambda cp: cp.start())
     for i in range(n):
-        for v, src in enumerate((wk, wv)):
-            w_copies.append(pltpu.make_async_copy(src.at[lo + i], w_s.at[2 * i + v], w_sems.at[2 * i + v]))
-    w_copies[0].start()
-    from_src(lambda cp: cp.start())
-    for cp in w_copies[1:]:
-        cp.start()
+        for v in range(2):
+            if i + v > 0:
+                w_copy(i, v).start()
     from_src(lambda cp: cp.wait())
 
     def out_copy(i, v, c):
-        at = pl.ds(c * CH, CH)
+        at = pl.ds(pl.multiple_of(c * CH, CH), CH)
         if v == 0:
             return pltpu.make_async_copy(k_s.at[i, at, :], k_out.at[i, at, :], o_sems.at[i, v, c])
         return pltpu.make_async_copy(vt_s.at[i, :, at], vt_out.at[i, :, at], o_sems.at[i, v, c])
 
-    for i in range(n):
+    def valid(c, go):
+        @pl.when(lim_ref[c] > 0)
+        def _():
+            go()
+
+    def layer_step(i, _):
         for v in range(2):
-            w_copies[2 * i + v].wait()
-            for c in range(rows // CH):
-                @pl.when(lim_ref[c] > 0)
-                def _(i=i, v=v, c=c):
+            w_copy(i, v).wait()
+
+            def chunk_step(c, _):
+                def work():
                     def step(r, _):
                         at = pl.ds(pl.multiple_of(c * CH + r * 256, 256), 256)
                         out = dot(mem[at, :], w_s[2 * i + v]).astype(BF16)
@@ -81,12 +87,18 @@
 
                     lax.fori_loop(0, CH // 256, step, 0)
                     out_copy(i, v, c).start()
+
+                valid(c, work)
+                return 0
+
+            lax.fori_loop(0, rows // CH, chunk_step, 0)
+        return 0
+
+    lax.fori_loop(0, n, layer_step, 0)
     for i in range(n):
         for v in range(2):
             for c in range(rows // CH):
-                @pl.when(lim_ref[c] > 0)
-                def _(i=i, v=v, c=c):
-                    out_copy(i, v, c).wait()
+                valid(c, lambda i=i, v=v, c=c: out_copy(i, v, c).wait())
 
 
 def kv_project(lims, pick, srcs, wk, wv, rows, layers):
@@ -129,19 +141,20 @@
 
     def stage1(group, j, buf):
         for h, s in enumerate(scores(group, j)):
-            s_refs[buf][h] = s
-            mx_refs[buf][h:h + 1, :] = jnp.max(s, axis=0, keepdims=True)
-
-    def stage2(group, j, buf):
-        vt = values(group, j)
-        for h in range(HEADS):
-            m_old = m_ref[group, h:h + 1, :]
-            m_new = jnp.maximum(m_old, mx_refs[buf][h:h + 1, :])
-            p = jnp.exp(s_refs[buf][h] - m_new)
-            alpha = jnp.exp(m_old - m_new)
-            m_ref[group, h:h + 1, :] = m_new
-            l_ref[group, h:h + 1, :] = l_ref[group, h:h + 1, :] * alpha + jnp.sum(p, axis=0, keepdims=True)
-            acc_ref[group, h] = acc_ref[group, h] * alpha + dot(vt[h * 64:(h + 1) * 64, :], p.astype(BF16))
+            first(h, s, buf)
+
+    def first(h, s, buf):
+        s_refs[buf][h] = s
+        mx_refs[buf][h:h + 1, :] = jnp.max(s, axis=0, keepdims=True)
+
+    def second(group, h, vt, buf):
+        m_old = m_ref[group, h:h + 1, :]
+        m_new = jnp.maximum(m_old, mx_refs[buf][h:h + 1, :])
+        p = jnp.exp(s_refs[buf][h] - m_new)
+        alpha = jnp.exp(m_old - m_new)
+        m_ref[group, h:h + 1, :] = m_new
+        l_ref[group, h:h + 1, :] = l_ref[group, h:h + 1, :] * alpha + jnp.sum(p, axis=0, keepdims=True)
+        acc_ref[group, h] = acc_ref[group, h] * alpha + dot(vt[h * 64:(h + 1) * 64, :], p.astype(BF16))
 
     def advance(group, j):
         wrap = j + 1 == n_chunks
@@ -157,8 +170,11 @@
         def _():
             enter(group_next)
 
-        stage1(jnp.minimum(group_next, groups - 1), j_next, 1 - buf)
-        stage2(group, j, buf)
+        made = scores(jnp.minimum(group_next, groups - 1), j_next)
+        vt = values(group, j)
+        for h in range(HEADS):
+            first(h, next(made), 1 - buf)
+            second(group, h, vt, buf)
 
         @pl.when(j_next == 0)
         def _():
@@ -213,8 +229,8 @@
         s2, refs = refs[0], refs[1:]
     scratch, (sems, near_sems, far_sems, fwd_sems) = refs[:7], refs[7:]
     rows, width = own_ref.shape
-    tiles = width // 256
     parts = far_sems.shape[1]
+    parts_half = parts // 2
     dev = lax.axis_index("sp")
     odd = lax.rem(dev, 2)
     chip1 = dev >= 2
@@ -290,50 +306,44 @@
             w_copies[0].wait()
             w_copies[2].start()
 
-        @pl.when(half == 1)
-        def _():
-            if not far_given:
-                for i in range(parts):
-                    far[i].wait_recv()
-                    fwd[i].start()
-            x_s[pl.ds(2 * rows, rows), :] = rms(s2[...], gain)
-            for cp in fwd:
-                cp.wait_recv()
-            x_s[pl.ds(3 * rows, rows), :] = rms(s3[...], gain)
-
-        def project_k(r, _):
+        def project_step(r, _):
             rows_at = tile(2 * half + r)
+            for first in range(0, parts, parts_half):
+                @pl.when((half == 1) & (r == first // parts_half))
+                def _(first=first):
+                    some = range(first, first + parts_half)
+                    if not far_given:
+                        for i in some:
+                            far[i].wait_recv()
+                            fwd[i].start()
+                    here = pl.ds(first * (rows // parts), rows // 2)
+                    x_s[pl.ds(2 * rows + 2 * first * (rows // parts), rows // 2), :] = rms(s2[here, :], gain)
+                    for i in some:
+                        fwd[i].wait_recv()
+                    x_s[pl.ds(2 * rows + 2 * first * (rows // parts) + rows // 2, rows // 2), :] = rms(s3[here, :], gain)
+
             k_s[rows_at, :] = dot(x_s[rows_at, :], w_s[0]).astype(BF16)
-            return 0
-
-        lax.fori_loop(0, 2, project_k, 0)
-
-        @pl.when(half == 0)
-        def _():
-            w_copies[1].wait()
-            w_copies[3].start()
-
-        def project_v(r, _):
-            rows_at = tile(2 * half + r)
+
+            @pl.when((half == 0) & (r == 0))
+            def _():
+                w_copies[1].wait()
+                w_copies[3].start()
+
             vt_s[:, rows_at] = dot(x_s[rows_at, :], w_s[1]).astype(BF16).T
             return 0
 
-        lax.fori_loop(0, 2, project_v, 0)
+        lax.fori_loop(0, 2, project_step, 0)
 
         @pl.when(half == 0)
         def _():
             w_copies[2].wait()
             w_copies[4].start()
 
-            def project_q(t, _):
-                qs[tile(t), :] = (dot(x_s[pl.ds(0, rows), :], w_s[2, :, tile(t)]).astype(BF16) * BF16(0.125)).T
-                return 0
-
-            lax.fori_loop(0, tiles, project_q, 0)
+            qs[...] = (dot(x_s[pl.ds(0, rows), :], w_s[2]).astype(BF16) * BF16(0.125)).T
 
         def scores(i, j):
             k = k_s[at, head_cols(i)]
-            return [dot(k[:, h // 2 * 128:(h // 2 + 1) * 128], q) + bias[half] for h, q in enumerate(head_queries(qs[head_cols(i), :]))]
+            return (dot(k[:, h // 2 * 128:(h // 2 + 1) * 128], q) + bias[half] for h, q in enumerate(head_queries(qs[head_cols(i), :])))
 
         attend_all(width // GW, 1, scores, lambda i, j: vt_s[head_cols(i), at], lambda i: None, lambda i: None, scratch)
         return 0
@@ -348,21 +358,11 @@
     a_s[...] = at_s[...].T
     w_copies[3].wait()
 
-    def project_o(t, _):
-        cols = tile(t)
-        hid_ref[:, cols] = (own_ref[:, cols].astype(F32) + dot(a_s[...], w_s[3, :, cols])).astype(BF16)
-        return 0
-
-    lax.fori_loop(0, tiles, project_o, 0)
+    hid_ref[...] = (own_ref[...].astype(F32) + dot(a_s[...], w_s[3])).astype(BF16)
     a_s[...] = rms(hid_ref[...], gc_ref[layer:layer + 1, :])
     w_copies[4].wait()
 
-    def project_cq(t, _):
-        cols = tile(t)
-        q_ref[cols, :] = (dot(a_s[...], w_s[4, :, cols]).astype(BF16) * BF16(0.125)).T
-        return 0
-
-    lax.fori_loop(0, tiles, project_cq, 0)
+    q_ref[...] = (dot(a_s[...], w_s[4]).astype(BF16) * BF16(0.125)).T
 
     @pl.when(odd == 0)
     def _():
@@ -383,7 +383,7 @@
 def self_attention(layer, own, far, gs, gc, wq, wk, wv, wo, wcq):
     rows, width = own.shape
     far_given = far is not None
-    parts = 1 if far_given else 4
+    parts = 2 if far_given else 4
     shape = jax.ShapeDtypeStruct((rows, width), BF16)
     flops = 2 * rows * width * width * 11 + 4 * rows * 4 * rows * width
     block = pltpu.VMEM((rows, width), BF16)
@@ -426,8 +426,8 @@
     hid_ref, gm_ref, wco, wg, wu, wd, out_ref = take(7)
     scratch = take(7)
     kbuf, vbuf, mask, list_s, kv_sems = take(5)
-    at_s, a_s, x_s, acc_o, wo_s, wg_s, wu_s, wd_s, o_sem, w_sems = take(10)
-    steps, ff = wg_s.shape[0], wg_s.shape[2]
+    at_s, a_s, act0, act1, acc_o, wo_s, wg_s, wu_s, wd_s, o_sem, w_sems = take(11)
+    steps, ff, down = wg_s.shape[0], wg_s.shape[2], wd_s.shape[0]
     width, rows = q_ref.shape
     groups = width // GW
 
@@ -451,7 +451,7 @@
         cols = pl.ds(pl.multiple_of(j * ff, ff), ff)
         return (pltpu.make_async_copy(wg.at[layer, :, cols], wg_s.at[j], w_sems.at[0, j]),
                 pltpu.make_async_copy(wu.at[layer, :, cols], wu_s.at[j], w_sems.at[1, j]),
-                pltpu.make_async_copy(wd.at[layer, cols, :], wd_s.at[j], w_sems.at[2, j]))
+                pltpu.make_async_copy(wd.at[layer, cols, :], wd_s.at[lax.rem(j, down)], w_sems.at[2, j]))
 
     attend_reset(scratch)
 
@@ -481,8 +481,13 @@
             o_copy.start()
 
         for j in range(2):
-            for cp in w_copies(2 * i + j):
-                cp.start()
+            gate_copy, up_copy, down_copy = w_copies(2 * i + j)
+            gate_copy.start()
+            up_copy.start()
+
+            @pl.when(2 * i + j < down)
+            def _(down_copy=down_copy):
+                down_copy.start()
 
     def leave(i):
         @pl.when(i + 2 < groups)
@@ -498,7 +503,7 @@
         k = kbuf[lax.rem(i, 2), chunk(j), :]
         ks = [jnp.concatenate([k[:, p * 128:(p + 1) * 128], mask[partial]], axis=1) for p in range(HEADS // 2)]
         queries = head_queries(q_ref[pl.ds(pl.multiple_of(i * GW, GW), GW), :], ones)
-        return [dot(ks[h // 2], q) for h, q in enumerate(queries)]
+        return (dot(ks[h // 2], q) for h, q in enumerate(queries))
 
     def values(i, j):
         return vbuf[lax.rem(i, 2), :, chunk(j)]
@@ -513,26 +518,42 @@
     a_s[...] = at_s[...].T
     o_copy.wait()
 
-    def project_o(t, _):
-        cols = pl.ds(pl.multiple_of(t * 256, 256), 256)
-        out_ref[:, cols] = (hid_ref[:, cols].astype(F32) + dot(a_s[...], wo_s[:, cols])).astype(BF16)
-        return 0
-
-    lax.fori_loop(0, width // 256, project_o, 0)
-    x_s[...] = rms(out_ref[...], gm_ref[layer:layer + 1, :])
+    out_ref[...] = (hid_ref[...].astype(F32) + dot(a_s[...], wo_s[...])).astype(BF16)
+    a_s[...] = rms(out_ref[...], gm_ref[layer:layer + 1, :])
     acc_o[...] = jnp.zeros_like(acc_o)
 
-    def mlp_step(j, _):
-        for cp in w_copies(j):
+    def wait_gate_up(j):
+        for cp in w_copies(j)[:2]:
             cp.wait()
-        x = x_s[...]
+
+    def gate_up(j, act_ref):
+        x = a_s[...]
         gate = dot(x, wg_s[j])
         up = dot(x, wu_s[j])
-        act = (gate / (1.0 + jnp.exp(-gate)) * up).astype(BF16)
-        acc_o[...] += dot(act, wd_s[j])
+        act_ref[...] = (gate / (1.0 + jnp.exp(-gate)) * up).astype(BF16)
+
+    wait_gate_up(0)
+    gate_up(0, act0)
+
+    def mlp_step(u, _):
+        for now, later, at in ((act0, act1, 0), (act1, act0, 1)):
+            j = 2 * u + at
+            w_copies(j)[2].wait()
+            following = jnp.minimum(j + 1, steps - 1)
+
+            @pl.when(j + 1 < steps)
+            def _(j=j):
+                wait_gate_up(j + 1)
+
+            acc_o[...] += dot(now[...], wd_s[lax.rem(j, down)])
+            gate_up(following, later)
+
+            @pl.when(j + down < steps)
+            def _(j=j):
+                w_copies(j + down)[2].start()
         return 0
 
-    lax.fori_loop(0, steps, mlp_step, 0)
+    lax.fori_loop(0, steps // 2, mlp_step, 0)
     out_ref[...] = (out_ref[...].astype(F32) + acc_o[...]).astype(BF16)
 
 
@@ -558,12 +579,13 @@
             pltpu.SemaphoreType.DMA((2, 2, n)),
             pltpu.VMEM((width, rows), BF16),
             pltpu.VMEM((rows, width), BF16),
-            pltpu.VMEM((rows, width), BF16),
+            pltpu.VMEM((rows, ff), BF16),
+            pltpu.VMEM((rows, ff), BF16),
             pltpu.VMEM((rows, width), F32),
             pltpu.VMEM((width, width), BF16),
             pltpu.VMEM((steps, width, ff), BF16),
             pltpu.VMEM((steps, width, ff), BF16),
-            pltpu.VMEM((steps, ff, width), BF16),
+            pltpu.VMEM((steps - 2, ff, width), BF16),
             pltpu.SemaphoreType.DMA,
             pltpu.SemaphoreType.DMA((3, steps)),
         ],

time: 265 us -> 257 us (0.970)
  Pallas kernels: 185 us -> 177 us
    pallas_call x2, Pallas kernels: 66.8 us -> 60.7 us  [self_attention(): pl.pallas_call(functools.partial(self_kernel, layer, far_given), in_specs...]
  transfers between devices with their start and end apart: 12 -> 12, of which waited for: 4 -> 4; matrix products, arithmetic and copies ran while one was open for 0% -> 0% of each run, Pallas kernels for 52% -> 51%
where the time goes in v4:
time: 257 us
  Pallas kernels  177 us (69%)
  waiting for transfers between devices  63.8 us (25%)
  starting transfers between devices  7.71 us (3%)
  local copies, waits for them, and re-layouts  6.24 us (2%)
    pallas_call x2, Pallas kernels, cross_mlp(): pl.pallas_call(functools.partial(cross_kernel, layer, planes, n), in_spec...  82.9 us
    pallas_call x2, Pallas kernels, self_attention(): pl.pallas_call(functools.partial(self_kernel, layer, far_given), in_specs...  60.7 us
    ppermute x1, waiting for transfers between devices, program(): rem_b = lax.ppermute(mem_b, 'sp', [(0, 2), (1, 3), (2, 1)])  39.5 us
    pallas_call x4, Pallas kernels, kv_project(): pl.pallas_call(functools.partial(kv_kernel, layers, len(srcs)), in_specs=...  33.8 us
    ppermute x1, waiting for transfers between devices, program(): rem_a = lax.ppermute(mem_a, 'sp', [(0, 2), (1, 3), (2, 0)])  19.7 us
  transfers between devices with their start and end apart: 12, of which 4 were waited for; matrix products, arithmetic and copies ran while one was open for 0% of the time, Pallas kernels for 51%

profile of v4, /device:TPU:7, one launch (start us, length us, event | category | flops | bytes accessed | tf_op | source)
XLA Modules:
  0.0 256.8 jit_solution(9608982715818677745)
XLA Ops:
  0.0 0.0 copy-start.5
  0.0 0.0 copy-start
  0.0 3.5 %fusion = (bf16[512,1280]{1,0:T(8,128)(2,1)}, bf16[512,1280]{1,0:T(8,128)(2,1)}) fusion(bf16[1024,1280]{1,0:T(8,128)(2,1)} %refs_0_.3), kind=kLoop, calls=%fused_computation.2 | loop fusion | bytes 5242880 | tf_op jit(solution)/shard_map/slice | solution.py:627
  3.5 1.3 collective-permute-start.1
  5.5 0.0 copy-done.5
  5.5 3.3 %collective-permute-done.1.refs_1_ = bf16[512,1280]{1,0:T(8,128)(2,1)} collective-permute-done((bf16[512,1280]{1,0:T(8,128)(2,1)}, bf16[512,1280]{1,0:T(8,128)(2,1)}, u32[]{:S(2)}, u32[]{:S(2)}) %collective-permute-start.1) | collective-permute-done | bytes 1310752 | tf_op jit(solution)/shard_map/ppermute | solution.py:628
  8.8 0.0 copy-done
  8.8 0.0 copy-start.4
  8.8 5.8 %kv_project.4 = (bf16[2,1024,1280]{2,1,0:T(8,128)(2,1)}, bf16[2,1280,1024]{2,1,0:T(8,128)(2,1)}) custom-call(s32[2]{0:T(128)S(1)} %slice_bitcast_fusion.lim_ref, s32[1]{0:T(128)} %bitcast.4.pick_ref, bf16[1024,1280]{1,0:T(8,128)(2,1)S(1)} %copy-done, bf16[512,1280]{1,0:T(8,128)(2,1)} %collective-permute-done.1.refs_1_, bf16[2,1280,1280]{2,1,0:T(8,128)(2,1)} %refs_1_.7, ...), custom_call_target="tpu_custom_call" | custom-call | flops 13421772800 | bytes 13107200 | tf_op jit(solution)/shard_map/kv_project/pallas_call | solution.py:108
  14.6 0.0 collective-permute-start.2
  14.7 0.5 collective-permute-start.7
  15.1 1.3 collective-permute-start.5
  16.4 0.0 copy-done.4
  16.4 1.3 collective-permute-start.3
  17.7 0.0 copy-done.6
  17.8 1.3 collective-permute-start
  19.1 0.6 fusion.1
  19.6 39.5 %collective-permute-done.5.refs_0_ = bf16[512,1280]{1,0:T(8,128)(2,1)S(1)} collective-permute-done((bf16[512,1280]{1,0:T(8,128)(2,1)}, bf16[512,1280]{1,0:T(8,128)(2,1)S(1)}, u32[]{:S(2)}, u32[]{:S(2)}) %collective-permute-start.5) | collective-permute-done | bytes 1310752 | tf_op jit(solution)/shard_map/ppermute | solution.py:630
  59.1 7.9 %kv_project.6 = (bf16[1,512,1280]{2,1,0:T(8,128)(2,1)S(1)}, bf16[1,1280,512]{2,1,0:T(8,128)(2,1)}) custom-call(s32[1]{0:T(128)} %bitcast.6.lim_ref, s32[1]{0:T(128)} %bitcast.4.pick_ref, bf16[512,1280]{1,0:T(8,128)(2,1)S(1)} %collective-permute-done.5.refs_0_, bf16[2,1280,1280]{2,1,0:T(8,128)(2,1)} %refs_1_.7, bf16[2,1280,1280]{2,1,0:T(8,128)(2,1)} %refs_2_.11), custom_call_target="tpu_custom_call" | custom-call | flops 3355443200 | bytes 6553600 | tf_op jit(solution)/shard_map/kv_project/pallas_call | solution.py:108
  67.1 0.0 copy-start.1
  67.1 0.5 collective-permute-start.6
  67.6 19.7 %collective-permute-done.3.refs_0_ = bf16[512,1280]{1,0:T(8,128)(2,1)S(1)} collective-permute-done((bf16[512,1280]{1,0:T(8,128)(2,1)S(1)}, bf16[512,1280]{1,0:T(8,128)(2,1)S(1)}, u32[]{:S(2)}, u32[]{:S(2)}) %collective-permute-start.3) | collective-permute-done | bytes 1310752 | tf_op jit(solution)/shard_map/ppermute | solution.py:629
  87.2 12.3 %kv_project.5 = (bf16[2,512,1280]{2,1,0:T(8,128)(2,1)}, bf16[2,1280,512]{2,1,0:T(8,128)(2,1)}) custom-call(s32[1]{0:T(128)} %bitcast.5.lim_ref, s32[1]{0:T(128)} %bitcast.4.pick_ref, bf16[512,1280]{1,0:T(8,128)(2,1)S(1)} %collective-permute-done.3.refs_0_, bf16[2,1280,1280]{2,1,0:T(8,128)(2,1)} %refs_1_.7, bf16[2,1280,1280]{2,1,0:T(8,128)(2,1)} %refs_2_.11), custom_call_target="tpu_custom_call" | custom-call | flops 6710886400 | bytes 13107200 | tf_op jit(solution)/shard_map/kv_project/pallas_call | solution.py:108
  99.5 0.0 copy-done.1
  99.5 0.5 collective-permute-start.4
  100.0 1.3 collective-permute-done.refs_1_
  101.3 0.4 collective-permute-start.8
  101.7 0.0 collective-permute-done.6.refs_5_
  101.7 1.1 copy-done.2
  102.8 0.2 collective-permute-start.9
  102.9 0.5 fusion.2.lim_ref
  103.5 0.0 copy-done.7
  103.5 31.1 %self_attention.2 = (bf16[256,1280]{1,0:T(8,128)(2,1)}, bf16[1280,256]{1,0:T(8,128)(2,1)}) custom-call(bf16[256,1280]{1,0:T(8,128)(2,1)} %refs_0_.2, bf16[256,1280]{1,0:T(8,128)(2,1)} %copy-done.7, bf16[2,1280]{1,0:T(2,128)(2,1)} %refs_1_.6, bf16[2,1280]{1,0:T(2,128)(2,1)} %refs_2_.10, bf16[2,1280,1280]{2,1,0:T(8,128)(2,1)} %refs_3_.5, ...), custom_call_target="tpu_custom_call" | custom-call | flops 10569646080 | bytes 16384000 | tf_op jit(solution)/shard_map/self_attention/pallas_call | solution.py:390
  134.6 7.8 %kv_project.7 = (bf16[1,512,1280]{2,1,0:T(8,128)(2,1)}, bf16[1,1280,512]{2,1,0:T(8,128)(2,1)}) custom-call(s32[1]{0:T(128)} %bitcast.6.lim_ref, s32[1]{0:T(128)} %bitcast.4.pick_ref, bf16[512,1280]{1,0:T(8,128)(2,1)S(1)} %collective-permute-done.5.refs_0_, bf16[2,1280,1280]{2,1,0:T(8,128)(2,1)} %refs_1_.7, bf16[2,1280,1280]{2,1,0:T(8,128)(2,1)} %refs_2_.11), custom_call_target="tpu_custom_call" | custom-call | flops 3355443200 | bytes 6553600 | tf_op jit(solution)/shard_map/kv_project/pallas_call | solution.py:108
  142.4 0.0 collective-permute-done.9.refs_11_
  142.4 0.0 collective-permute-start.10
  142.5 0.0 collective-permute-done.4.refs_3_
  142.5 0.5 collective-permute-start.11
  143.0 0.0 collective-permute-done.8.refs_9_
  143.0 0.0 collective-permute-done.2.refs_1_
  143.0 0.0 collective-permute-done.7.refs_7_
  143.0 41.4 %cross_mlp.2.refs_0_ = bf16[256,1280]{1,0:T(8,128)(2,1)} custom-call(s32[8]{0:T(128)} %fusion.2.lim_ref, bf16[1280,256]{1,0:T(8,128)(2,1)} %get-tuple-element.17.q_ref, bf16[2,1024,1280]{2,1,0:T(8,128)(2,1)} %get-tuple-element.18.refs_0_, bf16[2,1024,1280]{2,1,0:T(8,128)(2,1)} %collective-permute-done.2.refs_1_, ...), custom_call_target="tpu_custom_call" | custom-call | flops 14931722240 | bytes 42598400 | tf_op jit(solution)/shard_map/cross_mlp/pallas_call | solution.py:569
  184.4 29.6 %self_attention.3 = (bf16[256,1280]{1,0:T(8,128)(2,1)}, bf16[1280,256]{1,0:T(8,128)(2,1)}) custom-call(bf16[256,1280]{1,0:T(8,128)(2,1)} %cross_mlp.2.refs_0_, bf16[2,1280]{1,0:T(2,128)(2,1)} %refs_1_.6, bf16[2,1280]{1,0:T(2,128)(2,1)} %refs_2_.10, bf16[2,1280,1280]{2,1,0:T(8,128)(2,1)} %refs_3_.5, bf16[2,1280,1280]{2,1,0:T(8,128)(2,1)} %refs_4_.3, ...), custom_call_target="tpu_custom_call" | custom-call | flops 10569646080 | bytes 16384000 | tf_op jit(solution)/shard_map/self_attention/pallas_call | solution.py:390
  214.1 0.0 collective-permute-done.10.refs_5_
  214.1 0.0 copy-start.3
  214.1 0.0 collective-permute-done.11.refs_11_
  214.1 1.0 copy-done.3
  215.1 41.5 %cross_mlp.3 = bf16[256,1280]{1,0:T(8,128)(2,1)} custom-call(s32[8]{0:T(128)} %fusion.2.lim_ref, bf16[1280,256]{1,0:T(8,128)(2,1)} %get-tuple-element.25.q_ref, bf16[2,1024,1280]{2,1,0:T(8,128)(2,1)} %get-tuple-element.18.refs_0_, bf16[2,1024,1280]{2,1,0:T(8,128)(2,1)} %collective-permute-done.2.refs_1_, bf16[2,512,1280]{2,1,0:T(8,128)(2,1)} %get-tuple-element.19.refs_2_, ...), custom_call_target="tpu_custom_call" | custom-call | flops 14931722240 | bytes 42598400 | tf_op jit(solution)/shard_map/cross_mlp/pallas_call | solution.py:569
  (5 shorter events, 0.0 us)
Async XLA Ops:
  0.0 5.5 %copy-start.5 = (s32[4,8]{1,0:T(4,128)S(1)}, s32[4,8]{1,0:T(4,128)}, u32[]{:S(2)}) copy-start(s32[4,8]{1,0:T(4,128)} %constant.15.clone) | copy-start | bytes 388
  0.0 8.8 %copy-start = (bf16[1024,1280]{1,0:T(8,128)(2,1)S(1)}, bf16[1024,1280]{1,0:T(8,128)(2,1)}, u32[]{:S(2)}) copy-start(bf16[1024,1280]{1,0:T(8,128)(2,1)} %refs_0_.3) | copy-start | bytes 7864324
  3.5 5.3 %collective-permute-start.1 = (bf16[512,1280]{1,0:T(8,128)(2,1)}, bf16[512,1280]{1,0:T(8,128)(2,1)}, u32[]{:S(2)}, u32[]{:S(2)}) collective-permute-start(bf16[512,1280]{1,0:T(8,128)(2,1)} %get-tuple-element.30), channel_id=1, source_target_pairs={{2,3},{6,7}} | collective-permute-start | bytes 3932168 | tf_op jit(solution)/shard_map/ppermute | solution.py:628
  8.8 7.6 %copy-start.4 = (bf16[512,1280]{1,0:T(8,128)(2,1)S(1)}, bf16[512,1280]{1,0:T(8,128)(2,1)}, u32[]{:S(2)}) copy-start(bf16[512,1280]{1,0:T(8,128)(2,1)} %get-tuple-element.29) | copy-start | bytes 3932164
  8.8 9.0 %copy-start.6 = (bf16[256,1280]{1,0:T(8,128)(2,1)S(1)}, bf16[256,1280]{1,0:T(8,128)(2,1)}, u32[]{:S(2)}) copy-start(bf16[256,1280]{1,0:T(8,128)(2,1)} %refs_0_.2) | copy-start | bytes 1966084
  14.6 128.4 %collective-permute-start.2 = (bf16[2,1024,1280]{2,1,0:T(8,128)(2,1)}, bf16[2,1024,1280]{2,1,0:T(8,128)(2,1)}, u32[]{:S(2)}, u32[]{:S(2)}) collective-permute-start(bf16[2,1024,1280]{2,1,0:T(8,128)(2,1)} %get-tuple-element.18.refs_0_), channel_id=1, source_target_pairs={{0,1},{1,0},{2,3},{3,2},{4,5},{5,4},{6,7},{7,6}} | collective-permute-start | bytes 15728648 | tf_op jit(solution)/shard_map/ppermute | solution.py:623
  14.7 128.3 %collective-permute-start.7 = (bf16[2,1280,1024]{2,1,0:T(8,128)(2,1)}, bf16[2,1280,1024]{2,1,0:T(8,128)(2,1)}, u32[]{:S(2)}, u32[]{:S(2)}) collective-permute-start(bf16[2,1280,1024]{2,1,0:T(8,128)(2,1)} %get-tuple-element.21.refs_6_), channel_id=1, source_target_pairs={{0,1},{1,0},{2,3},{3,2},{4,5},{5,4},{6,7},{7,6}} | collective-permute-start | bytes 15728648 | tf_op jit(solution)/shard_map/ppermute | solution.py:623
  15.1 44.0 %collective-permute-start.5 = (bf16[512,1280]{1,0:T(8,128)(2,1)}, bf16[512,1280]{1,0:T(8,128)(2,1)S(1)}, u32[]{:S(2)}, u32[]{:S(2)}) collective-permute-start(bf16[512,1280]{1,0:T(8,128)(2,1)} %get-tuple-element.30), channel_id=1, source_target_pairs={{0,2},{1,3},{2,1},{4,6},{5,7},{6,5}} | collective-permute-start | bytes 3932168 | tf_op jit(solution)/shard_map/ppermute | solution.py:630
  16.4 70.8 %collective-permute-start.3 = (bf16[512,1280]{1,0:T(8,128)(2,1)S(1)}, bf16[512,1280]{1,0:T(8,128)(2,1)S(1)}, u32[]{:S(2)}, u32[]{:S(2)}) collective-permute-start(bf16[512,1280]{1,0:T(8,128)(2,1)S(1)} %copy-done.4), channel_id=1, source_target_pairs={{0,2},{1,3},{2,0},{4,6},{5,7},{6,4}} | collective-permute-start | bytes 3932168 | tf_op jit(solution)/shard_map/ppermute | solution.py:629
  17.8 83.5 %collective-permute-start = (bf16[256,1280]{1,0:T(8,128)(2,1)S(1)}, bf16[256,1280]{1,0:T(8,128)(2,1)S(1)}, u32[]{:S(2)}, u32[]{:S(2)}) collective-permute-start(bf16[256,1280]{1,0:T(8,128)(2,1)S(1)} %copy-done.6), channel_id=1, source_target_pairs={{0,2},{1,3},{4,6},{5,7}} | collective-permute-start | bytes 1966088 | tf_op jit(solution)/shard_map/ppermute | solution.py:626
  67.1 32.4 %copy-start.1 = (bf16[1,512,1280]{2,1,0:T(8,128)(2,1)}, bf16[1,512,1280]{2,1,0:T(8,128)(2,1)S(1)}, u32[]{:S(2)}) copy-start(bf16[1,512,1280]{2,1,0:T(8,128)(2,1)S(1)} %get-tuple-element.20.refs_4_) | copy-start | bytes 3932164
  67.1 34.6 %collective-permute-start.6 = (bf16[1,512,1280]{2,1,0:T(8,128)(2,1)S(1)}, bf16[1,512,1280]{2,1,0:T(8,128)(2,1)S(1)}, u32[]{:S(2)}, u32[]{:S(2)}) collective-permute-start(bf16[1,512,1280]{2,1,0:T(8,128)(2,1)S(1)} %get-tuple-element.20.refs_4_), channel_id=1, source_target_pairs={{0,1},{1,0},{2,3},{3,2},{4,5},{5,4},{6,7},{7,6}} | collective-permute-start | bytes 3932168 | tf_op jit(solution)/shard_map/ppermute | solution.py:623
  99.5 43.0 %collective-permute-start.4 = (bf16[2,512,1280]{2,1,0:T(8,128)(2,1)}, bf16[2,512,1280]{2,1,0:T(8,128)(2,1)}, u32[]{:S(2)}, u32[]{:S(2)}) collective-permute-start(bf16[2,512,1280]{2,1,0:T(8,128)(2,1)} %get-tuple-element.19.refs_2_), channel_id=1, source_target_pairs={{0,1},{1,0},{2,3},{3,2},{4,5},{5,4},{6,7},{7,6}} | collective-permute-start | bytes 7864328 | tf_op jit(solution)/shard_map/ppermute | solution.py:623
  101.3 2.2 copy-start.7
  101.3 41.7 %collective-permute-start.8 = (bf16[2,1280,512]{2,1,0:T(8,128)(2,1)}, bf16[2,1280,512]{2,1,0:T(8,128)(2,1)}, u32[]{:S(2)}, u32[]{:S(2)}) collective-permute-start(bf16[2,1280,512]{2,1,0:T(8,128)(2,1)} %get-tuple-element.22.refs_8_), channel_id=1, source_target_pairs={{0,1},{1,0},{2,3},{3,2},{4,5},{5,4},{6,7},{7,6}} | collective-permute-start | bytes 7864328 | tf_op jit(solution)/shard_map/ppermute | solution.py:623
  101.7 1.1 copy-start.2
  102.8 39.7 %collective-permute-start.9 = (bf16[1,1280,512]{2,1,0:T(8,128)(2,1)}, bf16[1,1280,512]{2,1,0:T(8,128)(2,1)}, u32[]{:S(2)}, u32[]{:S(2)}) collective-permute-start(bf16[1,1280,512]{2,1,0:T(8,128)(2,1)} %get-tuple-element.23.refs_10_), channel_id=1, source_target_pairs={{0,1},{1,0},{2,3},{3,2},{4,5},{5,4},{6,7},{7,6}} | collective-permute-start | bytes 3932168 | tf_op jit(solution)/shard_map/ppermute | solution.py:623
  142.4 71.6 %collective-permute-start.10 = (bf16[1,512,1280]{2,1,0:T(8,128)(2,1)}, bf16[1,512,1280]{2,1,0:T(8,128)(2,1)S(1)}, u32[]{:S(2)}, u32[]{:S(2)}) collective-permute-start(bf16[1,512,1280]{2,1,0:T(8,128)(2,1)} %get-tuple-element.26.refs_4_), channel_id=1, source_target_pairs={{0,1},{1,0},{2,3},{3,2},{4,5},{5,4},{6,7},{7,6}} | collective-permute-start | bytes 3932168 | tf_op jit(solution)/shard_map/ppermute | solution.py:623
  142.5 71.6 %collective-permute-start.11 = (bf16[1,1280,512]{2,1,0:T(8,128)(2,1)}, bf16[1,1280,512]{2,1,0:T(8,128)(2,1)}, u32[]{:S(2)}, u32[]{:S(2)}) collective-permute-start(bf16[1,1280,512]{2,1,0:T(8,128)(2,1)} %get-tuple-element.27.refs_10_), channel_id=1, source_target_pairs={{0,1},{1,0},{2,3},{3,2},{4,5},{5,4},{6,7},{7,6}} | collective-permute-start | bytes 3932168 | tf_op jit(solution)/shard_map/ppermute | solution.py:623
  214.1 1.1 copy-start.3

commit v5 on v4

--- a/solution.py
+++ b/solution.py
@@ -16,7 +16,7 @@
 HEADS = 4
 GW = HEADS * 64
 VMEM_LIMIT = 62 * 1024 * 1024
-ANY = pl.BlockSpec(memory_space=pl.ANY)
+ANY = pl.BlockSpec(memory_space=pltpu.HBM)
 SMEM = pl.BlockSpec(memory_space=pltpu.SMEM)
 VMEM = pl.BlockSpec(memory_space=pltpu.VMEM)
 
@@ -120,7 +120,7 @@
             pltpu.SemaphoreType.DMA((n, 2, rows // CH)),
         ],
         cost_estimate=pl.CostEstimate(flops=flops, bytes_accessed=n * 4 * width * cols, transcendentals=0),
-        compiler_params=pltpu.CompilerParams(vmem_limit_bytes=48 * 1024 * 1024),
+        compiler_params=pltpu.CompilerParams(vmem_limit_bytes=VMEM_LIMIT),
         name="kv_project",
     )(lims, pick, *srcs, wk, wv)
 
@@ -427,31 +427,38 @@
     scratch = take(7)
     kbuf, vbuf, mask, list_s, kv_sems = take(5)
     at_s, a_s, act0, act1, acc_o, wo_s, wg_s, wu_s, wd_s, o_sem, w_sems = take(11)
-    steps, ff, down = wg_s.shape[0], wg_s.shape[2], wd_s.shape[0]
+    ring, ff = wg_s.shape[0], wg_s.shape[2]
+    steps = wg.shape[2] // ff
     width, rows = q_ref.shape
     groups = width // GW
 
-    def kv_copies(i):
+    def kv_copies(i, go):
         slot = lax.rem(i, 2)
         cols = pl.ds(pl.multiple_of(i * GW, GW), GW)
-        out, at = [], 0
+        at = 0
         for n in range(n_kv):
-            n_rows = ks[n].shape[1]
-            out.append(pltpu.make_async_copy(ks[n].at[planes[n], :, cols], kbuf.at[slot, pl.ds(at, n_rows), :], kv_sems.at[slot, 0, n]))
-            out.append(pltpu.make_async_copy(vts[n].at[planes[n], cols, :], vbuf.at[slot, :, pl.ds(at, n_rows)], kv_sems.at[slot, 1, n]))
-            at += n_rows
-        return out
-
-    for i in range(2):
-        for cp in kv_copies(i):
-            cp.start()
+            there = pl.ds(at, ks[n].shape[1])
+            go(pltpu.make_async_copy(ks[n].at[planes[n], :, cols], kbuf.at[slot, there, :], kv_sems.at[slot, 0, n]))
+            go(pltpu.make_async_copy(vts[n].at[planes[n], cols, :], vbuf.at[slot, :, there], kv_sems.at[slot, 1, n]))
+            at += ks[n].shape[1]
+
+    def kv_start(i):
+        kv_copies(i, lambda cp: cp.start())
+
+    kv_start(0)
+    kv_start(1)
     o_copy = pltpu.make_async_copy(wco.at[layer], wo_s, o_sem)
 
     def w_copies(j):
         cols = pl.ds(pl.multiple_of(j * ff, ff), ff)
-        return (pltpu.make_async_copy(wg.at[layer, :, cols], wg_s.at[j], w_sems.at[0, j]),
-                pltpu.make_async_copy(wu.at[layer, :, cols], wu_s.at[j], w_sems.at[1, j]),
-                pltpu.make_async_copy(wd.at[layer, cols, :], wd_s.at[lax.rem(j, down)], w_sems.at[2, j]))
+        slot = lax.rem(j, ring)
+        return (pltpu.make_async_copy(wg.at[layer, :, cols], wg_s.at[slot], w_sems.at[0, slot]),
+                pltpu.make_async_copy(wu.at[layer, :, cols], wu_s.at[slot], w_sems.at[1, slot]),
+                pltpu.make_async_copy(wd.at[layer, cols, :], wd_s.at[slot], w_sems.at[2, slot]))
+
+    def w_start(j):
+        for cp in w_copies(j):
+            cp.start()
 
     attend_reset(scratch)
 
@@ -473,27 +480,20 @@
     ones = (lax.broadcasted_iota(jnp.int32, (128, rows), 0) == 0).astype(F32).astype(BF16)
 
     def enter(i):
-        for cp in kv_copies(i):
-            cp.wait()
+        kv_copies(i, lambda cp: cp.wait())
 
         @pl.when(i == 0)
         def _():
             o_copy.start()
-
-        for j in range(2):
-            gate_copy, up_copy, down_copy = w_copies(2 * i + j)
-            gate_copy.start()
-            up_copy.start()
-
-            @pl.when(2 * i + j < down)
-            def _(down_copy=down_copy):
-                down_copy.start()
+            for j in range(ring - groups):
+                w_start(j)
+
+        w_start(ring - groups + i)
 
     def leave(i):
         @pl.when(i + 2 < groups)
         def _():
-            for cp in kv_copies(i + 2):
-                cp.start()
+            kv_start(i + 2)
 
     def chunk(j):
         return pl.ds(pl.multiple_of(list_s[j] * CH, CH), CH)
@@ -528,8 +528,8 @@
 
     def gate_up(j, act_ref):
         x = a_s[...]
-        gate = dot(x, wg_s[j])
-        up = dot(x, wu_s[j])
+        gate = dot(x, wg_s[lax.rem(j, ring)])
+        up = dot(x, wu_s[lax.rem(j, ring)])
         act_ref[...] = (gate / (1.0 + jnp.exp(-gate)) * up).astype(BF16)
 
     wait_gate_up(0)
@@ -539,18 +539,17 @@
         for now, later, at in ((act0, act1, 0), (act1, act0, 1)):
             j = 2 * u + at
             w_copies(j)[2].wait()
-            following = jnp.minimum(j + 1, steps - 1)
 
             @pl.when(j + 1 < steps)
             def _(j=j):
                 wait_gate_up(j + 1)
 
-            acc_o[...] += dot(now[...], wd_s[lax.rem(j, down)])
-            gate_up(following, later)
-
-            @pl.when(j + down < steps)
+            acc_o[...] += dot(now[...], wd_s[lax.rem(j, ring)])
+            gate_up(jnp.minimum(j + 1, steps - 1), later)
+
+            @pl.when(j + ring < steps)
             def _(j=j):
-                w_copies(j + down)[2].start()
+                w_start(j + ring)
         return 0
 
     lax.fori_loop(0, steps // 2, mlp_step, 0)
@@ -564,8 +563,7 @@
     ks, vts = [k for k, _, _ in kvs], [v for _, v, _ in kvs]
     total = sum(k.shape[1] for k in ks)
     n = len(kvs)
-    steps = 2 * groups
-    ff = wg.shape[2] // steps
+    ff, ring = 512, 6
     return pl.pallas_call(
         functools.partial(cross_kernel, layer, planes, n),
         in_specs=[SMEM, VMEM] + [ANY] * (2 * n) + [VMEM] * 2 + [ANY] * 4,
@@ -583,11 +581,11 @@
             pltpu.VMEM((rows, ff), BF16),
             pltpu.VMEM((rows, width), F32),
             pltpu.VMEM((width, width), BF16),
-            pltpu.VMEM((steps, width, ff), BF16),
-            pltpu.VMEM((steps, width, ff), BF16),
-            pltpu.VMEM((steps - 2, ff, width), BF16),
+            pltpu.VMEM((ring, width, ff), BF16),
+            pltpu.VMEM((ring, width, ff), BF16),
+            pltpu.VMEM((ring, ff, width), BF16),
             pltpu.SemaphoreType.DMA,
-            pltpu.SemaphoreType.DMA((3, steps)),
+            pltpu.SemaphoreType.DMA((3, ring)),
         ],
         cost_estimate=pl.CostEstimate(
             flops=4 * rows * 3072 * width + 2 * rows * width * (width + 3 * wg.shape[2]),

time: 257 us -> 258 us (level)
    pallas_call x2, Pallas kernels: 82.9 us -> 76.3 us  [cross_mlp(): pl.pallas_call(functools.partial(cross_kernel, layer, planes, n), in_spec...]
    ppermute x1, waiting for transfers between devices: 39.5 us -> 42.9 us  [program(): rem_b = lax.ppermute(mem_b, 'sp', [(0, 2), (1, 3), (2, 1)])]
    pallas_call x4, Pallas kernels: 33.8 us -> 37.1 us  [kv_project(): pl.pallas_call(functools.partial(kv_kernel, layers, len(srcs)), in_specs=...]
  transfers between devices with their start and end apart: 12 -> 12, of which waited for: 4 -> 3; matrix products, arithmetic and copies ran while one was open for 0% -> 1% of each run, Pallas kernels for 51% -> 51%
where the time goes in v5:
time: 258 us
  Pallas kernels  177 us (69%)
  waiting for transfers between devices  63.7 us (25%)
  local copies, waits for them, and re-layouts  8.5 us (3%)
  starting transfers between devices  7.74 us (3%)
    pallas_call x2, Pallas kernels, cross_mlp(): pl.pallas_call(functools.partial(cross_kernel, layer, planes, n), in_spec...  76.3 us
    pallas_call x2, Pallas kernels, self_attention(): pl.pallas_call(functools.partial(self_kernel, layer, far_given), in_specs...  63.1 us
    ppermute x1, waiting for transfers between devices, program(): rem_b = lax.ppermute(mem_b, 'sp', [(0, 2), (1, 3), (2, 1)])  42.9 us
    pallas_call x4, Pallas kernels, kv_project(): pl.pallas_call(functools.partial(kv_kernel, layers, len(srcs)), in_specs=...  37.1 us
    ppermute x1, waiting for transfers between devices, program(): rem_a = lax.ppermute(mem_a, 'sp', [(0, 2), (1, 3), (2, 0)])  18.4 us
  transfers between devices with their start and end apart: 12, of which 3 were waited for; matrix products, arithmetic and copies ran while one was open for 1% of the time, Pallas kernels for 51%

profile of v5, /device:TPU:7, one launch (start us, length us, event | category | flops | bytes accessed | tf_op | source)
XLA Modules:
  0.0 258.0 jit_solution(13957840345064567255)
XLA Ops:
  0.0 0.0 copy-start.4
  0.0 3.0 %fusion = (bf16[512,1280]{1,0:T(8,128)(2,1)}, bf16[512,1280]{1,0:T(8,128)(2,1)S(1)}) fusion(bf16[1024,1280]{1,0:T(8,128)(2,1)} %refs_0_.3), kind=kLoop, calls=%fused_computation.2 | loop fusion | bytes 5242880 | tf_op jit(solution)/shard_map/slice | solution.py:625
  3.0 0.0 copy-start.3
  3.0 1.1 copy-done.3
  4.1 1.3 collective-permute-start.1
  6.0 0.0 copy-done.4
  6.0 0.6 slice_bitcast_fusion.lim_ref
  6.6 2.4 collective-permute-done.1.refs_1_
  9.0 0.0 copy-start.5
  9.0 1.1 copy-done.5
  10.1 0.0 copy-start.6
  10.1 6.0 %kv_project.4 = (bf16[2,1024,1280]{2,1,0:T(8,128)(2,1)}, bf16[2,1280,1024]{2,1,0:T(8,128)(2,1)}) custom-call(s32[2]{0:T(128)} %slice_bitcast_fusion.lim_ref, s32[1]{0:T(128)} %bitcast.4.pick_ref, bf16[1024,1280]{1,0:T(8,128)(2,1)} %refs_0_.3, bf16[512,1280]{1,0:T(8,128)(2,1)} %copy-done.5, bf16[2,1280,1280]{2,1,0:T(8,128)(2,1)} %refs_1_.7, ...), custom_call_target="tpu_custom_call" | custom-call | flops 13421772800 | bytes 13107200 | tf_op jit(solution)/shard_map/kv_project/pallas_call | solution.py:108
  16.1 0.6 collective-permute-start.2
  16.7 0.0 collective-permute-start.7
  16.7 1.3 collective-permute-start.5
  18.0 1.3 collective-permute-start.3
  19.3 0.0 copy-done.6
  19.3 1.3 collective-permute-start
  20.6 0.6 fusion.1
  21.2 42.9 %collective-permute-done.5.refs_0_ = bf16[512,1280]{1,0:T(8,128)(2,1)S(1)} collective-permute-done((bf16[512,1280]{1,0:T(8,128)(2,1)}, bf16[512,1280]{1,0:T(8,128)(2,1)S(1)}, u32[]{:S(2)}, u32[]{:S(2)}) %collective-permute-start.5) | collective-permute-done | bytes 1310752 | tf_op jit(solution)/shard_map/ppermute | solution.py:628
  64.2 1.1 copy-done
  65.2 8.3 %kv_project.6 = (bf16[1,512,1280]{2,1,0:T(8,128)(2,1)}, bf16[1,1280,512]{2,1,0:T(8,128)(2,1)}) custom-call(s32[1]{0:T(128)} %bitcast.6.lim_ref, s32[1]{0:T(128)} %bitcast.4.pick_ref, bf16[512,1280]{1,0:T(8,128)(2,1)} %copy-done, bf16[2,1280,1280]{2,1,0:T(8,128)(2,1)} %refs_1_.7, bf16[2,1280,1280]{2,1,0:T(8,128)(2,1)} %refs_2_.11), custom_call_target="tpu_custom_call" | custom-call | flops 3355443200 | bytes 6553600 | tf_op jit(solution)/shard_map/kv_project/pallas_call | solution.py:108
  73.5 0.5 collective-permute-start.6
  74.0 18.4 %collective-permute-done.3.refs_0_ = bf16[512,1280]{1,0:T(8,128)(2,1)} collective-permute-done((bf16[512,1280]{1,0:T(8,128)(2,1)}, bf16[512,1280]{1,0:T(8,128)(2,1)}, u32[]{:S(2)}, u32[]{:S(2)}) %collective-permute-start.3) | collective-permute-done | bytes 1310752 | tf_op jit(solution)/shard_map/ppermute | solution.py:627
  92.3 14.5 %kv_project.5 = (bf16[2,512,1280]{2,1,0:T(8,128)(2,1)}, bf16[2,1280,512]{2,1,0:T(8,128)(2,1)}) custom-call(s32[1]{0:T(128)} %bitcast.5.lim_ref, s32[1]{0:T(128)} %bitcast.4.pick_ref, bf16[512,1280]{1,0:T(8,128)(2,1)} %collective-permute-done.3.refs_0_, bf16[2,1280,1280]{2,1,0:T(8,128)(2,1)} %refs_1_.7, bf16[2,1280,1280]{2,1,0:T(8,128)(2,1)} %refs_2_.11), custom_call_target="tpu_custom_call" | custom-call | flops 6710886400 | bytes 13107200 | tf_op jit(solution)/shard_map/kv_project/pallas_call | solution.py:108
  106.9 0.5 collective-permute-start.4
  107.4 0.0 collective-permute-done.refs_1_
  107.4 0.1 collective-permute-start.8
  107.4 0.0 collective-permute-done.6.refs_5_
  107.4 0.0 copy-done.1
  107.4 0.4 collective-permute-start.9
  107.9 0.5 fusion.2.lim_ref
  108.4 33.6 %self_attention.2 = (bf16[256,1280]{1,0:T(8,128)(2,1)}, bf16[1280,256]{1,0:T(8,128)(2,1)}) custom-call(bf16[256,1280]{1,0:T(8,128)(2,1)} %refs_0_.2, bf16[256,1280]{1,0:T(8,128)(2,1)} %collective-permute-done.refs_1_, bf16[2,1280]{1,0:T(2,128)(2,1)} %refs_1_.6, bf16[2,1280]{1,0:T(2,128)(2,1)} %refs_2_.10, bf16[2,1280,1280]{2,1,0:T(8,128)(2,1)} %refs_3_.5, ...), custom_call_target="tpu_custom_call" | custom-call | flops 10569646080 | bytes 16384000 | tf_op jit(solution)/shard_map/self_attention/pallas_call | solution.py:390
  142.0 8.3 %kv_project.7 = (bf16[1,512,1280]{2,1,0:T(8,128)(2,1)}, bf16[1,1280,512]{2,1,0:T(8,128)(2,1)}) custom-call(s32[1]{0:T(128)} %bitcast.6.lim_ref, s32[1]{0:T(128)} %bitcast.4.pick_ref, bf16[512,1280]{1,0:T(8,128)(2,1)} %copy-done, bf16[2,1280,1280]{2,1,0:T(8,128)(2,1)} %refs_1_.7, bf16[2,1280,1280]{2,1,0:T(8,128)(2,1)} %refs_2_.11), custom_call_target="tpu_custom_call" | custom-call | flops 3355443200 | bytes 6553600 | tf_op jit(solution)/shard_map/kv_project/pallas_call | solution.py:108
  150.3 0.0 collective-permute-done.9.refs_11_
  150.3 0.0 collective-permute-start.10
  150.3 0.0 collective-permute-done.4.refs_3_
  150.3 0.5 collective-permute-start.11
  150.8 0.0 collective-permute-done.8.refs_9_
  150.8 0.0 collective-permute-done.2.refs_1_
  150.8 0.0 collective-permute-done.7.refs_7_
  150.8 38.0 %cross_mlp.2.refs_0_ = bf16[256,1280]{1,0:T(8,128)(2,1)} custom-call(s32[8]{0:T(128)} %fusion.2.lim_ref, bf16[1280,256]{1,0:T(8,128)(2,1)} %get-tuple-element.17.q_ref, bf16[2,1024,1280]{2,1,0:T(8,128)(2,1)} %get-tuple-element.18.refs_0_, bf16[2,1024,1280]{2,1,0:T(8,128)(2,1)} %collective-permute-done.2.refs_1_, ...), custom_call_target="tpu_custom_call" | custom-call | flops 14931722240 | bytes 42598400 | tf_op jit(solution)/shard_map/cross_mlp/pallas_call | solution.py:567
  188.8 29.6 %self_attention.3 = (bf16[256,1280]{1,0:T(8,128)(2,1)}, bf16[1280,256]{1,0:T(8,128)(2,1)}) custom-call(bf16[256,1280]{1,0:T(8,128)(2,1)} %cross_mlp.2.refs_0_, bf16[2,1280]{1,0:T(2,128)(2,1)} %refs_1_.6, bf16[2,1280]{1,0:T(2,128)(2,1)} %refs_2_.10, bf16[2,1280,1280]{2,1,0:T(8,128)(2,1)} %refs_3_.5, bf16[2,1280,1280]{2,1,0:T(8,128)(2,1)} %refs_4_.3, ...), custom_call_target="tpu_custom_call" | custom-call | flops 10569646080 | bytes 16384000 | tf_op jit(solution)/shard_map/self_attention/pallas_call | solution.py:390
  218.4 0.0 collective-permute-done.10.refs_5_
  218.4 0.0 copy-start.2
  218.4 0.0 collective-permute-done.11.refs_11_
  218.5 1.1 copy-done.2
  219.5 38.3 %cross_mlp.3 = bf16[256,1280]{1,0:T(8,128)(2,1)} custom-call(s32[8]{0:T(128)} %fusion.2.lim_ref, bf16[1280,256]{1,0:T(8,128)(2,1)} %get-tuple-element.25.q_ref, bf16[2,1024,1280]{2,1,0:T(8,128)(2,1)} %get-tuple-element.18.refs_0_, bf16[2,1024,1280]{2,1,0:T(8,128)(2,1)} %collective-permute-done.2.refs_1_, bf16[2,512,1280]{2,1,0:T(8,128)(2,1)} %get-tuple-element.19.refs_2_, ...), custom_call_target="tpu_custom_call" | custom-call | flops 14931722240 | bytes 42598400 | tf_op jit(solution)/shard_map/cross_mlp/pallas_call | solution.py:567
  (3 shorter events, 0.0 us)
Async XLA Ops:
  0.0 6.0 %copy-start.4 = (s32[4,8]{1,0:T(4,128)S(1)}, s32[4,8]{1,0:T(4,128)}, u32[]{:S(2)}) copy-start(s32[4,8]{1,0:T(4,128)} %constant.15.clone) | copy-start | bytes 388
  3.0 1.1 copy-start.3
  4.1 4.9 %collective-permute-start.1 = (bf16[512,1280]{1,0:T(8,128)(2,1)S(1)}, bf16[512,1280]{1,0:T(8,128)(2,1)S(1)}, u32[]{:S(2)}, u32[]{:S(2)}) collective-permute-start(bf16[512,1280]{1,0:T(8,128)(2,1)S(1)} %get-tuple-element.30), channel_id=1, source_target_pairs={{2,3},{6,7}} | collective-permute-start | bytes 3932168 | tf_op jit(solution)/shard_map/ppermute | solution.py:626
  9.0 1.1 copy-start.5
  10.1 9.3 %copy-start.6 = (bf16[256,1280]{1,0:T(8,128)(2,1)S(1)}, bf16[256,1280]{1,0:T(8,128)(2,1)}, u32[]{:S(2)}) copy-start(bf16[256,1280]{1,0:T(8,128)(2,1)} %refs_0_.2) | copy-start | bytes 1966084
  16.1 134.7 %collective-permute-start.2 = (bf16[2,1024,1280]{2,1,0:T(8,128)(2,1)}, bf16[2,1024,1280]{2,1,0:T(8,128)(2,1)}, u32[]{:S(2)}, u32[]{:S(2)}) collective-permute-start(bf16[2,1024,1280]{2,1,0:T(8,128)(2,1)} %get-tuple-element.18.refs_0_), channel_id=1, source_target_pairs={{0,1},{1,0},{2,3},{3,2},{4,5},{5,4},{6,7},{7,6}} | collective-permute-start | bytes 15728648 | tf_op jit(solution)/shard_map/ppermute | solution.py:621
  16.7 134.1 %collective-permute-start.7 = (bf16[2,1280,1024]{2,1,0:T(8,128)(2,1)}, bf16[2,1280,1024]{2,1,0:T(8,128)(2,1)}, u32[]{:S(2)}, u32[]{:S(2)}) collective-permute-start(bf16[2,1280,1024]{2,1,0:T(8,128)(2,1)} %get-tuple-element.21.refs_6_), channel_id=1, source_target_pairs={{0,1},{1,0},{2,3},{3,2},{4,5},{5,4},{6,7},{7,6}} | collective-permute-start | bytes 15728648 | tf_op jit(solution)/shard_map/ppermute | solution.py:621
  16.7 47.4 %collective-permute-start.5 = (bf16[512,1280]{1,0:T(8,128)(2,1)}, bf16[512,1280]{1,0:T(8,128)(2,1)S(1)}, u32[]{:S(2)}, u32[]{:S(2)}) collective-permute-start(bf16[512,1280]{1,0:T(8,128)(2,1)} %copy-done.3), channel_id=1, source_target_pairs={{0,2},{1,3},{2,1},{4,6},{5,7},{6,5}} | collective-permute-start | bytes 3932168 | tf_op jit(solution)/shard_map/ppermute | solution.py:628
  18.0 74.3 %collective-permute-start.3 = (bf16[512,1280]{1,0:T(8,128)(2,1)}, bf16[512,1280]{1,0:T(8,128)(2,1)}, u32[]{:S(2)}, u32[]{:S(2)}) collective-permute-start(bf16[512,1280]{1,0:T(8,128)(2,1)} %get-tuple-element.29), channel_id=1, source_target_pairs={{0,2},{1,3},{2,0},{4,6},{5,7},{6,4}} | collective-permute-start | bytes 3932168 | tf_op jit(solution)/shard_map/ppermute | solution.py:627
  19.3 88.1 %collective-permute-start = (bf16[256,1280]{1,0:T(8,128)(2,1)S(1)}, bf16[256,1280]{1,0:T(8,128)(2,1)}, u32[]{:S(2)}, u32[]{:S(2)}) collective-permute-start(bf16[256,1280]{1,0:T(8,128)(2,1)S(1)} %copy-done.6), channel_id=1, source_target_pairs={{0,2},{1,3},{4,6},{5,7}} | collective-permute-start | bytes 1966088 | tf_op jit(solution)/shard_map/ppermute | solution.py:624
  64.2 1.1 copy-start
  73.5 33.9 %collective-permute-start.6 = (bf16[1,512,1280]{2,1,0:T(8,128)(2,1)}, bf16[1,512,1280]{2,1,0:T(8,128)(2,1)}, u32[]{:S(2)}, u32[]{:S(2)}) collective-permute-start(bf16[1,512,1280]{2,1,0:T(8,128)(2,1)} %get-tuple-element.20.refs_4_), channel_id=1, source_target_pairs={{0,1},{1,0},{2,3},{3,2},{4,5},{5,4},{6,7},{7,6}} | collective-permute-start | bytes 3932168 | tf_op jit(solution)/shard_map/ppermute | solution.py:621
  92.3 15.1 %copy-start.1 = (bf16[1,1280,512]{2,1,0:T(8,128)(2,1)S(1)}, bf16[1,1280,512]{2,1,0:T(8,128)(2,1)}, u32[]{:S(2)}) copy-start(bf16[1,1280,512]{2,1,0:T(8,128)(2,1)} %get-tuple-element.23.refs_10_) | copy-start | bytes 3932164
  106.9 43.4 %collective-permute-start.4 = (bf16[2,512,1280]{2,1,0:T(8,128)(2,1)}, bf16[2,512,1280]{2,1,0:T(8,128)(2,1)}, u32[]{:S(2)}, u32[]{:S(2)}) collective-permute-start(bf16[2,512,1280]{2,1,0:T(8,128)(2,1)} %get-tuple-element.19.refs_2_), channel_id=1, source_target_pairs={{0,1},{1,0},{2,3},{3,2},{4,5},{5,4},{6,7},{7,6}} | collective-permute-start | bytes 7864328 | tf_op jit(solution)/shard_map/ppermute | solution.py:621
  107.4 43.4 %collective-permute-start.8 = (bf16[2,1280,512]{2,1,0:T(8,128)(2,1)}, bf16[2,1280,512]{2,1,0:T(8,128)(2,1)}, u32[]{:S(2)}, u32[]{:S(2)}) collective-permute-start(bf16[2,1280,512]{2,1,0:T(8,128)(2,1)} %get-tuple-element.22.refs_8_), channel_id=1, source_target_pairs={{0,1},{1,0},{2,3},{3,2},{4,5},{5,4},{6,7},{7,6}} | collective-permute-start | bytes 7864328 | tf_op jit(solution)/shard_map/ppermute | solution.py:621
  107.4 42.8 %collective-permute-start.9 = (bf16[1,1280,512]{2,1,0:T(8,128)(2,1)S(1)}, bf16[1,1280,512]{2,1,0:T(8,128)(2,1)}, u32[]{:S(2)}, u32[]{:S(2)}) collective-permute-start(bf16[1,1280,512]{2,1,0:T(8,128)(2,1)S(1)} %copy-done.1), channel_id=1, source_target_pairs={{0,1},{1,0},{2,3},{3,2},{4,5},{5,4},{6,7},{7,6}} | collective-permute-start | bytes 3932168 | tf_op jit(solution)/shard_map/ppermute | solution.py:621
  150.3 68.2 %collective-permute-start.10 = (bf16[1,512,1280]{2,1,0:T(8,128)(2,1)}, bf16[1,512,1280]{2,1,0:T(8,128)(2,1)S(1)}, u32[]{:S(2)}, u32[]{:S(2)}) collective-permute-start(bf16[1,512,1280]{2,1,0:T(8,128)(2,1)} %get-tuple-element.26.refs_4_), channel_id=1, source_target_pairs={{0,1},{1,0},{2,3},{3,2},{4,5},{5,4},{6,7},{7,6}} | collective-permute-start | bytes 3932168 | tf_op jit(solution)/shard_map/ppermute | solution.py:621
  150.3 68.1 %collective-permute-start.11 = (bf16[1,1280,512]{2,1,0:T(8,128)(2,1)}, bf16[1,1280,512]{2,1,0:T(8,128)(2,1)}, u32[]{:S(2)}, u32[]{:S(2)}) collective-permute-start(bf16[1,1280,512]{2,1,0:T(8,128)(2,1)} %get-tuple-element.27.refs_10_), channel_id=1, source_target_pairs={{0,1},{1,0},{2,3},{3,2},{4,5},{5,4},{6,7},{7,6}} | collective-permute-start | bytes 3932168 | tf_op jit(solution)/shard_map/ppermute | solution.py:621
  218.4 1.1 copy-start.2

commit v6 on v5

--- a/solution.py
+++ b/solution.py
@@ -15,6 +15,7 @@
 CH = 512
 HEADS = 4
 GW = HEADS * 64
+ORDER = (("F", 0), ("F", 1), ("S", 0), ("S", 1), ("F", 2), ("F", 3), ("S", 2), ("S", 3))
 VMEM_LIMIT = 62 * 1024 * 1024
 ANY = pl.BlockSpec(memory_space=pltpu.HBM)
 SMEM = pl.BlockSpec(memory_space=pltpu.SMEM)
@@ -53,11 +54,8 @@
 
     w_copy(0, 0).start()
     from_src(lambda cp: cp.start())
-    for i in range(n):
-        for v in range(2):
-            if i + v > 0:
-                w_copy(i, v).start()
     from_src(lambda cp: cp.wait())
+    w_copy(0, 1).start()
 
     def out_copy(i, v, c):
         at = pl.ds(pl.multiple_of(c * CH, CH), CH)
@@ -73,6 +71,10 @@
     def layer_step(i, _):
         for v in range(2):
             w_copy(i, v).wait()
+
+            @pl.when(i + 1 < n)
+            def _(v=v):
+                w_copy(i + 1, v).start()
 
             def chunk_step(c, _):
                 def work():
@@ -172,9 +174,11 @@
 
         made = scores(jnp.minimum(group_next, groups - 1), j_next)
         vt = values(group, j)
-        for h in range(HEADS):
-            first(h, next(made), 1 - buf)
-            second(group, h, vt, buf)
+        for what, h in ORDER:
+            if what == "F":
+                first(h, next(made), 1 - buf)
+            else:
+                second(group, h, vt, buf)
 
         @pl.when(j_next == 0)
         def _():
@@ -536,17 +540,21 @@
     gate_up(0, act0)
 
     def mlp_step(u, _):
-        for now, later, at in ((act0, act1, 0), (act1, act0, 1)):
-            j = 2 * u + at
-            w_copies(j)[2].wait()
-
-            @pl.when(j + 1 < steps)
-            def _(j=j):
-                wait_gate_up(j + 1)
-
-            acc_o[...] += dot(now[...], wd_s[lax.rem(j, ring)])
-            gate_up(jnp.minimum(j + 1, steps - 1), later)
-
+        first = 2 * u
+        w_copies(first)[2].wait()
+        wait_gate_up(first + 1)
+        w_copies(first + 1)[2].wait()
+
+        @pl.when(first + 2 < steps)
+        def _():
+            wait_gate_up(first + 2)
+
+        acc_o[...] += dot(act0[...], wd_s[lax.rem(first, ring)])
+        gate_up(first + 1, act1)
+        acc_o[...] += dot(act1[...], wd_s[lax.rem(first + 1, ring)])
+        gate_up(jnp.minimum(first + 2, steps - 1), act0)
+
+        for j in (first, first + 1):
             @pl.when(j + ring < steps)
             def _(j=j):
                 w_start(j + ring)

time: 258 us -> 254 us (0.984)
  waiting for transfers between devices: 63.7 us -> 60.5 us
    ppermute x1, waiting for transfers between devices: 42.9 us -> 38.9 us  [program(): rem_b = lax.ppermute(mem_b, 'sp', [(0, 2), (1, 3), (2, 1)])]
  transfers between devices with their start and end apart: 12 -> 12, of which waited for: 3 -> 4; matrix products, arithmetic and copies ran while one was open for 1% -> 1% of each run, Pallas kernels for 51% -> 51%
where the time goes in v6:
time: 254 us
  Pallas kernels  175 us (69%)
  waiting for transfers between devices  60.5 us (24%)
  local copies, waits for them, and re-layouts  8.5 us (3%)
  starting transfers between devices  7.76 us (3%)
    pallas_call x2, Pallas kernels, cross_mlp(): pl.pallas_call(functools.partial(cross_kernel, layer, planes, n), in_spec...  76 us
    pallas_call x2, Pallas kernels, self_attention(): pl.pallas_call(functools.partial(self_kernel, layer, far_given), in_specs...  62.8 us
    ppermute x1, waiting for transfers between devices, program(): rem_b = lax.ppermute(mem_b, 'sp', [(0, 2), (1, 3), (2, 1)])  38.9 us
    pallas_call x4, Pallas kernels, kv_project(): pl.pallas_call(functools.partial(kv_kernel, layers, len(srcs)), in_specs=...  36.5 us
    ppermute x1, waiting for transfers between devices, program(): rem_a = lax.ppermute(mem_a, 'sp', [(0, 2), (1, 3), (2, 0)])  18.4 us
  transfers between devices with their start and end apart: 12, of which 4 were waited for; matrix products, arithmetic and copies ran while one was open for 1% of the time, Pallas kernels for 51%

profile of v6, /device:TPU:7, one launch (start us, length us, event | category | flops | bytes accessed | tf_op | source)
XLA Modules:
  0.0 253.6 jit_solution(13045729625301734142)
XLA Ops:
  0.0 0.0 copy-start.4
  0.0 3.0 %fusion = (bf16[512,1280]{1,0:T(8,128)(2,1)}, bf16[512,1280]{1,0:T(8,128)(2,1)S(1)}) fusion(bf16[1024,1280]{1,0:T(8,128)(2,1)} %refs_0_.3), kind=kLoop, calls=%fused_computation.2 | loop fusion | bytes 5242880 | tf_op jit(solution)/shard_map/slice | solution.py:633
  3.0 0.0 copy-start.3
  3.0 1.1 copy-done.3
  4.1 1.3 collective-permute-start.1
  6.0 0.0 copy-done.4
  6.0 0.6 slice_bitcast_fusion.lim_ref
  6.6 2.4 collective-permute-done.1.refs_1_
  9.0 0.0 copy-start.5
  9.0 1.1 copy-done.5
  10.1 0.0 copy-start.6
  10.1 7.3 %kv_project.4 = (bf16[2,1024,1280]{2,1,0:T(8,128)(2,1)}, bf16[2,1280,1024]{2,1,0:T(8,128)(2,1)}) custom-call(s32[2]{0:T(128)} %slice_bitcast_fusion.lim_ref, s32[1]{0:T(128)} %bitcast.4.pick_ref, bf16[1024,1280]{1,0:T(8,128)(2,1)} %refs_0_.3, bf16[512,1280]{1,0:T(8,128)(2,1)} %copy-done.5, bf16[2,1280,1280]{2,1,0:T(8,128)(2,1)} %refs_1_.7, ...), custom_call_target="tpu_custom_call" | custom-call | flops 13421772800 | bytes 13107200 | tf_op jit(solution)/shard_map/kv_project/pallas_call | solution.py:110
  17.4 0.6 collective-permute-start.2
  17.9 0.0 collective-permute-start.7
  18.0 1.3 collective-permute-start.5
  19.3 1.3 collective-permute-start.3
  20.6 0.0 copy-done.6
  20.6 1.3 collective-permute-start
  21.9 0.6 fusion.1
  22.5 38.9 %collective-permute-done.5.refs_0_ = bf16[512,1280]{1,0:T(8,128)(2,1)S(1)} collective-permute-done((bf16[512,1280]{1,0:T(8,128)(2,1)}, bf16[512,1280]{1,0:T(8,128)(2,1)S(1)}, u32[]{:S(2)}, u32[]{:S(2)}) %collective-permute-start.5) | collective-permute-done | bytes 1310752 | tf_op jit(solution)/shard_map/ppermute | solution.py:636
  61.4 1.1 copy-done
  62.4 8.3 %kv_project.6 = (bf16[1,512,1280]{2,1,0:T(8,128)(2,1)}, bf16[1,1280,512]{2,1,0:T(8,128)(2,1)}) custom-call(s32[1]{0:T(128)} %bitcast.6.lim_ref, s32[1]{0:T(128)} %bitcast.4.pick_ref, bf16[512,1280]{1,0:T(8,128)(2,1)} %copy-done, bf16[2,1280,1280]{2,1,0:T(8,128)(2,1)} %refs_1_.7, bf16[2,1280,1280]{2,1,0:T(8,128)(2,1)} %refs_2_.11), custom_call_target="tpu_custom_call" | custom-call | flops 3355443200 | bytes 6553600 | tf_op jit(solution)/shard_map/kv_project/pallas_call | solution.py:110
  70.7 0.5 collective-permute-start.6
  71.2 18.4 %collective-permute-done.3.refs_0_ = bf16[512,1280]{1,0:T(8,128)(2,1)} collective-permute-done((bf16[512,1280]{1,0:T(8,128)(2,1)}, bf16[512,1280]{1,0:T(8,128)(2,1)}, u32[]{:S(2)}, u32[]{:S(2)}) %collective-permute-start.3) | collective-permute-done | bytes 1310752 | tf_op jit(solution)/shard_map/ppermute | solution.py:635
  89.5 12.7 %kv_project.5 = (bf16[2,512,1280]{2,1,0:T(8,128)(2,1)}, bf16[2,1280,512]{2,1,0:T(8,128)(2,1)}) custom-call(s32[1]{0:T(128)} %bitcast.5.lim_ref, s32[1]{0:T(128)} %bitcast.4.pick_ref, bf16[512,1280]{1,0:T(8,128)(2,1)} %collective-permute-done.3.refs_0_, bf16[2,1280,1280]{2,1,0:T(8,128)(2,1)} %refs_1_.7, bf16[2,1280,1280]{2,1,0:T(8,128)(2,1)} %refs_2_.11), custom_call_target="tpu_custom_call" | custom-call | flops 6710886400 | bytes 13107200 | tf_op jit(solution)/shard_map/kv_project/pallas_call | solution.py:110
  102.2 0.5 collective-permute-start.4
  102.7 0.9 collective-permute-done.refs_1_
  103.6 0.4 collective-permute-start.8
  104.0 0.0 collective-permute-done.6.refs_5_
  104.0 0.0 copy-done.1
  104.0 0.1 collective-permute-start.9
  104.1 0.5 fusion.2.lim_ref
  104.6 33.0 %self_attention.2 = (bf16[256,1280]{1,0:T(8,128)(2,1)}, bf16[1280,256]{1,0:T(8,128)(2,1)}) custom-call(bf16[256,1280]{1,0:T(8,128)(2,1)} %refs_0_.2, bf16[256,1280]{1,0:T(8,128)(2,1)} %collective-permute-done.refs_1_, bf16[2,1280]{1,0:T(2,128)(2,1)} %refs_1_.6, bf16[2,1280]{1,0:T(2,128)(2,1)} %refs_2_.10, bf16[2,1280,1280]{2,1,0:T(8,128)(2,1)} %refs_3_.5, ...), custom_call_target="tpu_custom_call" | custom-call | flops 10569646080 | bytes 16384000 | tf_op jit(solution)/shard_map/self_attention/pallas_call | solution.py:394
  137.7 8.3 %kv_project.7 = (bf16[1,512,1280]{2,1,0:T(8,128)(2,1)}, bf16[1,1280,512]{2,1,0:T(8,128)(2,1)}) custom-call(s32[1]{0:T(128)} %bitcast.6.lim_ref, s32[1]{0:T(128)} %bitcast.4.pick_ref, bf16[512,1280]{1,0:T(8,128)(2,1)} %copy-done, bf16[2,1280,1280]{2,1,0:T(8,128)(2,1)} %refs_1_.7, bf16[2,1280,1280]{2,1,0:T(8,128)(2,1)} %refs_2_.11), custom_call_target="tpu_custom_call" | custom-call | flops 3355443200 | bytes 6553600 | tf_op jit(solution)/shard_map/kv_project/pallas_call | solution.py:110
  145.9 0.0 collective-permute-done.9.refs_11_
  146.0 0.0 collective-permute-start.10
  146.0 0.0 collective-permute-done.4.refs_3_
  146.0 0.5 collective-permute-start.11
  146.5 0.0 collective-permute-done.8.refs_9_
  146.5 0.0 collective-permute-done.2.refs_1_
  146.5 0.0 collective-permute-done.7.refs_7_
  146.5 37.9 %cross_mlp.2.refs_0_ = bf16[256,1280]{1,0:T(8,128)(2,1)} custom-call(s32[8]{0:T(128)} %fusion.2.lim_ref, bf16[1280,256]{1,0:T(8,128)(2,1)} %get-tuple-element.17.q_ref, bf16[2,1024,1280]{2,1,0:T(8,128)(2,1)} %get-tuple-element.18.refs_0_, bf16[2,1024,1280]{2,1,0:T(8,128)(2,1)} %collective-permute-done.2.refs_1_, ...), custom_call_target="tpu_custom_call" | custom-call | flops 14931722240 | bytes 42598400 | tf_op jit(solution)/shard_map/cross_mlp/pallas_call | solution.py:575
  184.4 29.8 %self_attention.3 = (bf16[256,1280]{1,0:T(8,128)(2,1)}, bf16[1280,256]{1,0:T(8,128)(2,1)}) custom-call(bf16[256,1280]{1,0:T(8,128)(2,1)} %cross_mlp.2.refs_0_, bf16[2,1280]{1,0:T(2,128)(2,1)} %refs_1_.6, bf16[2,1280]{1,0:T(2,128)(2,1)} %refs_2_.10, bf16[2,1280,1280]{2,1,0:T(8,128)(2,1)} %refs_3_.5, bf16[2,1280,1280]{2,1,0:T(8,128)(2,1)} %refs_4_.3, ...), custom_call_target="tpu_custom_call" | custom-call | flops 10569646080 | bytes 16384000 | tf_op jit(solution)/shard_map/self_attention/pallas_call | solution.py:394
  214.2 0.0 collective-permute-done.10.refs_5_
  214.2 0.0 copy-start.2
  214.2 0.0 collective-permute-done.11.refs_11_
  214.2 1.1 copy-done.2
  215.3 38.1 %cross_mlp.3 = bf16[256,1280]{1,0:T(8,128)(2,1)} custom-call(s32[8]{0:T(128)} %fusion.2.lim_ref, bf16[1280,256]{1,0:T(8,128)(2,1)} %get-tuple-element.25.q_ref, bf16[2,1024,1280]{2,1,0:T(8,128)(2,1)} %get-tuple-element.18.refs_0_, bf16[2,1024,1280]{2,1,0:T(8,128)(2,1)} %collective-permute-done.2.refs_1_, bf16[2,512,1280]{2,1,0:T(8,128)(2,1)} %get-tuple-element.19.refs_2_, ...), custom_call_target="tpu_custom_call" | custom-call | flops 14931722240 | bytes 42598400 | tf_op jit(solution)/shard_map/cross_mlp/pallas_call | solution.py:575
  (3 shorter events, 0.0 us)
Async XLA Ops:
  0.0 6.0 %copy-start.4 = (s32[4,8]{1,0:T(4,128)S(1)}, s32[4,8]{1,0:T(4,128)}, u32[]{:S(2)}) copy-start(s32[4,8]{1,0:T(4,128)} %constant.15.clone) | copy-start | bytes 388
  3.0 1.1 copy-start.3
  4.1 4.9 %collective-permute-start.1 = (bf16[512,1280]{1,0:T(8,128)(2,1)S(1)}, bf16[512,1280]{1,0:T(8,128)(2,1)S(1)}, u32[]{:S(2)}, u32[]{:S(2)}) collective-permute-start(bf16[512,1280]{1,0:T(8,128)(2,1)S(1)} %get-tuple-element.30), channel_id=1, source_target_pairs={{2,3},{6,7}} | collective-permute-start | bytes 3932168 | tf_op jit(solution)/shard_map/ppermute | solution.py:634
  9.0 1.1 copy-start.5
  10.1 10.5 %copy-start.6 = (bf16[256,1280]{1,0:T(8,128)(2,1)S(1)}, bf16[256,1280]{1,0:T(8,128)(2,1)}, u32[]{:S(2)}) copy-start(bf16[256,1280]{1,0:T(8,128)(2,1)} %refs_0_.2) | copy-start | bytes 1966084
  17.4 129.1 %collective-permute-start.2 = (bf16[2,1024,1280]{2,1,0:T(8,128)(2,1)}, bf16[2,1024,1280]{2,1,0:T(8,128)(2,1)}, u32[]{:S(2)}, u32[]{:S(2)}) collective-permute-start(bf16[2,1024,1280]{2,1,0:T(8,128)(2,1)} %get-tuple-element.18.refs_0_), channel_id=1, source_target_pairs={{0,1},{1,0},{2,3},{3,2},{4,5},{5,4},{6,7},{7,6}} | collective-permute-start | bytes 15728648 | tf_op jit(solution)/shard_map/ppermute | solution.py:629
  17.9 128.6 %collective-permute-start.7 = (bf16[2,1280,1024]{2,1,0:T(8,128)(2,1)}, bf16[2,1280,1024]{2,1,0:T(8,128)(2,1)}, u32[]{:S(2)}, u32[]{:S(2)}) collective-permute-start(bf16[2,1280,1024]{2,1,0:T(8,128)(2,1)} %get-tuple-element.21.refs_6_), channel_id=1, source_target_pairs={{0,1},{1,0},{2,3},{3,2},{4,5},{5,4},{6,7},{7,6}} | collective-permute-start | bytes 15728648 | tf_op jit(solution)/shard_map/ppermute | solution.py:629
  18.0 43.4 %collective-permute-start.5 = (bf16[512,1280]{1,0:T(8,128)(2,1)}, bf16[512,1280]{1,0:T(8,128)(2,1)S(1)}, u32[]{:S(2)}, u32[]{:S(2)}) collective-permute-start(bf16[512,1280]{1,0:T(8,128)(2,1)} %copy-done.3), channel_id=1, source_target_pairs={{0,2},{1,3},{2,1},{4,6},{5,7},{6,5}} | collective-permute-start | bytes 3932168 | tf_op jit(solution)/shard_map/ppermute | solution.py:636
  19.3 70.3 %collective-permute-start.3 = (bf16[512,1280]{1,0:T(8,128)(2,1)}, bf16[512,1280]{1,0:T(8,128)(2,1)}, u32[]{:S(2)}, u32[]{:S(2)}) collective-permute-start(bf16[512,1280]{1,0:T(8,128)(2,1)} %get-tuple-element.29), channel_id=1, source_target_pairs={{0,2},{1,3},{2,0},{4,6},{5,7},{6,4}} | collective-permute-start | bytes 3932168 | tf_op jit(solution)/shard_map/ppermute | solution.py:635
  20.6 83.0 %collective-permute-start = (bf16[256,1280]{1,0:T(8,128)(2,1)S(1)}, bf16[256,1280]{1,0:T(8,128)(2,1)}, u32[]{:S(2)}, u32[]{:S(2)}) collective-permute-start(bf16[256,1280]{1,0:T(8,128)(2,1)S(1)} %copy-done.6), channel_id=1, source_target_pairs={{0,2},{1,3},{4,6},{5,7}} | collective-permute-start | bytes 1966088 | tf_op jit(solution)/shard_map/ppermute | solution.py:632
  61.3 1.1 copy-start
  70.7 33.3 %collective-permute-start.6 = (bf16[1,512,1280]{2,1,0:T(8,128)(2,1)}, bf16[1,512,1280]{2,1,0:T(8,128)(2,1)}, u32[]{:S(2)}, u32[]{:S(2)}) collective-permute-start(bf16[1,512,1280]{2,1,0:T(8,128)(2,1)} %get-tuple-element.20.refs_4_), channel_id=1, source_target_pairs={{0,1},{1,0},{2,3},{3,2},{4,5},{5,4},{6,7},{7,6}} | collective-permute-start | bytes 3932168 | tf_op jit(solution)/shard_map/ppermute | solution.py:629
  89.5 14.5 %copy-start.1 = (bf16[1,1280,512]{2,1,0:T(8,128)(2,1)S(1)}, bf16[1,1280,512]{2,1,0:T(8,128)(2,1)}, u32[]{:S(2)}) copy-start(bf16[1,1280,512]{2,1,0:T(8,128)(2,1)} %get-tuple-element.23.refs_10_) | copy-start | bytes 3932164
  102.2 43.8 %collective-permute-start.4 = (bf16[2,512,1280]{2,1,0:T(8,128)(2,1)}, bf16[2,512,1280]{2,1,0:T(8,128)(2,1)}, u32[]{:S(2)}, u32[]{:S(2)}) collective-permute-start(bf16[2,512,1280]{2,1,0:T(8,128)(2,1)} %get-tuple-element.19.refs_2_), channel_id=1, source_target_pairs={{0,1},{1,0},{2,3},{3,2},{4,5},{5,4},{6,7},{7,6}} | collective-permute-start | bytes 7864328 | tf_op jit(solution)/shard_map/ppermute | solution.py:629
  103.6 42.9 %collective-permute-start.8 = (bf16[2,1280,512]{2,1,0:T(8,128)(2,1)}, bf16[2,1280,512]{2,1,0:T(8,128)(2,1)}, u32[]{:S(2)}, u32[]{:S(2)}) collective-permute-start(bf16[2,1280,512]{2,1,0:T(8,128)(2,1)} %get-tuple-element.22.refs_8_), channel_id=1, source_target_pairs={{0,1},{1,0},{2,3},{3,2},{4,5},{5,4},{6,7},{7,6}} | collective-permute-start | bytes 7864328 | tf_op jit(solution)/shard_map/ppermute | solution.py:629
  104.0 41.9 %collective-permute-start.9 = (bf16[1,1280,512]{2,1,0:T(8,128)(2,1)S(1)}, bf16[1,1280,512]{2,1,0:T(8,128)(2,1)}, u32[]{:S(2)}, u32[]{:S(2)}) collective-permute-start(bf16[1,1280,512]{2,1,0:T(8,128)(2,1)S(1)} %copy-done.1), channel_id=1, source_target_pairs={{0,1},{1,0},{2,3},{3,2},{4,5},{5,4},{6,7},{7,6}} | collective-permute-start | bytes 3932168 | tf_op jit(solution)/shard_map/ppermute | solution.py:629
  146.0 68.2 %collective-permute-start.10 = (bf16[1,512,1280]{2,1,0:T(8,128)(2,1)}, bf16[1,512,1280]{2,1,0:T(8,128)(2,1)S(1)}, u32[]{:S(2)}, u32[]{:S(2)}) collective-permute-start(bf16[1,512,1280]{2,1,0:T(8,128)(2,1)} %get-tuple-element.26.refs_4_), channel_id=1, source_target_pairs={{0,1},{1,0},{2,3},{3,2},{4,5},{5,4},{6,7},{7,6}} | collective-permute-start | bytes 3932168 | tf_op jit(solution)/shard_map/ppermute | solution.py:629
  146.0 68.2 %collective-permute-start.11 = (bf16[1,1280,512]{2,1,0:T(8,128)(2,1)}, bf16[1,1280,512]{2,1,0:T(8,128)(2,1)}, u32[]{:S(2)}, u32[]{:S(2)}) collective-permute-start(bf16[1,1280,512]{2,1,0:T(8,128)(2,1)} %get-tuple-element.27.refs_10_), channel_id=1, source_target_pairs={{0,1},{1,0},{2,3},{3,2},{4,5},{5,4},{6,7},{7,6}} | collective-permute-start | bytes 3932168 | tf_op jit(solution)/shard_map/ppermute | solution.py:629
  214.2 1.1 copy-start.2

commit v7 on v6

--- a/solution.py
+++ b/solution.py
@@ -13,9 +13,9 @@
 F32 = jnp.float32
 BF16 = jnp.bfloat16
 CH = 512
+TILE = 256
 HEADS = 4
 GW = HEADS * 64
-ORDER = (("F", 0), ("F", 1), ("S", 0), ("S", 1), ("F", 2), ("F", 3), ("S", 2), ("S", 3))
 VMEM_LIMIT = 62 * 1024 * 1024
 ANY = pl.BlockSpec(memory_space=pltpu.HBM)
 SMEM = pl.BlockSpec(memory_space=pltpu.SMEM)
@@ -47,7 +47,7 @@
 
             @pl.when(pick_ref[0] != 0)
             def _():
-                go(pltpu.make_async_copy(srcs[1], mem.at[pl.ds(0, CH)], sem))
+                go(pltpu.make_async_copy(srcs[1], mem.at[pl.ds(0, srcs[1].shape[0])], sem))
 
     def w_copy(i, v):
         return pltpu.make_async_copy((wk, wv)[v].at[lo + i], w_s.at[2 * i + v], w_sems.at[2 * i + v])
@@ -58,13 +58,13 @@
     w_copy(0, 1).start()
 
     def out_copy(i, v, c):
-        at = pl.ds(pl.multiple_of(c * CH, CH), CH)
+        at = pl.ds(pl.multiple_of(c * TILE, TILE), TILE)
         if v == 0:
             return pltpu.make_async_copy(k_s.at[i, at, :], k_out.at[i, at, :], o_sems.at[i, v, c])
         return pltpu.make_async_copy(vt_s.at[i, :, at], vt_out.at[i, :, at], o_sems.at[i, v, c])
 
     def valid(c, go):
-        @pl.when(lim_ref[c] > 0)
+        @pl.when(lim_ref[c * TILE // CH] > 0)
         def _():
             go()
 
@@ -76,30 +76,26 @@
             def _(v=v):
                 w_copy(i + 1, v).start()
 
-            def chunk_step(c, _):
+            def tile_step(c, _):
                 def work():
-                    def step(r, _):
-                        at = pl.ds(pl.multiple_of(c * CH + r * 256, 256), 256)
-                        out = dot(mem[at, :], w_s[2 * i + v]).astype(BF16)
-                        if v == 0:
-                            k_s[i, at, :] = out
-                        else:
-                            vt_s[i, :, at] = out.T
-                        return 0
-
-                    lax.fori_loop(0, CH // 256, step, 0)
+                    at = pl.ds(pl.multiple_of(c * TILE, TILE), TILE)
+                    out = dot(mem[at, :], w_s[2 * i + v]).astype(BF16)
+                    if v == 0:
+                        k_s[i, at, :] = out
+                    else:
+                        vt_s[i, :, at] = out.T
                     out_copy(i, v, c).start()
 
                 valid(c, work)
                 return 0
 
-            lax.fori_loop(0, rows // CH, chunk_step, 0)
+            lax.fori_loop(0, rows // TILE, tile_step, 0)
         return 0
 
     lax.fori_loop(0, n, layer_step, 0)
     for i in range(n):
         for v in range(2):
-            for c in range(rows // CH):
+            for c in range(rows // TILE):
                 valid(c, lambda i=i, v=v, c=c: out_copy(i, v, c).wait())
 
 
@@ -119,7 +115,7 @@
             pltpu.VMEM((n, cols, rows), BF16),
             pltpu.SemaphoreType.DMA,
             pltpu.SemaphoreType.DMA((2 * n,)),
-            pltpu.SemaphoreType.DMA((n, 2, rows // CH)),
+            pltpu.SemaphoreType.DMA((n, 2, rows // TILE)),
         ],
         cost_estimate=pl.CostEstimate(flops=flops, bytes_accessed=n * 4 * width * cols, transcendentals=0),
         compiler_params=pltpu.CompilerParams(vmem_limit_bytes=VMEM_LIMIT),
@@ -174,11 +170,9 @@
 
         made = scores(jnp.minimum(group_next, groups - 1), j_next)
         vt = values(group, j)
-        for what, h in ORDER:
-            if what == "F":
-                first(h, next(made), 1 - buf)
-            else:
-                second(group, h, vt, buf)
+        for h in range(HEADS):
+            first(h, next(made), 1 - buf)
+            second(group, h, vt, buf)
 
         @pl.when(j_next == 0)
         def _():
@@ -605,11 +599,12 @@
 
 NONE = 1 << 20
 BASES = (
-    (0, 512, 1024, 1536, 2048, NONE, NONE, 2560),
-    (1024, 1536, 0, 512, NONE, 2048, 2560, NONE),
-    (2048, NONE, 2560, NONE, 0, 1024, 512, 1536),
-    (2560, NONE, 2048, NONE, 1024, 0, 1536, 512),
+    (0, 512, 1024, 1536, 2048, NONE, 2560, NONE),
+    (1024, 1536, 0, 512, 2560, NONE, 2048, NONE),
+    (2048, NONE, 2560, NONE, 0, 512, 1024, 1536),
+    (2560, NONE, 2048, NONE, 1024, 1536, 0, 512),
 )
+FIRST = 768
 
 
 def solution(mesh):
@@ -623,28 +618,29 @@
         dev_arr = dev.astype(jnp.int32).reshape(1)
         bases = jnp.array(BASES, jnp.int32)[dev]
         lims = jnp.clip(mem_len[0] - bases, 0, CH)
-        is3 = (dev_arr == 3).astype(jnp.int32)
+        is1, is3 = (dev_arr == 1).astype(jnp.int32), (dev_arr == 3).astype(jnp.int32)
 
         def swap(x):
             return lax.ppermute(x, 'sp', [(0, 1), (1, 0), (2, 3), (3, 2)])
 
         def program(hidden):
             far = lax.ppermute(hidden, 'sp', [(0, 2), (1, 3)])
-            mem_a, mem_b = memory[:CH], memory[CH:]
-            c2b = lax.ppermute(mem_b, 'sp', [(2, 3)])
+            mem_a, mem_b, mem_c = memory[:FIRST], memory[FIRST:], memory[CH:]
+            c2b = lax.ppermute(mem_c, 'sp', [(2, 3)])
             rem_a = lax.ppermute(mem_a, 'sp', [(0, 2), (1, 3), (2, 0)])
-            rem_b = lax.ppermute(mem_b, 'sp', [(0, 2), (1, 3), (2, 1)])
+            back = lax.ppermute(c2b, 'sp', [(3, 1)])
+            rem_b = lax.ppermute(mem_b, 'sp', [(0, 2), (1, 3)])
 
             both = (0, layers)
             ka, va = kv_project(lims[0:2], is3, [memory, c2b], cross_k, cross_v, 2 * CH, both)
             kas, vas = swap(ka), swap(va)
-            kb, vb = kv_project(lims[4:5], is3, [rem_a], cross_k, cross_v, CH, both)
+            kb, vb = kv_project(lims[4:6], is1, [rem_a, back], cross_k, cross_v, FIRST, both)
             kbs, vbs = swap(kb), swap(vb)
             kvs = []
             for layer in range(layers):
-                kc, vc = kv_project(lims[6:7], is3, [rem_b], cross_k, cross_v, CH, (layer, 1))
+                kc, vc = kv_project(lims[5:6], is1, [rem_b], cross_k, cross_v, 2 * CH - FIRST, (layer, 1))
                 kcs, vcs = swap(kc), swap(vc)
-                kvs.append([(ka, va, layer), (kas, vas, layer), (kb, vb, layer), (kbs, vbs, layer), (kc, vc, 0), (kcs, vcs, 0)])
+                kvs.append([(ka, va, layer), (kas, vas, layer), (kb, vb, layer), (kc, vc, 0), (kbs, vbs, layer), (kcs, vcs, 0)])
 
             for layer in range(layers):
                 hidden, q = self_attention(layer, hidden, far, norm_self, norm_cross, self_q, self_k, self_v, w_so, cross_q)

time: 254 us -> 249 us (0.980)
  the two profiles are of different devices: /device:TPU:7 before, /device:TPU:3 now
where the time goes in v7:
time: 249 us
  Pallas kernels  170 us (68%)
  waiting for transfers between devices  52.2 us (21%)
  starting transfers between devices  18.7 us (8%)
  local copies, waits for them, and re-layouts  6.3 us (3%)
    pallas_call x2, Pallas kernels, cross_mlp(): pl.pallas_call(functools.partial(cross_kernel, layer, planes, n), in_spec...  75.4 us
    pallas_call x2, Pallas kernels, self_attention(): pl.pallas_call(functools.partial(self_kernel, layer, far_given), in_specs...  56.7 us
    pallas_call x4, Pallas kernels, kv_project(): pl.pallas_call(functools.partial(kv_kernel, layers, len(srcs)), in_specs=...  37.7 us
    ppermute x1, waiting for transfers between devices, program(): rem_a = lax.ppermute(mem_a, 'sp', [(0, 2), (1, 3), (2, 0)])  27.4 us
    ppermute x1, waiting for transfers between devices, program(): rem_b = lax.ppermute(mem_b, 'sp', [(0, 2), (1, 3)])  16.4 us
    ppermute x1, waiting for transfers between devices, program(): far = lax.ppermute(hidden, 'sp', [(0, 2), (1, 3)])  8.28 us
    ppermute x8, starting transfers between devices, swap(): return lax.ppermute(x, 'sp', [(0, 1), (1, 0), (2, 3), (3, 2)])  7.2 us
    ppermute x1, starting transfers between devices, program(): back = lax.ppermute(c2b, 'sp', [(3, 1)])  6.37 us
  transfers between devices with their start and end apart: 13, of which 3 were waited for; matrix products, arithmetic and copies ran while one was open for 2% of the time, Pallas kernels for 53%

profile of v7, /device:TPU:3, one launch (start us, length us, event | category | flops | bytes accessed | tf_op | source)
XLA Modules:
  0.0 248.6 jit_solution(14943075046607150910)
XLA Ops:
  0.0 1.4 slice.30
  1.4 1.3 collective-permute-start.1
  2.7 1.7 slice.33
  4.4 1.3 collective-permute-start.3
  6.4 0.0 copy-done.6
  6.4 0.6 slice_bitcast_fusion
  7.0 0.0 collective-permute-done.1.refs_1_
  7.0 6.4 %collective-permute-start.4 = (bf16[512,1280]{1,0:T(8,128)(2,1)}, bf16[512,1280]{1,0:T(8,128)(2,1)}, u32[]{:S(2)}, u32[]{:S(2)}) collective-permute-start(bf16[512,1280]{1,0:T(8,128)(2,1)} %collective-permute-done.1.refs_1_), channel_id=1, source_target_pairs={{3,1},{7,5}} | collective-permute-start | bytes 3932168 | tf_op jit(solution)/shard_map/ppermute | solution.py:631
  13.4 7.2 %kv_project.4 = (bf16[2,1024,1280]{2,1,0:T(8,128)(2,1)}, bf16[2,1280,1024]{2,1,0:T(8,128)(2,1)}) custom-call(s32[2]{0:T(128)} %get-tuple-element.30.lim_ref, s32[1]{0:T(128)} %bitcast.4.pick_ref, bf16[1024,1280]{1,0:T(8,128)(2,1)} %refs_0_.3, bf16[512,1280]{1,0:T(8,128)(2,1)} %collective-permute-done.1.refs_1_, bf16[2,1280,1280]{2,1,0:T(8,128)(2,1)} %refs_1_.5, ...), custom_call_target="tpu_custom_call" | custom-call | flops 13421772800 | bytes 13107200 | tf_op jit(solution)/shard_map/kv_project/pallas_call | solution.py:106
  20.6 0.0 collective-permute-start.2
  20.6 0.5 collective-permute-start.8
  21.1 27.4 %collective-permute-done.3.refs_0_ = bf16[768,1280]{1,0:T(8,128)(2,1)} collective-permute-done((bf16[768,1280]{1,0:T(8,128)(2,1)S(1)}, bf16[768,1280]{1,0:T(8,128)(2,1)}, u32[]{:S(2)}, u32[]{:S(2)}) %collective-permute-start.3) | collective-permute-done | bytes 1966112 | tf_op jit(solution)/shard_map/ppermute | solution.py:630
  48.6 0.0 collective-permute-done.4.refs_1_
  48.6 17.2 %kv_project.5 = (bf16[2,768,1280]{2,1,0:T(8,128)(2,1)}, bf16[2,1280,768]{2,1,0:T(8,128)(2,1)}) custom-call(s32[2]{0:T(128)} %get-tuple-element.29.lim_ref, s32[1]{0:T(128)} %bitcast.6.pick_ref, bf16[768,1280]{1,0:T(8,128)(2,1)} %collective-permute-done.3.refs_0_, bf16[512,1280]{1,0:T(8,128)(2,1)} %collective-permute-done.4.refs_1_, ...), custom_call_target="tpu_custom_call" | custom-call | flops 10066329600 | bytes 13107200 | tf_op jit(solution)/shard_map/kv_project/pallas_call | solution.py:106
  65.8 3.1 %collective-permute-start.6 = (bf16[2,768,1280]{2,1,0:T(8,128)(2,1)}, bf16[2,768,1280]{2,1,0:T(8,128)(2,1)}, u32[]{:S(2)}, u32[]{:S(2)}) collective-permute-start(bf16[2,768,1280]{2,1,0:T(8,128)(2,1)} %get-tuple-element.19.refs_2_), channel_id=1, source_target_pairs={{0,1},{1,0},{2,3},{3,2},{4,5},{5,4},{6,7},{7,6}} | collective-permute-start | bytes 11796488 | tf_op jit(solution)/shard_map/ppermute | solution.py:624
  68.9 0.0 collective-permute-start.9
  68.9 1.1 slice.36
  70.1 1.3 collective-permute-start.5
  71.4 16.4 %collective-permute-done.5.refs_0_ = bf16[256,1280]{1,0:T(8,128)(2,1)S(1)} collective-permute-done((bf16[256,1280]{1,0:T(8,128)(2,1)S(1)}, bf16[256,1280]{1,0:T(8,128)(2,1)S(1)}, u32[]{:S(2)}, u32[]{:S(2)}) %collective-permute-start.5) | collective-permute-done | bytes 655392 | tf_op jit(solution)/shard_map/ppermute | solution.py:632
  87.8 0.0 copy-done.7
  87.8 1.3 collective-permute-start
  89.1 0.6 slice.34
  89.7 0.0 copy-done
  89.7 6.6 %kv_project.6 = (bf16[1,256,1280]{2,1,0:T(8,128)(2,1)}, bf16[1,1280,256]{2,1,0:T(8,128)(2,1)}) custom-call(s32[1]{0:T(128)} %bitcast.7.lim_ref, s32[1]{0:T(128)} %bitcast.6.pick_ref, bf16[256,1280]{1,0:T(8,128)(2,1)} %copy-done, bf16[2,1280,1280]{2,1,0:T(8,128)(2,1)} %refs_1_.5, bf16[2,1280,1280]{2,1,0:T(8,128)(2,1)} %refs_2_.11), custom_call_target="tpu_custom_call" | custom-call | flops 1677721600 | bytes 6553600 | tf_op jit(solution)/shard_map/kv_project/pallas_call | solution.py:106
  96.3 8.3 %collective-permute-done.refs_1_ = bf16[256,1280]{1,0:T(8,128)(2,1)S(1)} collective-permute-done((bf16[256,1280]{1,0:T(8,128)(2,1)S(1)}, bf16[256,1280]{1,0:T(8,128)(2,1)S(1)}, u32[]{:S(2)}, u32[]{:S(2)}) %collective-permute-start) | collective-permute-done | bytes 655392 | tf_op jit(solution)/shard_map/ppermute | solution.py:627
  104.6 2.2 collective-permute-start.7
  106.8 0.6 fusion.lim_ref
  107.4 6.7 %kv_project.7 = (bf16[1,256,1280]{2,1,0:T(8,128)(2,1)}, bf16[1,1280,256]{2,1,0:T(8,128)(2,1)}) custom-call(s32[1]{0:T(128)} %bitcast.7.lim_ref, s32[1]{0:T(128)} %bitcast.6.pick_ref, bf16[256,1280]{1,0:T(8,128)(2,1)} %copy-done, bf16[2,1280,1280]{2,1,0:T(8,128)(2,1)} %refs_1_.5, bf16[2,1280,1280]{2,1,0:T(8,128)(2,1)} %refs_2_.11), custom_call_target="tpu_custom_call" | custom-call | flops 1677721600 | bytes 6553600 | tf_op jit(solution)/shard_map/kv_project/pallas_call | solution.py:106
  114.1 0.0 collective-permute-done.7.refs_5_
  114.1 0.0 copy-start.4
  114.1 0.0 copy-done.3
  114.1 0.9 collective-permute-start.10
  115.0 0.0 copy-done.4
  115.0 27.1 %self_attention.2 = (bf16[256,1280]{1,0:T(8,128)(2,1)}, bf16[1280,256]{1,0:T(8,128)(2,1)}) custom-call(bf16[256,1280]{1,0:T(8,128)(2,1)} %refs_0_.2, bf16[256,1280]{1,0:T(8,128)(2,1)} %copy-done.8, bf16[2,1280]{1,0:T(2,128)(2,1)} %refs_1_.4, bf16[2,1280]{1,0:T(2,128)(2,1)} %refs_2_.10, bf16[2,1280,1280]{2,1,0:T(8,128)(2,1)} %refs_3_.7, ...), custom_call_target="tpu_custom_call" | custom-call | flops 10569646080 | bytes 16384000 | tf_op jit(solution)/shard_map/self_attention/pallas_call | solution.py:388
  142.1 0.0 collective-permute-done.10.refs_11_
  142.1 0.0 collective-permute-start.11
  142.1 0.0 collective-permute-done.2.refs_1_
  142.1 0.0 copy-done.2
  142.2 0.5 collective-permute-start.12
  142.6 0.0 collective-permute-done.6.refs_4_
  142.6 0.0 collective-permute-done.8.refs_7_
  142.6 0.0 collective-permute-done.9.refs_10_
  142.6 37.6 %cross_mlp.2.refs_0_ = bf16[256,1280]{1,0:T(8,128)(2,1)} custom-call(s32[8]{0:T(128)} %fusion.lim_ref, bf16[1280,256]{1,0:T(8,128)(2,1)} %get-tuple-element.17.q_ref, bf16[2,1024,1280]{2,1,0:T(8,128)(2,1)} %get-tuple-element.18.refs_0_, bf16[2,1024,1280]{2,1,0:T(8,128)(2,1)} %collective-permute-done.2.refs_1_, ...), custom_call_target="tpu_custom_call" | custom-call | flops 14931722240 | bytes 42598400 | tf_op jit(solution)/shard_map/cross_mlp/pallas_call | solution.py:569
  180.2 29.6 %self_attention.3 = (bf16[256,1280]{1,0:T(8,128)(2,1)}, bf16[1280,256]{1,0:T(8,128)(2,1)}) custom-call(bf16[256,1280]{1,0:T(8,128)(2,1)} %cross_mlp.2.refs_0_, bf16[2,1280]{1,0:T(2,128)(2,1)} %refs_1_.4, bf16[2,1280]{1,0:T(2,128)(2,1)} %refs_2_.10, bf16[2,1280,1280]{2,1,0:T(8,128)(2,1)} %refs_3_.7, bf16[2,1280,1280]{2,1,0:T(8,128)(2,1)} %refs_4_.3, ...), custom_call_target="tpu_custom_call" | custom-call | flops 10569646080 | bytes 16384000 | tf_op jit(solution)/shard_map/self_attention/pallas_call | solution.py:388
  209.8 0.0 collective-permute-done.11.refs_5_
  209.8 0.0 collective-permute-done.12.refs_11_
  209.8 0.8 copy-done.5
  210.6 37.8 %cross_mlp.3 = bf16[256,1280]{1,0:T(8,128)(2,1)} custom-call(s32[8]{0:T(128)} %fusion.lim_ref, bf16[1280,256]{1,0:T(8,128)(2,1)} %get-tuple-element.25.q_ref, bf16[2,1024,1280]{2,1,0:T(8,128)(2,1)} %get-tuple-element.18.refs_0_, bf16[2,1024,1280]{2,1,0:T(8,128)(2,1)} %collective-permute-done.2.refs_1_, bf16[2,768,1280]{2,1,0:T(8,128)(2,1)} %get-tuple-element.19.refs_2_, ...), custom_call_target="tpu_custom_call" | custom-call | flops 14931722240 | bytes 42598400 | tf_op jit(solution)/shard_map/cross_mlp/pallas_call | solution.py:569
  (11 shorter events, 0.0 us)
Async XLA Ops:
  0.0 6.4 %copy-start.6 = (s32[4,8]{1,0:T(4,128)S(1)}, s32[4,8]{1,0:T(4,128)}, u32[]{:S(2)}) copy-start(s32[4,8]{1,0:T(4,128)} %constant.18.clone) | copy-start | bytes 388
  1.4 5.6 %collective-permute-start.1 = (bf16[512,1280]{1,0:T(8,128)(2,1)S(1)}, bf16[512,1280]{1,0:T(8,128)(2,1)}, u32[]{:S(2)}, u32[]{:S(2)}) collective-permute-start(bf16[512,1280]{1,0:T(8,128)(2,1)S(1)} %slice.30), channel_id=1, source_target_pairs={{2,3},{6,7}} | collective-permute-start | bytes 3932168 | tf_op jit(solution)/shard_map/ppermute | solution.py:629
  4.4 44.2 %collective-permute-start.3 = (bf16[768,1280]{1,0:T(8,128)(2,1)S(1)}, bf16[768,1280]{1,0:T(8,128)(2,1)}, u32[]{:S(2)}, u32[]{:S(2)}) collective-permute-start(bf16[768,1280]{1,0:T(8,128)(2,1)S(1)} %slice.33), channel_id=1, source_target_pairs={{0,2},{1,3},{2,0},{4,6},{5,7},{6,4}} | collective-permute-start | bytes 5898248 | tf_op jit(solution)/shard_map/ppermute | solution.py:630
  7.0 41.6 %collective-permute-start.4 = (bf16[512,1280]{1,0:T(8,128)(2,1)}, bf16[512,1280]{1,0:T(8,128)(2,1)}, u32[]{:S(2)}, u32[]{:S(2)}) collective-permute-start(bf16[512,1280]{1,0:T(8,128)(2,1)} %collective-permute-done.1.refs_1_), channel_id=1, source_target_pairs={{3,1},{7,5}} | collective-permute-start | bytes 3932168 | tf_op jit(solution)/shard_map/ppermute | solution.py:631
  20.6 121.5 %collective-permute-start.2 = (bf16[2,1024,1280]{2,1,0:T(8,128)(2,1)}, bf16[2,1024,1280]{2,1,0:T(8,128)(2,1)}, u32[]{:S(2)}, u32[]{:S(2)}) collective-permute-start(bf16[2,1024,1280]{2,1,0:T(8,128)(2,1)} %get-tuple-element.18.refs_0_), channel_id=1, source_target_pairs={{0,1},{1,0},{2,3},{3,2},{4,5},{5,4},{6,7},{7,6}} | collective-permute-start | bytes 15728648 | tf_op jit(solution)/shard_map/ppermute | solution.py:624
  20.6 122.0 %collective-permute-start.8 = (bf16[2,1280,1024]{2,1,0:T(8,128)(2,1)}, bf16[2,1280,1024]{2,1,0:T(8,128)(2,1)}, u32[]{:S(2)}, u32[]{:S(2)}) collective-permute-start(bf16[2,1280,1024]{2,1,0:T(8,128)(2,1)} %get-tuple-element.21.refs_6_), channel_id=1, source_target_pairs={{0,1},{1,0},{2,3},{3,2},{4,5},{5,4},{6,7},{7,6}} | collective-permute-start | bytes 15728648 | tf_op jit(solution)/shard_map/ppermute | solution.py:624
  48.6 39.2 %copy-start.7 = (bf16[256,1280]{1,0:T(8,128)(2,1)S(1)}, bf16[256,1280]{1,0:T(8,128)(2,1)}, u32[]{:S(2)}) copy-start(bf16[256,1280]{1,0:T(8,128)(2,1)} %refs_0_.2) | copy-start | bytes 1966084
  65.8 76.8 %collective-permute-start.6 = (bf16[2,768,1280]{2,1,0:T(8,128)(2,1)}, bf16[2,768,1280]{2,1,0:T(8,128)(2,1)}, u32[]{:S(2)}, u32[]{:S(2)}) collective-permute-start(bf16[2,768,1280]{2,1,0:T(8,128)(2,1)} %get-tuple-element.19.refs_2_), channel_id=1, source_target_pairs={{0,1},{1,0},{2,3},{3,2},{4,5},{5,4},{6,7},{7,6}} | collective-permute-start | bytes 11796488 | tf_op jit(solution)/shard_map/ppermute | solution.py:624
  68.9 73.8 %collective-permute-start.9 = (bf16[2,1280,768]{2,1,0:T(8,128)(2,1)}, bf16[2,1280,768]{2,1,0:T(8,128)(2,1)}, u32[]{:S(2)}, u32[]{:S(2)}) collective-permute-start(bf16[2,1280,768]{2,1,0:T(8,128)(2,1)} %get-tuple-element.22.refs_8_), channel_id=1, source_target_pairs={{0,1},{1,0},{2,3},{3,2},{4,5},{5,4},{6,7},{7,6}} | collective-permute-start | bytes 11796488 | tf_op jit(solution)/shard_map/ppermute | solution.py:624
  70.1 17.7 %collective-permute-start.5 = (bf16[256,1280]{1,0:T(8,128)(2,1)S(1)}, bf16[256,1280]{1,0:T(8,128)(2,1)S(1)}, u32[]{:S(2)}, u32[]{:S(2)}) collective-permute-start(bf16[256,1280]{1,0:T(8,128)(2,1)S(1)} %slice.36), channel_id=1, source_target_pairs={{0,2},{1,3},{4,6},{5,7}} | collective-permute-start | bytes 1966088 | tf_op jit(solution)/shard_map/ppermute | solution.py:632
  87.8 1.9 copy-start
  87.8 16.8 %collective-permute-start = (bf16[256,1280]{1,0:T(8,128)(2,1)S(1)}, bf16[256,1280]{1,0:T(8,128)(2,1)S(1)}, u32[]{:S(2)}, u32[]{:S(2)}) collective-permute-start(bf16[256,1280]{1,0:T(8,128)(2,1)S(1)} %copy-done.7), channel_id=1, source_target_pairs={{0,2},{1,3},{4,6},{5,7}} | collective-permute-start | bytes 1966088 | tf_op jit(solution)/shard_map/ppermute | solution.py:627
  104.6 2.2 copy-start.8
  104.6 9.5 %collective-permute-start.7 = (bf16[1,256,1280]{2,1,0:T(8,128)(2,1)}, bf16[1,256,1280]{2,1,0:T(8,128)(2,1)S(1)}, u32[]{:S(2)}, u32[]{:S(2)}) collective-permute-start(bf16[1,256,1280]{2,1,0:T(8,128)(2,1)} %get-tuple-element.20.refs_3_), channel_id=1, source_target_pairs={{0,1},{1,0},{2,3},{3,2},{4,5},{5,4},{6,7},{7,6}} | collective-permute-start | bytes 1966088 | tf_op jit(solution)/shard_map/ppermute | solution.py:624
  107.4 6.7 %copy-start.3 = (bf16[1,1280,256]{2,1,0:T(8,128)(2,1)S(1)}, bf16[1,1280,256]{2,1,0:T(8,128)(2,1)}, u32[]{:S(2)}) copy-start(bf16[1,1280,256]{2,1,0:T(8,128)(2,1)} %get-tuple-element.23.refs_9_) | copy-start | bytes 1966084
  114.1 0.9 copy-start.4
  114.1 28.0 %collective-permute-start.10 = (bf16[1,1280,256]{2,1,0:T(8,128)(2,1)S(1)}, bf16[1,1280,256]{2,1,0:T(8,128)(2,1)}, u32[]{:S(2)}, u32[]{:S(2)}) collective-permute-start(bf16[1,1280,256]{2,1,0:T(8,128)(2,1)S(1)} %copy-done.3), channel_id=1, source_target_pairs={{0,1},{1,0},{2,3},{3,2},{4,5},{5,4},{6,7},{7,6}} | collective-permute-start | bytes 1966088 | tf_op jit(solution)/shard_map/ppermute | solution.py:624
  115.0 27.1 %copy-start.1 = (bf16[1,256,1280]{2,1,0:T(8,128)(2,1)S(1)}, bf16[1,256,1280]{2,1,0:T(8,128)(2,1)}, u32[]{:S(2)}) copy-start(bf16[1,256,1280]{2,1,0:T(8,128)(2,1)} %get-tuple-element.26.refs_3_) | copy-start | bytes 1966084
  115.0 27.2 %copy-start.2 = (bf16[1,1280,256]{2,1,0:T(8,128)(2,1)S(1)}, bf16[1,1280,256]{2,1,0:T(8,128)(2,1)}, u32[]{:S(2)}) copy-start(bf16[1,1280,256]{2,1,0:T(8,128)(2,1)} %get-tuple-element.27.refs_9_) | copy-start | bytes 1966084
  142.1 67.7 %collective-permute-start.11 = (bf16[1,256,1280]{2,1,0:T(8,128)(2,1)S(1)}, bf16[1,256,1280]{2,1,0:T(8,128)(2,1)S(1)}, u32[]{:S(2)}, u32[]{:S(2)}) collective-permute-start(bf16[1,256,1280]{2,1,0:T(8,128)(2,1)S(1)} %copy-done.1), channel_id=1, source_target_pairs={{0,1},{1,0},{2,3},{3,2},{4,5},{5,4},{6,7},{7,6}} | collective-permute-start | bytes 1966088 | tf_op jit(solution)/shard_map/ppermute | solution.py:624
  142.2 67.7 %collective-permute-start.12 = (bf16[1,1280,256]{2,1,0:T(8,128)(2,1)S(1)}, bf16[1,1280,256]{2,1,0:T(8,128)(2,1)}, u32[]{:S(2)}, u32[]{:S(2)}) collective-permute-start(bf16[1,1280,256]{2,1,0:T(8,128)(2,1)S(1)} %copy-done.2), channel_id=1, source_target_pairs={{0,1},{1,0},{2,3},{3,2},{4,5},{5,4},{6,7},{7,6}} | collective-permute-start | bytes 1966088 | tf_op jit(solution)/shard_map/ppermute | solution.py:624
  209.8 0.8 copy-start.5

commit v8 on v6

--- a/solution.py
+++ b/solution.py
@@ -15,7 +15,6 @@
 CH = 512
 HEADS = 4
 GW = HEADS * 64
-ORDER = (("F", 0), ("F", 1), ("S", 0), ("S", 1), ("F", 2), ("F", 3), ("S", 2), ("S", 3))
 VMEM_LIMIT = 62 * 1024 * 1024
 ANY = pl.BlockSpec(memory_space=pltpu.HBM)
 SMEM = pl.BlockSpec(memory_space=pltpu.SMEM)
@@ -174,11 +173,9 @@
 
         made = scores(jnp.minimum(group_next, groups - 1), j_next)
         vt = values(group, j)
-        for what, h in ORDER:
-            if what == "F":
-                first(h, next(made), 1 - buf)
-            else:
-                second(group, h, vt, buf)
+        for h in range(HEADS):
+            first(h, next(made), 1 - buf)
+            second(group, h, vt, buf)
 
         @pl.when(j_next == 0)
         def _():
@@ -450,7 +447,6 @@
         kv_copies(i, lambda cp: cp.start())
 
     kv_start(0)
-    kv_start(1)
     o_copy = pltpu.make_async_copy(wco.at[layer], wo_s, o_sem)
 
     def w_copies(j):
@@ -488,6 +484,7 @@
 
         @pl.when(i == 0)
         def _():
+            kv_start(1)
             o_copy.start()
             for j in range(ring - groups):
                 w_start(j)

time: 254 us -> 254 us (level)
  no operation moved by 1% of the time
where the time goes in v8:
time: 254 us; the launch traced here: 253 us
  Pallas kernels  175 us (69%)
  waiting for transfers between devices  60.5 us (24%)
  local copies, waits for them, and re-layouts  8.5 us (3%)
  starting transfers between devices  7.76 us (3%)
    pallas_call x2, Pallas kernels, cross_mlp(): pl.pallas_call(functools.partial(cross_kernel, layer, planes, n), in_spec...  76.4 us
    pallas_call x2, Pallas kernels, self_attention(): pl.pallas_call(functools.partial(self_kernel, layer, far_given), in_specs...  62.3 us
    ppermute x1, waiting for transfers between devices, program(): rem_b = lax.ppermute(mem_b, 'sp', [(0, 2), (1, 3), (2, 1)])  38.9 us
    pallas_call x4, Pallas kernels, kv_project(): pl.pallas_call(functools.partial(kv_kernel, layers, len(srcs)), in_specs=...  36.5 us
    ppermute x1, waiting for transfers between devices, program(): rem_a = lax.ppermute(mem_a, 'sp', [(0, 2), (1, 3), (2, 0)])  18.4 us
  transfers between devices with their start and end apart: 12, of which 4 were waited for; matrix products, arithmetic and copies ran while one was open for 1% of the time, Pallas kernels for 51%

profile of v8, /device:TPU:7, one launch (start us, length us, event | category | flops | bytes accessed | tf_op | source)
XLA Modules:
  0.0 253.4 jit_solution(7809168589329559574)
XLA Ops:
  0.0 0.0 copy-start.4
  0.0 3.0 %fusion = (bf16[512,1280]{1,0:T(8,128)(2,1)}, bf16[512,1280]{1,0:T(8,128)(2,1)S(1)}) fusion(bf16[1024,1280]{1,0:T(8,128)(2,1)} %refs_0_.3), kind=kLoop, calls=%fused_computation.2 | loop fusion | bytes 5242880 | tf_op jit(solution)/shard_map/slice | solution.py:630
  3.0 0.0 copy-start.3
  3.0 1.1 copy-done.3
  4.1 1.3 collective-permute-start.1
  6.0 0.0 copy-done.4
  6.0 0.6 slice_bitcast_fusion.lim_ref
  6.6 2.4 collective-permute-done.1.refs_1_
  9.0 0.0 copy-start.5
  9.0 1.1 copy-done.5
  10.1 0.0 copy-start.6
  10.1 7.3 %kv_project.4 = (bf16[2,1024,1280]{2,1,0:T(8,128)(2,1)}, bf16[2,1280,1024]{2,1,0:T(8,128)(2,1)}) custom-call(s32[2]{0:T(128)} %slice_bitcast_fusion.lim_ref, s32[1]{0:T(128)} %bitcast.4.pick_ref, bf16[1024,1280]{1,0:T(8,128)(2,1)} %refs_0_.3, bf16[512,1280]{1,0:T(8,128)(2,1)} %copy-done.5, bf16[2,1280,1280]{2,1,0:T(8,128)(2,1)} %refs_1_.7, ...), custom_call_target="tpu_custom_call" | custom-call | flops 13421772800 | bytes 13107200 | tf_op jit(solution)/shard_map/kv_project/pallas_call | solution.py:109
  17.4 0.6 collective-permute-start.2
  17.9 0.0 collective-permute-start.7
  18.0 1.3 collective-permute-start.5
  19.3 1.3 collective-permute-start.3
  20.6 0.0 copy-done.6
  20.6 1.3 collective-permute-start
  21.9 0.6 fusion.1
  22.5 38.9 %collective-permute-done.5.refs_0_ = bf16[512,1280]{1,0:T(8,128)(2,1)S(1)} collective-permute-done((bf16[512,1280]{1,0:T(8,128)(2,1)}, bf16[512,1280]{1,0:T(8,128)(2,1)S(1)}, u32[]{:S(2)}, u32[]{:S(2)}) %collective-permute-start.5) | collective-permute-done | bytes 1310752 | tf_op jit(solution)/shard_map/ppermute | solution.py:633
  61.4 1.1 copy-done
  62.4 8.3 %kv_project.6 = (bf16[1,512,1280]{2,1,0:T(8,128)(2,1)}, bf16[1,1280,512]{2,1,0:T(8,128)(2,1)}) custom-call(s32[1]{0:T(128)} %bitcast.6.lim_ref, s32[1]{0:T(128)} %bitcast.4.pick_ref, bf16[512,1280]{1,0:T(8,128)(2,1)} %copy-done, bf16[2,1280,1280]{2,1,0:T(8,128)(2,1)} %refs_1_.7, bf16[2,1280,1280]{2,1,0:T(8,128)(2,1)} %refs_2_.11), custom_call_target="tpu_custom_call" | custom-call | flops 3355443200 | bytes 6553600 | tf_op jit(solution)/shard_map/kv_project/pallas_call | solution.py:109
  70.7 0.5 collective-permute-start.6
  71.2 18.4 %collective-permute-done.3.refs_0_ = bf16[512,1280]{1,0:T(8,128)(2,1)} collective-permute-done((bf16[512,1280]{1,0:T(8,128)(2,1)}, bf16[512,1280]{1,0:T(8,128)(2,1)}, u32[]{:S(2)}, u32[]{:S(2)}) %collective-permute-start.3) | collective-permute-done | bytes 1310752 | tf_op jit(solution)/shard_map/ppermute | solution.py:632
  89.5 12.7 %kv_project.5 = (bf16[2,512,1280]{2,1,0:T(8,128)(2,1)}, bf16[2,1280,512]{2,1,0:T(8,128)(2,1)}) custom-call(s32[1]{0:T(128)} %bitcast.5.lim_ref, s32[1]{0:T(128)} %bitcast.4.pick_ref, bf16[512,1280]{1,0:T(8,128)(2,1)} %collective-permute-done.3.refs_0_, bf16[2,1280,1280]{2,1,0:T(8,128)(2,1)} %refs_1_.7, bf16[2,1280,1280]{2,1,0:T(8,128)(2,1)} %refs_2_.11), custom_call_target="tpu_custom_call" | custom-call | flops 6710886400 | bytes 13107200 | tf_op jit(solution)/shard_map/kv_project/pallas_call | solution.py:109
  102.2 0.5 collective-permute-start.4
  102.7 0.9 collective-permute-done.refs_1_
  103.6 0.4 collective-permute-start.8
  104.0 0.0 collective-permute-done.6.refs_5_
  104.0 0.0 copy-done.1
  104.0 0.1 collective-permute-start.9
  104.1 0.5 fusion.2.lim_ref
  104.6 32.7 %self_attention.2 = (bf16[256,1280]{1,0:T(8,128)(2,1)}, bf16[1280,256]{1,0:T(8,128)(2,1)}) custom-call(bf16[256,1280]{1,0:T(8,128)(2,1)} %refs_0_.2, bf16[256,1280]{1,0:T(8,128)(2,1)} %collective-permute-done.refs_1_, bf16[2,1280]{1,0:T(2,128)(2,1)} %refs_1_.6, bf16[2,1280]{1,0:T(2,128)(2,1)} %refs_2_.10, bf16[2,1280,1280]{2,1,0:T(8,128)(2,1)} %refs_3_.5, ...), custom_call_target="tpu_custom_call" | custom-call | flops 10569646080 | bytes 16384000 | tf_op jit(solution)/shard_map/self_attention/pallas_call | solution.py:391
  137.3 8.3 %kv_project.7 = (bf16[1,512,1280]{2,1,0:T(8,128)(2,1)}, bf16[1,1280,512]{2,1,0:T(8,128)(2,1)}) custom-call(s32[1]{0:T(128)} %bitcast.6.lim_ref, s32[1]{0:T(128)} %bitcast.4.pick_ref, bf16[512,1280]{1,0:T(8,128)(2,1)} %copy-done, bf16[2,1280,1280]{2,1,0:T(8,128)(2,1)} %refs_1_.7, bf16[2,1280,1280]{2,1,0:T(8,128)(2,1)} %refs_2_.11), custom_call_target="tpu_custom_call" | custom-call | flops 3355443200 | bytes 6553600 | tf_op jit(solution)/shard_map/kv_project/pallas_call | solution.py:109
  145.6 0.0 collective-permute-done.9.refs_11_
  145.6 0.0 collective-permute-start.10
  145.6 0.0 collective-permute-done.4.refs_3_
  145.6 0.5 collective-permute-start.11
  146.1 0.0 collective-permute-done.8.refs_9_
  146.1 0.0 collective-permute-done.2.refs_1_
  146.1 0.0 collective-permute-done.7.refs_7_
  146.1 38.7 %cross_mlp.2.refs_0_ = bf16[256,1280]{1,0:T(8,128)(2,1)} custom-call(s32[8]{0:T(128)} %fusion.2.lim_ref, bf16[1280,256]{1,0:T(8,128)(2,1)} %get-tuple-element.17.q_ref, bf16[2,1024,1280]{2,1,0:T(8,128)(2,1)} %get-tuple-element.18.refs_0_, bf16[2,1024,1280]{2,1,0:T(8,128)(2,1)} %collective-permute-done.2.refs_1_, ...), custom_call_target="tpu_custom_call" | custom-call | flops 14931722240 | bytes 42598400 | tf_op jit(solution)/shard_map/cross_mlp/pallas_call | solution.py:572
  184.9 29.6 %self_attention.3 = (bf16[256,1280]{1,0:T(8,128)(2,1)}, bf16[1280,256]{1,0:T(8,128)(2,1)}) custom-call(bf16[256,1280]{1,0:T(8,128)(2,1)} %cross_mlp.2.refs_0_, bf16[2,1280]{1,0:T(2,128)(2,1)} %refs_1_.6, bf16[2,1280]{1,0:T(2,128)(2,1)} %refs_2_.10, bf16[2,1280,1280]{2,1,0:T(8,128)(2,1)} %refs_3_.5, bf16[2,1280,1280]{2,1,0:T(8,128)(2,1)} %refs_4_.3, ...), custom_call_target="tpu_custom_call" | custom-call | flops 10569646080 | bytes 16384000 | tf_op jit(solution)/shard_map/self_attention/pallas_call | solution.py:391
  214.5 0.0 collective-permute-done.10.refs_5_
  214.5 0.0 copy-start.2
  214.5 0.0 collective-permute-done.11.refs_11_
  214.5 1.1 copy-done.2
  215.6 37.6 %cross_mlp.3 = bf16[256,1280]{1,0:T(8,128)(2,1)} custom-call(s32[8]{0:T(128)} %fusion.2.lim_ref, bf16[1280,256]{1,0:T(8,128)(2,1)} %get-tuple-element.25.q_ref, bf16[2,1024,1280]{2,1,0:T(8,128)(2,1)} %get-tuple-element.18.refs_0_, bf16[2,1024,1280]{2,1,0:T(8,128)(2,1)} %collective-permute-done.2.refs_1_, bf16[2,512,1280]{2,1,0:T(8,128)(2,1)} %get-tuple-element.19.refs_2_, ...), custom_call_target="tpu_custom_call" | custom-call | flops 14931722240 | bytes 42598400 | tf_op jit(solution)/shard_map/cross_mlp/pallas_call | solution.py:572
  (3 shorter events, 0.0 us)
Async XLA Ops:
  0.0 6.0 %copy-start.4 = (s32[4,8]{1,0:T(4,128)S(1)}, s32[4,8]{1,0:T(4,128)}, u32[]{:S(2)}) copy-start(s32[4,8]{1,0:T(4,128)} %constant.15.clone) | copy-start | bytes 388
  3.0 1.1 copy-start.3
  4.1 4.9 %collective-permute-start.1 = (bf16[512,1280]{1,0:T(8,128)(2,1)S(1)}, bf16[512,1280]{1,0:T(8,128)(2,1)S(1)}, u32[]{:S(2)}, u32[]{:S(2)}) collective-permute-start(bf16[512,1280]{1,0:T(8,128)(2,1)S(1)} %get-tuple-element.30), channel_id=1, source_target_pairs={{2,3},{6,7}} | collective-permute-start | bytes 3932168 | tf_op jit(solution)/shard_map/ppermute | solution.py:631
  9.0 1.1 copy-start.5
  10.1 10.5 %copy-start.6 = (bf16[256,1280]{1,0:T(8,128)(2,1)S(1)}, bf16[256,1280]{1,0:T(8,128)(2,1)}, u32[]{:S(2)}) copy-start(bf16[256,1280]{1,0:T(8,128)(2,1)} %refs_0_.2) | copy-start | bytes 1966084
  17.4 128.8 %collective-permute-start.2 = (bf16[2,1024,1280]{2,1,0:T(8,128)(2,1)}, bf16[2,1024,1280]{2,1,0:T(8,128)(2,1)}, u32[]{:S(2)}, u32[]{:S(2)}) collective-permute-start(bf16[2,1024,1280]{2,1,0:T(8,128)(2,1)} %get-tuple-element.18.refs_0_), channel_id=1, source_target_pairs={{0,1},{1,0},{2,3},{3,2},{4,5},{5,4},{6,7},{7,6}} | collective-permute-start | bytes 15728648 | tf_op jit(solution)/shard_map/ppermute | solution.py:626
  17.9 128.2 %collective-permute-start.7 = (bf16[2,1280,1024]{2,1,0:T(8,128)(2,1)}, bf16[2,1280,1024]{2,1,0:T(8,128)(2,1)}, u32[]{:S(2)}, u32[]{:S(2)}) collective-permute-start(bf16[2,1280,1024]{2,1,0:T(8,128)(2,1)} %get-tuple-element.21.refs_6_), channel_id=1, source_target_pairs={{0,1},{1,0},{2,3},{3,2},{4,5},{5,4},{6,7},{7,6}} | collective-permute-start | bytes 15728648 | tf_op jit(solution)/shard_map/ppermute | solution.py:626
  18.0 43.4 %collective-permute-start.5 = (bf16[512,1280]{1,0:T(8,128)(2,1)}, bf16[512,1280]{1,0:T(8,128)(2,1)S(1)}, u32[]{:S(2)}, u32[]{:S(2)}) collective-permute-start(bf16[512,1280]{1,0:T(8,128)(2,1)} %copy-done.3), channel_id=1, source_target_pairs={{0,2},{1,3},{2,1},{4,6},{5,7},{6,5}} | collective-permute-start | bytes 3932168 | tf_op jit(solution)/shard_map/ppermute | solution.py:633
  19.3 70.3 %collective-permute-start.3 = (bf16[512,1280]{1,0:T(8,128)(2,1)}, bf16[512,1280]{1,0:T(8,128)(2,1)}, u32[]{:S(2)}, u32[]{:S(2)}) collective-permute-start(bf16[512,1280]{1,0:T(8,128)(2,1)} %get-tuple-element.29), channel_id=1, source_target_pairs={{0,2},{1,3},{2,0},{4,6},{5,7},{6,4}} | collective-permute-start | bytes 3932168 | tf_op jit(solution)/shard_map/ppermute | solution.py:632
  20.6 83.0 %collective-permute-start = (bf16[256,1280]{1,0:T(8,128)(2,1)S(1)}, bf16[256,1280]{1,0:T(8,128)(2,1)}, u32[]{:S(2)}, u32[]{:S(2)}) collective-permute-start(bf16[256,1280]{1,0:T(8,128)(2,1)S(1)} %copy-done.6), channel_id=1, source_target_pairs={{0,2},{1,3},{4,6},{5,7}} | collective-permute-start | bytes 1966088 | tf_op jit(solution)/shard_map/ppermute | solution.py:629
  61.3 1.1 copy-start
  70.7 33.3 %collective-permute-start.6 = (bf16[1,512,1280]{2,1,0:T(8,128)(2,1)}, bf16[1,512,1280]{2,1,0:T(8,128)(2,1)}, u32[]{:S(2)}, u32[]{:S(2)}) collective-permute-start(bf16[1,512,1280]{2,1,0:T(8,128)(2,1)} %get-tuple-element.20.refs_4_), channel_id=1, source_target_pairs={{0,1},{1,0},{2,3},{3,2},{4,5},{5,4},{6,7},{7,6}} | collective-permute-start | bytes 3932168 | tf_op jit(solution)/shard_map/ppermute | solution.py:626
  89.5 14.5 %copy-start.1 = (bf16[1,1280,512]{2,1,0:T(8,128)(2,1)S(1)}, bf16[1,1280,512]{2,1,0:T(8,128)(2,1)}, u32[]{:S(2)}) copy-start(bf16[1,1280,512]{2,1,0:T(8,128)(2,1)} %get-tuple-element.23.refs_10_) | copy-start | bytes 3932164
  102.2 43.4 %collective-permute-start.4 = (bf16[2,512,1280]{2,1,0:T(8,128)(2,1)}, bf16[2,512,1280]{2,1,0:T(8,128)(2,1)}, u32[]{:S(2)}, u32[]{:S(2)}) collective-permute-start(bf16[2,512,1280]{2,1,0:T(8,128)(2,1)} %get-tuple-element.19.refs_2_), channel_id=1, source_target_pairs={{0,1},{1,0},{2,3},{3,2},{4,5},{5,4},{6,7},{7,6}} | collective-permute-start | bytes 7864328 | tf_op jit(solution)/shard_map/ppermute | solution.py:626
  103.6 42.5 %collective-permute-start.8 = (bf16[2,1280,512]{2,1,0:T(8,128)(2,1)}, bf16[2,1280,512]{2,1,0:T(8,128)(2,1)}, u32[]{:S(2)}, u32[]{:S(2)}) collective-permute-start(bf16[2,1280,512]{2,1,0:T(8,128)(2,1)} %get-tuple-element.22.refs_8_), channel_id=1, source_target_pairs={{0,1},{1,0},{2,3},{3,2},{4,5},{5,4},{6,7},{7,6}} | collective-permute-start | bytes 7864328 | tf_op jit(solution)/shard_map/ppermute | solution.py:626
  104.0 41.6 %collective-permute-start.9 = (bf16[1,1280,512]{2,1,0:T(8,128)(2,1)S(1)}, bf16[1,1280,512]{2,1,0:T(8,128)(2,1)}, u32[]{:S(2)}, u32[]{:S(2)}) collective-permute-start(bf16[1,1280,512]{2,1,0:T(8,128)(2,1)S(1)} %copy-done.1), channel_id=1, source_target_pairs={{0,1},{1,0},{2,3},{3,2},{4,5},{5,4},{6,7},{7,6}} | collective-permute-start | bytes 3932168 | tf_op jit(solution)/shard_map/ppermute | solution.py:626
  145.6 68.9 %collective-permute-start.10 = (bf16[1,512,1280]{2,1,0:T(8,128)(2,1)}, bf16[1,512,1280]{2,1,0:T(8,128)(2,1)S(1)}, u32[]{:S(2)}, u32[]{:S(2)}) collective-permute-start(bf16[1,512,1280]{2,1,0:T(8,128)(2,1)} %get-tuple-element.26.refs_4_), channel_id=1, source_target_pairs={{0,1},{1,0},{2,3},{3,2},{4,5},{5,4},{6,7},{7,6}} | collective-permute-start | bytes 3932168 | tf_op jit(solution)/shard_map/ppermute | solution.py:626
  145.6 68.9 %collective-permute-start.11 = (bf16[1,1280,512]{2,1,0:T(8,128)(2,1)}, bf16[1,1280,512]{2,1,0:T(8,128)(2,1)}, u32[]{:S(2)}, u32[]{:S(2)}) collective-permute-start(bf16[1,1280,512]{2,1,0:T(8,128)(2,1)} %get-tuple-element.27.refs_10_), channel_id=1, source_target_pairs={{0,1},{1,0},{2,3},{3,2},{4,5},{5,4},{6,7},{7,6}} | collective-permute-start | bytes 3932168 | tf_op jit(solution)/shard_map/ppermute | solution.py:626
  214.5 1.1 copy-start.2

commit v9 on v8

--- a/solution.py
+++ b/solution.py
@@ -32,14 +32,16 @@
 
 
 def kv_kernel(layers, n_src, lim_ref, pick_ref, *refs):
-    srcs, (wk, wv, k_out, vt_out, mem, w_s, k_s, vt_s, sem, w_sems, o_sems) = refs[:n_src], refs[n_src:]
+    srcs, (wk, wv, k_out, vt_out), refs = refs[:n_src], refs[n_src:n_src + 4], refs[n_src + 4:]
+    if n_src == 1:
+        mem, (w_s, k_s, vt_s, sem, w_sems, o_sems) = srcs[0], refs
+    else:
+        mem, w_s, k_s, vt_s, sem, w_sems, o_sems = refs
     rows = mem.shape[0]
     lo, n = layers
 
     def from_src(go):
-        if n_src == 1:
-            go(pltpu.make_async_copy(srcs[0], mem, sem))
-        else:
+        if n_src > 1:
             @pl.when(pick_ref[0] == 0)
             def _():
                 go(pltpu.make_async_copy(srcs[0], mem, sem))
@@ -108,11 +110,11 @@
     flops = n * 4 * rows * width * cols
     return pl.pallas_call(
         functools.partial(kv_kernel, layers, len(srcs)),
-        in_specs=[SMEM, SMEM] + [ANY] * (len(srcs) + 2),
+        in_specs=[SMEM, SMEM] + [VMEM if len(srcs) == 1 else ANY] * len(srcs) + [ANY, ANY],
         out_specs=[ANY, ANY],
         out_shape=[jax.ShapeDtypeStruct((n, rows, cols), BF16), jax.ShapeDtypeStruct((n, cols, rows), BF16)],
         scratch_shapes=[
-            pltpu.VMEM((rows, width), BF16),
+            *([pltpu.VMEM((rows, width), BF16)] if len(srcs) > 1 else []),
             pltpu.VMEM((2 * n, width, cols), BF16),
             pltpu.VMEM((n, rows, cols), BF16),
             pltpu.VMEM((n, cols, rows), BF16),
@@ -447,6 +449,7 @@
         kv_copies(i, lambda cp: cp.start())
 
     kv_start(0)
+    kv_start(1)
     o_copy = pltpu.make_async_copy(wco.at[layer], wo_s, o_sem)
 
     def w_copies(j):
@@ -484,7 +487,6 @@
 
         @pl.when(i == 0)
         def _():
-            kv_start(1)
             o_copy.start()
             for j in range(ring - groups):
                 w_start(j)

time: 254 us -> 255 us (level)
  Pallas kernels: 175 us -> 178 us
    pallas_call x4, Pallas kernels: 36.5 us -> 39.3 us  [kv_project(): pl.pallas_call(functools.partial(kv_kernel, layers, len(srcs)), in_specs=...]
  transfers between devices with their start and end apart: 12 -> 12, of which waited for: 4 -> 3; matrix products, arithmetic and copies ran while one was open for 1% -> 1% of each run, Pallas kernels for 51% -> 52%
where the time goes in v9:
time: 255 us; the launch traced here: 254 us
  Pallas kernels  178 us (70%)
  waiting for transfers between devices  58.7 us (23%)
  local copies, waits for them, and re-layouts  8.5 us (3%)
  starting transfers between devices  7.74 us (3%)
    pallas_call x2, Pallas kernels, cross_mlp(): pl.pallas_call(functools.partial(cross_kernel, layer, planes, n), in_spec...  75.5 us
    pallas_call x2, Pallas kernels, self_attention(): pl.pallas_call(functools.partial(self_kernel, layer, far_given), in_specs...  63.1 us
    pallas_call x4, Pallas kernels, kv_project(): pl.pallas_call(functools.partial(kv_kernel, layers, len(srcs)), in_specs=...  39.3 us
    ppermute x1, waiting for transfers between devices, program(): rem_b = lax.ppermute(mem_b, 'sp', [(0, 2), (1, 3), (2, 1)])  38.9 us
    ppermute x1, waiting for transfers between devices, program(): rem_a = lax.ppermute(mem_a, 'sp', [(0, 2), (1, 3), (2, 0)])  17.4 us
  transfers between devices with their start and end apart: 12, of which 3 were waited for; matrix products, arithmetic and copies ran while one was open for 1% of the time, Pallas kernels for 52%

profile of v9, /device:TPU:7, one launch (start us, length us, event | category | flops | bytes accessed | tf_op | source)
XLA Modules:
  0.0 254.4 jit_solution(10377551448981972053)
XLA Ops:
  0.0 0.0 copy-start.4
  0.0 3.0 %fusion = (bf16[512,1280]{1,0:T(8,128)(2,1)}, bf16[512,1280]{1,0:T(8,128)(2,1)S(1)}) fusion(bf16[1024,1280]{1,0:T(8,128)(2,1)} %refs_0_.3), kind=kLoop, calls=%fused_computation.2 | loop fusion | bytes 5242880 | tf_op jit(solution)/shard_map/slice | solution.py:632
  3.0 0.0 copy-start.3
  3.0 1.1 copy-done.3
  4.1 1.3 collective-permute-start.1
  6.0 0.0 copy-done.4
  6.0 0.6 slice_bitcast_fusion.lim_ref
  6.6 2.4 collective-permute-done.1.refs_1_
  9.0 0.0 copy-start.5
  9.0 1.1 copy-done.5
  10.1 0.0 copy-start.6
  10.1 7.3 %kv_project.4 = (bf16[2,1024,1280]{2,1,0:T(8,128)(2,1)}, bf16[2,1280,1024]{2,1,0:T(8,128)(2,1)}) custom-call(s32[2]{0:T(128)} %slice_bitcast_fusion.lim_ref, s32[1]{0:T(128)} %bitcast.4.pick_ref, bf16[1024,1280]{1,0:T(8,128)(2,1)} %refs_0_.3, bf16[512,1280]{1,0:T(8,128)(2,1)} %copy-done.5, bf16[2,1280,1280]{2,1,0:T(8,128)(2,1)} %refs_1_.7, ...), custom_call_target="tpu_custom_call" | custom-call | flops 13421772800 | bytes 13107200 | tf_op jit(solution)/shard_map/kv_project/pallas_call | solution.py:111
  17.4 0.6 collective-permute-start.2
  17.9 0.0 collective-permute-start.7
  18.0 1.3 collective-permute-start.5
  19.3 1.3 collective-permute-start.3
  20.6 0.0 copy-done.6
  20.6 1.3 collective-permute-start
  21.9 0.6 fusion.1
  22.5 38.9 %collective-permute-done.5.refs_0_ = bf16[512,1280]{1,0:T(8,128)(2,1)S(1)} collective-permute-done((bf16[512,1280]{1,0:T(8,128)(2,1)}, bf16[512,1280]{1,0:T(8,128)(2,1)S(1)}, u32[]{:S(2)}, u32[]{:S(2)}) %collective-permute-start.5) | collective-permute-done | bytes 1310752 | tf_op jit(solution)/shard_map/ppermute | solution.py:635
  61.4 1.1 copy-done
  62.4 9.2 %kv_project.6 = (bf16[1,512,1280]{2,1,0:T(8,128)(2,1)}, bf16[1,1280,512]{2,1,0:T(8,128)(2,1)}) custom-call(s32[1]{0:T(128)} %bitcast.6.lim_ref, s32[1]{0:T(128)} %bitcast.4.pick_ref, bf16[512,1280]{1,0:T(8,128)(2,1)} %copy-done, bf16[2,1280,1280]{2,1,0:T(8,128)(2,1)} %refs_1_.7, bf16[2,1280,1280]{2,1,0:T(8,128)(2,1)} %refs_2_.11), custom_call_target="tpu_custom_call" | custom-call | flops 3355443200 | bytes 6553600 | tf_op jit(solution)/shard_map/kv_project/pallas_call | solution.py:111
  71.6 0.5 collective-permute-start.6
  72.1 17.4 %collective-permute-done.3.refs_0_ = bf16[512,1280]{1,0:T(8,128)(2,1)} collective-permute-done((bf16[512,1280]{1,0:T(8,128)(2,1)}, bf16[512,1280]{1,0:T(8,128)(2,1)}, u32[]{:S(2)}, u32[]{:S(2)}) %collective-permute-start.3) | collective-permute-done | bytes 1310752 | tf_op jit(solution)/shard_map/ppermute | solution.py:634
  89.5 13.6 %kv_project.5 = (bf16[2,512,1280]{2,1,0:T(8,128)(2,1)}, bf16[2,1280,512]{2,1,0:T(8,128)(2,1)}) custom-call(s32[1]{0:T(128)} %bitcast.5.lim_ref, s32[1]{0:T(128)} %bitcast.4.pick_ref, bf16[512,1280]{1,0:T(8,128)(2,1)} %collective-permute-done.3.refs_0_, bf16[2,1280,1280]{2,1,0:T(8,128)(2,1)} %refs_1_.7, bf16[2,1280,1280]{2,1,0:T(8,128)(2,1)} %refs_2_.11), custom_call_target="tpu_custom_call" | custom-call | flops 6710886400 | bytes 13107200 | tf_op jit(solution)/shard_map/kv_project/pallas_call | solution.py:111
  103.2 0.5 collective-permute-start.4
  103.6 0.0 collective-permute-done.refs_1_
  103.6 0.4 collective-permute-start.8
  104.0 0.0 collective-permute-done.6.refs_5_
  104.0 0.0 copy-done.1
  104.0 0.1 collective-permute-start.9
  104.2 0.5 fusion.2.lim_ref
  104.7 33.6 %self_attention.2 = (bf16[256,1280]{1,0:T(8,128)(2,1)}, bf16[1280,256]{1,0:T(8,128)(2,1)}) custom-call(bf16[256,1280]{1,0:T(8,128)(2,1)} %refs_0_.2, bf16[256,1280]{1,0:T(8,128)(2,1)} %collective-permute-done.refs_1_, bf16[2,1280]{1,0:T(2,128)(2,1)} %refs_1_.6, bf16[2,1280]{1,0:T(2,128)(2,1)} %refs_2_.10, bf16[2,1280,1280]{2,1,0:T(8,128)(2,1)} %refs_3_.5, ...), custom_call_target="tpu_custom_call" | custom-call | flops 10569646080 | bytes 16384000 | tf_op jit(solution)/shard_map/self_attention/pallas_call | solution.py:393
  138.3 9.2 %kv_project.7 = (bf16[1,512,1280]{2,1,0:T(8,128)(2,1)}, bf16[1,1280,512]{2,1,0:T(8,128)(2,1)}) custom-call(s32[1]{0:T(128)} %bitcast.6.lim_ref, s32[1]{0:T(128)} %bitcast.4.pick_ref, bf16[512,1280]{1,0:T(8,128)(2,1)} %copy-done, bf16[2,1280,1280]{2,1,0:T(8,128)(2,1)} %refs_1_.7, bf16[2,1280,1280]{2,1,0:T(8,128)(2,1)} %refs_2_.11), custom_call_target="tpu_custom_call" | custom-call | flops 3355443200 | bytes 6553600 | tf_op jit(solution)/shard_map/kv_project/pallas_call | solution.py:111
  147.5 0.0 collective-permute-done.9.refs_11_
  147.5 0.0 collective-permute-start.10
  147.5 0.0 collective-permute-done.4.refs_3_
  147.5 0.5 collective-permute-start.11
  148.0 0.0 collective-permute-done.8.refs_9_
  148.0 0.0 collective-permute-done.2.refs_1_
  148.0 0.0 collective-permute-done.7.refs_7_
  148.0 37.6 %cross_mlp.2.refs_0_ = bf16[256,1280]{1,0:T(8,128)(2,1)} custom-call(s32[8]{0:T(128)} %fusion.2.lim_ref, bf16[1280,256]{1,0:T(8,128)(2,1)} %get-tuple-element.17.q_ref, bf16[2,1024,1280]{2,1,0:T(8,128)(2,1)} %get-tuple-element.18.refs_0_, bf16[2,1024,1280]{2,1,0:T(8,128)(2,1)} %collective-permute-done.2.refs_1_, ...), custom_call_target="tpu_custom_call" | custom-call | flops 14931722240 | bytes 42598400 | tf_op jit(solution)/shard_map/cross_mlp/pallas_call | solution.py:574
  185.7 29.6 %self_attention.3 = (bf16[256,1280]{1,0:T(8,128)(2,1)}, bf16[1280,256]{1,0:T(8,128)(2,1)}) custom-call(bf16[256,1280]{1,0:T(8,128)(2,1)} %cross_mlp.2.refs_0_, bf16[2,1280]{1,0:T(2,128)(2,1)} %refs_1_.6, bf16[2,1280]{1,0:T(2,128)(2,1)} %refs_2_.10, bf16[2,1280,1280]{2,1,0:T(8,128)(2,1)} %refs_3_.5, bf16[2,1280,1280]{2,1,0:T(8,128)(2,1)} %refs_4_.3, ...), custom_call_target="tpu_custom_call" | custom-call | flops 10569646080 | bytes 16384000 | tf_op jit(solution)/shard_map/self_attention/pallas_call | solution.py:393
  215.2 0.0 collective-permute-done.10.refs_5_
  215.3 0.0 copy-start.2
  215.3 0.0 collective-permute-done.11.refs_11_
  215.3 1.1 copy-done.2
  216.4 37.9 %cross_mlp.3 = bf16[256,1280]{1,0:T(8,128)(2,1)} custom-call(s32[8]{0:T(128)} %fusion.2.lim_ref, bf16[1280,256]{1,0:T(8,128)(2,1)} %get-tuple-element.25.q_ref, bf16[2,1024,1280]{2,1,0:T(8,128)(2,1)} %get-tuple-element.18.refs_0_, bf16[2,1024,1280]{2,1,0:T(8,128)(2,1)} %collective-permute-done.2.refs_1_, bf16[2,512,1280]{2,1,0:T(8,128)(2,1)} %get-tuple-element.19.refs_2_, ...), custom_call_target="tpu_custom_call" | custom-call | flops 14931722240 | bytes 42598400 | tf_op jit(solution)/shard_map/cross_mlp/pallas_call | solution.py:574
  (3 shorter events, 0.0 us)
Async XLA Ops:
  0.0 6.0 %copy-start.4 = (s32[4,8]{1,0:T(4,128)S(1)}, s32[4,8]{1,0:T(4,128)}, u32[]{:S(2)}) copy-start(s32[4,8]{1,0:T(4,128)} %constant.15.clone) | copy-start | bytes 388
  3.0 1.1 copy-start.3
  4.1 4.9 %collective-permute-start.1 = (bf16[512,1280]{1,0:T(8,128)(2,1)S(1)}, bf16[512,1280]{1,0:T(8,128)(2,1)S(1)}, u32[]{:S(2)}, u32[]{:S(2)}) collective-permute-start(bf16[512,1280]{1,0:T(8,128)(2,1)S(1)} %get-tuple-element.30), channel_id=1, source_target_pairs={{2,3},{6,7}} | collective-permute-start | bytes 3932168 | tf_op jit(solution)/shard_map/ppermute | solution.py:633
  9.0 1.1 copy-start.5
  10.1 10.5 %copy-start.6 = (bf16[256,1280]{1,0:T(8,128)(2,1)S(1)}, bf16[256,1280]{1,0:T(8,128)(2,1)}, u32[]{:S(2)}) copy-start(bf16[256,1280]{1,0:T(8,128)(2,1)} %refs_0_.2) | copy-start | bytes 1966084
  17.4 130.7 %collective-permute-start.2 = (bf16[2,1024,1280]{2,1,0:T(8,128)(2,1)}, bf16[2,1024,1280]{2,1,0:T(8,128)(2,1)}, u32[]{:S(2)}, u32[]{:S(2)}) collective-permute-start(bf16[2,1024,1280]{2,1,0:T(8,128)(2,1)} %get-tuple-element.18.refs_0_), channel_id=1, source_target_pairs={{0,1},{1,0},{2,3},{3,2},{4,5},{5,4},{6,7},{7,6}} | collective-permute-start | bytes 15728648 | tf_op jit(solution)/shard_map/ppermute | solution.py:628
  17.9 130.1 %collective-permute-start.7 = (bf16[2,1280,1024]{2,1,0:T(8,128)(2,1)}, bf16[2,1280,1024]{2,1,0:T(8,128)(2,1)}, u32[]{:S(2)}, u32[]{:S(2)}) collective-permute-start(bf16[2,1280,1024]{2,1,0:T(8,128)(2,1)} %get-tuple-element.21.refs_6_), channel_id=1, source_target_pairs={{0,1},{1,0},{2,3},{3,2},{4,5},{5,4},{6,7},{7,6}} | collective-permute-start | bytes 15728648 | tf_op jit(solution)/shard_map/ppermute | solution.py:628
  18.0 43.4 %collective-permute-start.5 = (bf16[512,1280]{1,0:T(8,128)(2,1)}, bf16[512,1280]{1,0:T(8,128)(2,1)S(1)}, u32[]{:S(2)}, u32[]{:S(2)}) collective-permute-start(bf16[512,1280]{1,0:T(8,128)(2,1)} %copy-done.3), channel_id=1, source_target_pairs={{0,2},{1,3},{2,1},{4,6},{5,7},{6,5}} | collective-permute-start | bytes 3932168 | tf_op jit(solution)/shard_map/ppermute | solution.py:635
  19.3 70.3 %collective-permute-start.3 = (bf16[512,1280]{1,0:T(8,128)(2,1)}, bf16[512,1280]{1,0:T(8,128)(2,1)}, u32[]{:S(2)}, u32[]{:S(2)}) collective-permute-start(bf16[512,1280]{1,0:T(8,128)(2,1)} %get-tuple-element.29), channel_id=1, source_target_pairs={{0,2},{1,3},{2,0},{4,6},{5,7},{6,4}} | collective-permute-start | bytes 3932168 | tf_op jit(solution)/shard_map/ppermute | solution.py:634
  20.6 83.1 %collective-permute-start = (bf16[256,1280]{1,0:T(8,128)(2,1)S(1)}, bf16[256,1280]{1,0:T(8,128)(2,1)}, u32[]{:S(2)}, u32[]{:S(2)}) collective-permute-start(bf16[256,1280]{1,0:T(8,128)(2,1)S(1)} %copy-done.6), channel_id=1, source_target_pairs={{0,2},{1,3},{4,6},{5,7}} | collective-permute-start | bytes 1966088 | tf_op jit(solution)/shard_map/ppermute | solution.py:631
  61.3 1.1 copy-start
  71.6 32.4 %collective-permute-start.6 = (bf16[1,512,1280]{2,1,0:T(8,128)(2,1)}, bf16[1,512,1280]{2,1,0:T(8,128)(2,1)}, u32[]{:S(2)}, u32[]{:S(2)}) collective-permute-start(bf16[1,512,1280]{2,1,0:T(8,128)(2,1)} %get-tuple-element.20.refs_4_), channel_id=1, source_target_pairs={{0,1},{1,0},{2,3},{3,2},{4,5},{5,4},{6,7},{7,6}} | collective-permute-start | bytes 3932168 | tf_op jit(solution)/shard_map/ppermute | solution.py:628
  89.5 14.5 %copy-start.1 = (bf16[1,1280,512]{2,1,0:T(8,128)(2,1)S(1)}, bf16[1,1280,512]{2,1,0:T(8,128)(2,1)}, u32[]{:S(2)}) copy-start(bf16[1,1280,512]{2,1,0:T(8,128)(2,1)} %get-tuple-element.23.refs_10_) | copy-start | bytes 3932164
  103.2 44.3 %collective-permute-start.4 = (bf16[2,512,1280]{2,1,0:T(8,128)(2,1)}, bf16[2,512,1280]{2,1,0:T(8,128)(2,1)}, u32[]{:S(2)}, u32[]{:S(2)}) collective-permute-start(bf16[2,512,1280]{2,1,0:T(8,128)(2,1)} %get-tuple-element.19.refs_2_), channel_id=1, source_target_pairs={{0,1},{1,0},{2,3},{3,2},{4,5},{5,4},{6,7},{7,6}} | collective-permute-start | bytes 7864328 | tf_op jit(solution)/shard_map/ppermute | solution.py:628
  103.6 44.4 %collective-permute-start.8 = (bf16[2,1280,512]{2,1,0:T(8,128)(2,1)}, bf16[2,1280,512]{2,1,0:T(8,128)(2,1)}, u32[]{:S(2)}, u32[]{:S(2)}) collective-permute-start(bf16[2,1280,512]{2,1,0:T(8,128)(2,1)} %get-tuple-element.22.refs_8_), channel_id=1, source_target_pairs={{0,1},{1,0},{2,3},{3,2},{4,5},{5,4},{6,7},{7,6}} | collective-permute-start | bytes 7864328 | tf_op jit(solution)/shard_map/ppermute | solution.py:628
  104.0 43.5 %collective-permute-start.9 = (bf16[1,1280,512]{2,1,0:T(8,128)(2,1)S(1)}, bf16[1,1280,512]{2,1,0:T(8,128)(2,1)}, u32[]{:S(2)}, u32[]{:S(2)}) collective-permute-start(bf16[1,1280,512]{2,1,0:T(8,128)(2,1)S(1)} %copy-done.1), channel_id=1, source_target_pairs={{0,1},{1,0},{2,3},{3,2},{4,5},{5,4},{6,7},{7,6}} | collective-permute-start | bytes 3932168 | tf_op jit(solution)/shard_map/ppermute | solution.py:628
  147.5 67.8 %collective-permute-start.10 = (bf16[1,512,1280]{2,1,0:T(8,128)(2,1)}, bf16[1,512,1280]{2,1,0:T(8,128)(2,1)S(1)}, u32[]{:S(2)}, u32[]{:S(2)}) collective-permute-start(bf16[1,512,1280]{2,1,0:T(8,128)(2,1)} %get-tuple-element.26.refs_4_), channel_id=1, source_target_pairs={{0,1},{1,0},{2,3},{3,2},{4,5},{5,4},{6,7},{7,6}} | collective-permute-start | bytes 3932168 | tf_op jit(solution)/shard_map/ppermute | solution.py:628
  147.5 67.7 %collective-permute-start.11 = (bf16[1,1280,512]{2,1,0:T(8,128)(2,1)}, bf16[1,1280,512]{2,1,0:T(8,128)(2,1)}, u32[]{:S(2)}, u32[]{:S(2)}) collective-permute-start(bf16[1,1280,512]{2,1,0:T(8,128)(2,1)} %get-tuple-element.27.refs_10_), channel_id=1, source_target_pairs={{0,1},{1,0},{2,3},{3,2},{4,5},{5,4},{6,7},{7,6}} | collective-permute-start | bytes 3932168 | tf_op jit(solution)/shard_map/ppermute | solution.py:628
  215.3 1.1 copy-start.2
